TPU v7x, 32 devices: a whole 2x2x4 slice. The times are simulated.
32 devices in a mesh: dp: 16 (over z, y, x), tensor: 2 (over core).
Axes of the slice: x: 2, y: 2, z: 4, core: 2. Of those that a mesh axis runs over, the one named last changes fastest.
Arguments:
- tokens: bfloat16 [16384, 1536], P(('dp', 'tensor')), may hold values from -6 to 6
- segment_ids: int32 [16384], P('dp'), may hold values from -1 to 127, as said below
- norm_gain: float32 [1536], replicated, may hold values from 0.5 to 1.5
- in_gate_inner: bfloat16 [1536, 2, 3072], P('dp', None, 'tensor'), may hold values from -0.15625 to 0.15625
- in_state: bfloat16 [1536, 2, 128], P('dp'), may hold values from -0.15625 to 0.15625
- in_step: bfloat16 [1536, 48], P('dp', 'tensor'), may hold values from -0.15625 to 0.15625
- conv_inner: float32 [4, 3072], P(None, 'tensor'), may hold values from -3 to 3
- conv_inner_bias: float32 [3072], P('tensor'), may hold values from -3 to 3
- conv_state: float32 [4, 2, 128], replicated, may hold values from -3 to 3
- conv_state_bias: float32 [2, 128], replicated, may hold values from -3 to 3
- step_bias: float32 [48], P('tensor'), may hold values from -7 to -4
- decay_log: float32 [48], P('tensor'), may hold values from 0 to 2.5
- skip_gain: float32 [48], P('tensor'), may hold values from 0.5 to 1.5
- gate_gain: float32 [3072], P('tensor'), may hold values from 0.5 to 1.5
- out_proj: bfloat16 [3072, 1536], P('tensor', 'dp'), may hold values from -0.109375 to 0.109375
- cotangent: bfloat16 [16384, 1536], P(('dp', 'tensor')), may hold values from -6 to 6
Outputs:
- block_out: bfloat16 [16384, 1536], P(('dp', 'tensor'))
- grad_tokens: float32 [16384, 1536], P(('dp', 'tensor'))
- grad_norm_gain: float32 [1536], replicated
- grad_in_gate_inner: float32 [1536, 2, 3072], P('dp', None, 'tensor')
- grad_in_state: float32 [1536, 2, 128], P('dp')
- grad_in_step: float32 [1536, 48], P('dp', 'tensor')
- grad_conv_inner: float32 [4, 3072], P(None, 'tensor')
- grad_conv_inner_bias: float32 [3072], P('tensor')
- grad_conv_state: float32 [4, 2, 128], replicated
- grad_conv_state_bias: float32 [2, 128], replicated
- grad_step_bias: float32 [48], P('tensor')
- grad_decay_log: float32 [48], P('tensor')
- grad_skip_gain: float32 [48], P('tensor')
- grad_gate_gain: float32 [3072], P('tensor')
- grad_out_proj: float32 [3072, 1536], P('tensor', 'dp')
Inputs may be any that keep to these rules, and one draw needn't show every extreme that they name: `segment_ids`: within each block of 1024 slots (one index of dp) the live slots come first and carry sequence numbers counting from 0 in order; every sequence starts at a slot whose place in its block is a multiple of 8 and has at most 1024 slots; the rest carry -1. Every block has at least 512 live slots. One block is fully live and begins with a sequence of exactly 1024 slots, another has exactly 512 live slots, and a third is fully live with sequences of 8 slots each.
All inputs are finite; a program needn't handle non-finite values.
Results may differ from a plain program's by a relative error of at most 0.0079.
Values may be sent and summed in bfloat16 or wider, within the bound.
A program may use at most 256 MiB of HBM per device.

v0:
```python
from functools import partial

import jax
import jax.numpy as jnp
from jax import lax
from jax.sharding import PartitionSpec as P

SPAN = 256


EPSILON = 1e-05
HIGHEST = lax.Precision.HIGHEST


def shift_down(values, steps_back, filler):
    leading = jnp.full((steps_back,) + values.shape[1:], filler, values.dtype)
    return jnp.concatenate([leading, values[: values.shape[0] - steps_back]], axis=0)


def causal_conv(values, conv_taps, conv_bias, segment):
    taps_count = conv_taps.shape[0]
    result = conv_bias[None, :] + conv_taps[taps_count - 1][None, :] * values
    for steps_back in range(1, taps_count):
        earlier = shift_down(values, steps_back, 0.0)
        same_seq = (shift_down(segment, steps_back, -2) == segment).astype(values.dtype)
        result = (
            result + conv_taps[taps_count - 1 - steps_back][None, :] * earlier * same_seq[:, None]
        )
    return result


def span_step(carried_in, block_data):
    state_now, last_segment = carried_in
    inner_blk, state_in, state_out, step_blk, log_blk, seg_blk = block_data
    block_len = seg_blk.shape[0]
    cum_heads = jnp.cumsum(log_blk, axis=0).T
    places = jnp.arange(block_len)
    allowed = (places[:, None] >= places[None, :]) & (seg_blk[:, None] == seg_blk[None, :])
    spread = jnp.where(allowed[None], cum_heads[:, :, None] - cum_heads[:, None, :], 0.0)
    scores = jnp.dot(state_out, state_in.T, precision=HIGHEST)
    mixing = jnp.exp(spread) * (scores * allowed)[None] * step_blk.T[:, None, :]
    within = jnp.einsum("hts,shp->thp", mixing, inner_blk, precision=HIGHEST)
    carried = (seg_blk == last_segment).astype(jnp.float32)
    reach = jnp.exp(cum_heads).T * carried[:, None]
    from_state = (
        jnp.einsum("tn,hnp->thp", state_out, state_now, precision=HIGHEST) * reach[:, :, None]
    )
    end_segment = seg_blk[block_len - 1]
    keep_end = (seg_blk == end_segment).astype(jnp.float32)
    to_end = (
        jnp.exp(cum_heads[:, block_len - 1][:, None] - cum_heads).T * keep_end[:, None] * step_blk
    )
    fresh = jnp.einsum("sn,shp->hnp", state_in, inner_blk * to_end[:, :, None], precision=HIGHEST)
    kept_share = jnp.exp(cum_heads[:, block_len - 1]) * (end_segment == last_segment).astype(
        jnp.float32
    )
    new_state = fresh + state_now * kept_share[:, None, None]
    return ((new_state, end_segment), within + from_state)


def mixer(
    gate_inner,
    state_act,
    step_proj,
    conv_inner,
    conv_inner_bias,
    step_bias,
    decay_log,
    skip_gain,
    segment,
):
    length = gate_inner.shape[0]
    inner_dev = gate_inner.shape[1] // 2
    heads_dev = step_proj.shape[1]
    head_size = inner_dev // heads_dev
    state_dim = state_act.shape[1] // 2
    blocks = length // SPAN
    inner_act = jax.nn.silu(
        causal_conv(gate_inner[:, inner_dev:], conv_inner, conv_inner_bias, segment)
    )
    step_size = jax.nn.softplus(step_proj + step_bias[None, :])
    log_decay = step_size * (-jnp.exp(decay_log))[None, :]
    heads_inner = inner_act.reshape(length, heads_dev, head_size)
    initial = (jnp.zeros((heads_dev, state_dim, head_size), jnp.float32), jnp.int32(-2))
    scanned = (
        heads_inner.reshape(blocks, SPAN, heads_dev, head_size),
        state_act[:, :state_dim].reshape(blocks, SPAN, state_dim),
        state_act[:, state_dim:].reshape(blocks, SPAN, state_dim),
        step_size.reshape(blocks, SPAN, heads_dev),
        log_decay.reshape(blocks, SPAN, heads_dev),
        segment.reshape(blocks, SPAN),
    )
    unused, ssd_out = lax.scan(jax.checkpoint(span_step), initial, scanned)
    mixed_heads = (
        ssd_out.reshape(length, heads_dev, head_size) + skip_gain[None, :, None] * heads_inner
    )
    return mixed_heads.reshape(length, inner_dev) * jax.nn.silu(gate_inner[:, :inner_dev])


def shards(
    tokens,
    segment_ids,
    norm_gain,
    in_gate_inner,
    in_state,
    in_step,
    conv_inner,
    conv_inner_bias,
    conv_state,
    conv_state_bias,
    step_bias,
    decay_log,
    skip_gain,
    gate_gain,
    out_proj,
    cotangent,
):
    half_rows = tokens.shape[0]
    model_width = tokens.shape[1]
    tensor_place = lax.axis_index("tensor")
    own_segment = lax.dynamic_slice_in_dim(segment_ids, tensor_place * half_rows, half_rows)
    own_live = (own_segment >= 0).astype(jnp.float32)[:, None]
    own_rows = tokens.astype(jnp.float32)
    row_scale = lax.rsqrt(jnp.mean(own_rows * own_rows, axis=1, keepdims=True) + EPSILON)
    normed_own = (own_rows * row_scale * norm_gain[None, :]).astype(jnp.bfloat16)
    gate_weights, state_weights, step_weights, out_weights = (
        lax.all_gather(in_gate_inner, "dp", axis=0, tiled=True),
        lax.all_gather(in_state, "dp", axis=0, tiled=True),
        lax.all_gather(in_step, "dp", axis=0, tiled=True),
        lax.all_gather(out_proj, "dp", axis=1, tiled=True),
    )
    normed = lax.all_gather(normed_own, "tensor", axis=0, tiled=True)
    inner_dev = gate_weights.shape[2]
    gate_inner = jnp.dot(
        normed, gate_weights.reshape(model_width, 2 * inner_dev), preferred_element_type=jnp.float32
    )
    state_proj = jnp.dot(
        normed, state_weights.reshape(model_width, -1), preferred_element_type=jnp.float32
    )
    step_proj = jnp.dot(normed, step_weights, preferred_element_type=jnp.float32)

    def state_piece(state_values, conv_taps, conv_bias):
        return jax.nn.silu(
            causal_conv(
                state_values,
                conv_taps.reshape(conv_taps.shape[0], -1),
                conv_bias.reshape(-1),
                segment_ids,
            )
        )

    state_act, state_back = jax.vjp(state_piece, state_proj, conv_state, conv_state_bias)
    gated_values, mixer_back = jax.vjp(
        partial(mixer, segment=segment_ids),
        gate_inner,
        state_act,
        step_proj,
        conv_inner,
        conv_inner_bias,
        step_bias,
        decay_log,
        skip_gain,
    )
    full_inner = inner_dev * lax.axis_size("tensor")
    squares = lax.psum(jnp.sum(gated_values * gated_values, axis=1), "tensor")
    gate_scale = lax.rsqrt(squares / full_inner + EPSILON)[:, None]
    normed_inner = (gated_values * gate_scale * gate_gain[None, :]).astype(jnp.bfloat16)
    partial_out = jnp.dot(normed_inner, out_weights, preferred_element_type=jnp.float32)
    branch_own = lax.psum_scatter(partial_out, "tensor", scatter_dimension=0, tiled=True)
    block_out = (own_rows + own_live * branch_own).astype(jnp.bfloat16)
    gate_weights, state_weights, step_weights, out_weights = (
        lax.all_gather(in_gate_inner, "dp", axis=0, tiled=True),
        lax.all_gather(in_state, "dp", axis=0, tiled=True),
        lax.all_gather(in_step, "dp", axis=0, tiled=True),
        lax.all_gather(out_proj, "dp", axis=1, tiled=True),
    )
    cot_rows = cotangent.astype(jnp.float32)
    branch_grad_own = (own_live * cot_rows).astype(jnp.bfloat16)
    branch_grad = lax.all_gather(branch_grad_own, "tensor", axis=0, tiled=True)
    grad_out_proj = jnp.einsum(
        "tc,td->cd", normed_inner, branch_grad, preferred_element_type=jnp.float32
    )
    grad_normed_inner = jnp.einsum(
        "td,cd->tc", branch_grad, out_weights, preferred_element_type=jnp.float32
    )
    grad_gate_gain = jnp.sum(grad_normed_inner * gated_values * gate_scale, axis=0)
    scaled_grad = grad_normed_inner * gate_gain[None, :]
    products = lax.psum(jnp.sum(scaled_grad * gated_values, axis=1), "tensor")
    grad_gated = (
        gate_scale * scaled_grad - gated_values * gate_scale**3 * (products / full_inner)[:, None]
    )
    (
        grad_gate_inner,
        grad_state_part,
        grad_step_proj,
        grad_conv_inner,
        grad_conv_inner_bias,
        grad_step_bias,
        grad_decay_log,
        grad_skip_gain,
    ) = mixer_back(grad_gated)
    grad_state_act = lax.psum(grad_state_part, "tensor")
    grad_state_proj, grad_conv_state, grad_conv_state_bias = state_back(grad_state_act)
    low_gate_inner = grad_gate_inner.astype(jnp.bfloat16)
    low_state = grad_state_proj.astype(jnp.bfloat16)
    low_step = grad_step_proj.astype(jnp.bfloat16)
    grad_in_gate_inner = jnp.einsum(
        "td,tc->dc", normed, low_gate_inner, preferred_element_type=jnp.float32
    ).reshape(model_width, 2, inner_dev)
    grad_in_state = jnp.einsum(
        "td,tc->dc", normed, low_state, preferred_element_type=jnp.float32
    ).reshape(model_width, 2, -1)
    grad_in_step = jnp.einsum("td,th->dh", normed, low_step, preferred_element_type=jnp.float32)
    head_grads = jnp.einsum(
        "tc,dc->td",
        low_gate_inner,
        gate_weights.reshape(model_width, 2 * inner_dev),
        preferred_element_type=jnp.float32,
    )
    head_grads = head_grads + jnp.einsum(
        "th,dh->td", low_step, step_weights, preferred_element_type=jnp.float32
    )
    normed_grad_own = lax.psum_scatter(head_grads, "tensor", scatter_dimension=0, tiled=True)
    own_state_grad = lax.dynamic_slice_in_dim(low_state, tensor_place * half_rows, half_rows)
    normed_grad_own = normed_grad_own + jnp.einsum(
        "tc,dc->td",
        own_state_grad,
        state_weights.reshape(model_width, -1),
        preferred_element_type=jnp.float32,
    )
    grad_norm_part = jnp.sum(normed_grad_own * own_rows * row_scale, axis=0)
    scaled_rows = normed_grad_own * norm_gain[None, :]
    row_products = jnp.sum(scaled_rows * own_rows, axis=1, keepdims=True)
    grad_tokens = (
        cot_rows + row_scale * scaled_rows - own_rows * row_scale**3 * row_products / model_width
    )
    grad_norm_gain = lax.psum(grad_norm_part, ("dp", "tensor"))
    summed_weights = (
        lax.psum_scatter(grad_in_gate_inner, "dp", scatter_dimension=0, tiled=True),
        lax.psum_scatter(grad_in_state, "dp", scatter_dimension=0, tiled=True),
        lax.psum_scatter(grad_in_step, "dp", scatter_dimension=0, tiled=True),
        lax.psum_scatter(grad_out_proj, "dp", scatter_dimension=1, tiled=True),
    )
    summed_small = lax.psum(
        (
            grad_conv_inner,
            grad_conv_inner_bias,
            grad_conv_state,
            grad_conv_state_bias,
            grad_step_bias,
            grad_decay_log,
            grad_skip_gain,
            grad_gate_gain,
        ),
        "dp",
    )
    return (
        block_out,
        grad_tokens,
        grad_norm_gain,
        summed_weights[0],
        summed_weights[1],
        summed_weights[2],
        summed_small[0],
        summed_small[1],
        summed_small[2],
        summed_small[3],
        summed_small[4],
        summed_small[5],
        summed_small[6],
        summed_small[7],
        summed_weights[3],
    )


def solution(mesh):
    in_specs = (
        P(("dp", "tensor"), None),
        P("dp"),
        P(),
        P("dp", None, "tensor"),
        P("dp", None, None),
        P("dp", "tensor"),
        P(None, "tensor"),
        P("tensor"),
        P(),
        P(),
        P("tensor"),
        P("tensor"),
        P("tensor"),
        P("tensor"),
        P("tensor", "dp"),
        P(("dp", "tensor"), None),
    )
    out_specs = (
        P(("dp", "tensor"), None),
        P(("dp", "tensor"), None),
        P(),
        P("dp", None, "tensor"),
        P("dp", None, None),
        P("dp", "tensor"),
        P(None, "tensor"),
        P("tensor"),
        P(),
        P(),
        P("tensor"),
        P("tensor"),
        P("tensor"),
        P("tensor"),
        P("tensor", "dp"),
    )
    return jax.shard_map(shards, mesh=mesh, in_specs=in_specs, out_specs=out_specs, check_vma=False)
```

profile of v0, /device:TPU:0, one launch (start us, length us, event | category | flops | bytes accessed | tf_op | source)
XLA Modules:
  0.0 1630.3 jit_solution(11517697395150460704)
XLA Ops:
  16.3 43.3 %all-gather = bf16[16,96,24]{1,2,0:T(8,128)(2,1)S(1)} all-gather(bf16[1,96,24]{1,2,0:T(8,128)(2,1)S(1)} %bitcast.498), channel_id=1, replica_groups=mesh['dp'=16,'tensor'=2] {'dp'}, dimensions={0}, use_global_device_ids=true | all-gather | bytes 78336 | tf_op jit(solution)/shard_map/all_gather | solution.py:129
  59.8 48.5 %all_gather.25 = bf16[1536,2,128]{2,1,0:T(2,128)(2,1)} all-gather(bf16[96,2,128]{2,1,0:T(2,128)(2,1)S(1)} %copy-done.41), channel_id=1, replica_groups=mesh['dp'=16,'tensor'=2] {'dp'}, dimensions={0}, use_global_device_ids=true | all-gather | bytes 835584 | tf_op jit(solution)/shard_map/all_gather | solution.py:128
  117.6 46.8 %all-gather.8.cloned.1.call-done = bf16[1536,2,1536]{2,1,0:T(2,128)(2,1)} async-done(((bf16[96,2,1536]{2,1,0:T(2,128)(2,1)}), bf16[1536,2,1536]{2,1,0:T(2,128)(2,1)}) %all-gather.8.cloned.1.call-update) | async-done | bytes 9437200 | tf_op jit(solution)/shard_map/all_gather | solution.py:127
  164.4 10.5 copy.221
  174.9 12.4 fusion.166
  198.1 15.3 fusion.116
  213.4 9.9 reshape.573
  223.3 9.9 copy.140
  236.6 97.7 %while.45 = (s32[]{:T(128)}, f32[24,128,64]{1,2,0:T(8,128)S(1)}, s32[]{:T(128)}, f32[4,256,24,64]{1,3,2,0:T(8,128)}, f32[4,24,128,64]{2,3,1,0:T(8,128)}, /*index...) while((s32[]{:T(128)}, f32[24,128,64]{1,2,0:T(8,128)S(1)}, ...), condition=%wide.region_4.5_spmd.clone, body=%wide.region_1.4_spmd.clone.sunk | while | flops 2525926400 | bytes 14220909 | solution.py:93
  251.1 9.4 bitcast_dynamic-update-slice_fusion.7
  275.5 9.4 bitcast_dynamic-update-slice_fusion.7
  299.9 9.4 bitcast_dynamic-update-slice_fusion.7
  324.2 9.4 bitcast_dynamic-update-slice_fusion.7
  334.3 9.7 copy.155
  344.0 11.2 reshape.566
  355.2 10.0 multiply_reduce_fusion.12
  367.7 11.5 multiply_reduce_fusion.5
  381.7 18.8 %multiply_reduce_fusion.6 = (f32[1536]{0:T(1024)}, f32[1024,1536]{1,0:T(8,128)}, f32[1024,1536]{1,0:T(8,128)}) fusion(f32[1024,1536]{1,0:T(8,128)} %get-tuple-element.811, f32[1024,3072]{1,0:T(8,128)} %copy-done.1, f32[1024]{0:T(1024)S(1)} %broadcast_multiply_fusion.7, f32[1024,1536]{1,0:T(8,128)} %get-tuple-element.807, f32[1024]{0:T(1024)S(1)} %get-tuple-element.844, ...), kind=kLoop, calls=%fused_computation.166 | loop fusion | flops 39320064 | bytes 44070912 | tf_op jit(solution)/shard_map/transpose(jvp())/reduce_sum | solution.py:95
  400.5 10.0 reshape.567
  410.5 9.8 copy.149
  426.7 247.5 %while.46 = (s32[]{:T(128)}, f32[24,128,64]{1,2,0:T(8,128)S(1)}, f32[4,256,24,64]{1,3,2,0:T(8,128)}, f32[4,256,128]{2,1,0:T(8,128)}, f32[4,256,128]{2,1,0:T(8,12...) while((s32[]{:T(128)}, f32[24,128,64]{1,2,0:T(8,128)S(1)}, ...), condition=%wide.region_23.24_spmd.clone, body=%wide.region_10.23_spmd.clone.sunk | while | flops 5771760640 | bytes 49443552 | solution.py:93
  440.1 11.9 fusion.265
  480.7 8.0 bitcast_dynamic-update-slice_fusion.8
  501.9 11.9 fusion.265
  542.4 8.0 bitcast_dynamic-update-slice_fusion.8
  563.6 11.9 fusion.265
  604.1 8.0 bitcast_dynamic-update-slice_fusion.8
  625.4 11.9 fusion.265
  665.9 8.0 bitcast_dynamic-update-slice_fusion.8
  678.4 9.8 copy.158
  688.2 11.4 reshape.568
  699.7 13.3 multiply_reduce_fusion.10
  713.0 9.2 multiply_reduce_fusion.9
  722.3 6.3 slice_multiply_fusion.1
  734.1 6.3 slice_multiply_fusion.2
  740.6 14.1 fusion.156
  754.6 17.5 %fusion.134 = f32[1024,1536]{1,0:T(8,128)} fusion(bf16[1536,3072]{1,0:T(8,128)(2,1)} %bitcast.471, f32[1024,1536]{1,0:T(8,128)} %get-tuple-element.831, f32[1024,1536]{1,0:T(8,128)} %get-tuple-element.830), kind=kOutput, calls=%fused_computation.219 | convolution fusion | flops 9669967872 | bytes 28311552 | tf_op jit(solution)/shard_map/tc,dc->td/dot_general | solution.py:214
  772.2 6.5 convolution_add_fusion.2
  779.3 10.6 fusion.155
  790.0 18.1 %fusion.133 = f32[1536,3072]{1,0:T(8,128)} fusion(bf16[1024,1536]{1,0:T(8,128)(2,1)S(1)} %copy-done.6, f32[1024,1536]{1,0:T(8,128)} %get-tuple-element.831, f32[1024,1536]{1,0:T(8,128)} %get-tuple-element.830), kind=kOutput, calls=%fused_computation.218 | convolution fusion | flops 9669967872 | bytes 34603008 | tf_op jit(solution)/shard_map/td,tc->dc/dot_general | solution.py:207
  808.1 24.7 %reshape.536 = f32[1536,2,1536]{2,1,0:T(2,128)} reshape(f32[1536,3072]{1,0:T(8,128)} %fusion.133) | data formatting | bytes 37748736 | tf_op jit(solution)/shard_map/reshape | solution.py:209
  842.4 10.6 fusion.154
  855.2 8.7 reduce-scatter.13.cloned.1.call-done
  865.4 77.9 %all-reduce.30 = (f32[4,1536]{1,0:T(4,128)}, f32[1536]{0:T(1024)}, f32[4,2,128]{2,1,0:T(2,128)}, f32[2,128]{1,0:T(2,128)}, f32[24]{0:T(128)}, /*index=5*/f32[24]{0:T(128)}, f32[24]{0:T(128)}, f32[1536]{0:T(1024)}) all-reduce(f32[4,1536]{1,0:T(4,128)S(1)} %pad_add_fusion.1, ...), channel_id=1, replica_groups=mesh['dp'=16,'tensor'=2] {'dp'}, use_global_device_ids=true, to_apply=%region_36.37 | all-reduce | flops 10568 | bytes 84544 | tf_op jit(solution)/shard_map/psum | solution.py:244
  948.4 41.2 %psum.87 = f32[1536]{0:T(1024)} all-reduce(f32[1536]{0:T(1024)S(1)} %get-tuple-element.712), channel_id=1, replica_groups=mesh['dp'=16,'tensor'=2] {'dp','tensor'}, use_global_device_ids=true, to_apply=%region_28.29 | all-reduce | flops 1536 | bytes 12288 | tf_op jit(solution)/shard_map/psum | solution.py:237
  989.6 5.4 fusion.118
  995.0 451.7 %all-reduce.37.cloned.1.call-done = (f32[1536,2,1536]{2,1,0:T(2,128)}, f32[1536,2,128]{2,1,0:T(2,128)}) async-done(((f32[1536,2,1536]{2,1,0:T(2,128)}, f32[1536,2,128]{2,1,0:T(2,128)}), (f32[1536,2,1536]{2,1,0:T(2,128)}, f32[1536,2,128]{2,1,0:T(2,128)})) %all-reduce.37.cloned.1.call-update) | async-done | bytes 20447248
  1450.6 172.6 %reduce-scatter.11.cloned.1.call-done = f32[1536,96]{0,1:T(8,128)} async-done(((f32[1536,1536]{0,1:T(8,128)}), f32[1536,96]{0,1:T(8,128)}) %reduce-scatter.11.cloned.1.call-update) | async-done | bytes 589840 | tf_op jit(solution)/shard_map/reduce_scatter | solution.py:242
  (536 shorter events, 291.5 us)
Async XLA Ops:
  7.3 52.5 %copy-start.41 = (bf16[96,2,128]{2,1,0:T(2,128)(2,1)S(1)}, bf16[96,2,128]{2,1,0:T(2,128)(2,1)}, u32[]{:S(2)}) copy-start(bf16[96,2,128]{2,1,0:T(2,128)(2,1)} %param.24) | copy-start | bytes 147460
  7.3 101.1 %all-gather.6.cloned.1.call-start = ((), (), s32[]{:S(2)}) async-start(), calls=%async_computation.4 | async-start | bytes 4718592 | tf_op jit(solution)/shard_map/all_gather | solution.py:132
  9.8 98.6 %copy-start.43 = (f32[512]{0:T(512)}, f32[512]{0:T(512)S(1)}, u32[]{:S(2)}) copy-start(f32[512]{0:T(512)S(1)} %get-tuple-element.854) | copy-start | bytes 6148
  12.8 151.7 %all-gather.8.cloned.1.call-start = ((), (), s32[]{:S(2)}) async-start(), calls=%async_computation.5 | async-start | bytes 10027008 | tf_op jit(solution)/shard_map/all_gather | solution.py:127
  13.5 354.2 %all-gather.12.cloned.1.call-start = ((), (), s32[]{:S(2)}) async-start(), calls=%async_computation.8 | async-start | bytes 4718592 | tf_op jit(solution)/shard_map/all_gather | solution.py:179
  13.7 94.7 %copy-start.46 = (f32[512]{0:T(512)}, f32[512]{0:T(512)S(1)}, u32[]{:S(2)}) copy-start(f32[512]{0:T(512)S(1)} %fusion.150) | copy-start | bytes 6148
  15.2 96.7 %copy-start.68 = (f32[2,128]{1,0:T(2,128)S(1)}, f32[2,128]{1,0:T(2,128)}, u32[]{:S(2)}) copy-start(f32[2,128]{1,0:T(2,128)} %param.29) | copy-start | bytes 3076
  15.2 352.5 %all-gather.10.cloned.1.call-start = ((), (), s32[]{:S(2)}) async-start(), calls=%async_computation.6 | async-start | bytes 5013504 | tf_op jit(solution)/shard_map/all_gather | solution.py:130
  15.8 817.0 %all-reduce.35.cloned.1.call-start = ((), (), s32[]{:S(2)}) async-start(), calls=%async_computation.10 | async-start | bytes 2097152 | tf_op jit(solution)/shard_map/psum | solution.py:202
  15.9 99.4 %copy-start.64 = (f32[24]{0:T(128)}, f32[24]{0:T(128)S(1)}, u32[]{:S(2)}) copy-start(f32[24]{0:T(128)S(1)} %exponential_negate_fusion) | copy-start | bytes 292
  15.9 98.3 %copy-start.50 = (f32[256]{0:T(256)}, f32[256]{0:T(256)S(1)}, u32[]{:S(2)}) copy-start(f32[256]{0:T(256)S(1)} %get-tuple-element.846) | copy-start | bytes 3076
  16.0 98.3 %copy-start.52 = (f32[256]{0:T(256)}, f32[256]{0:T(256)S(1)}, u32[]{:S(2)}) copy-start(f32[256]{0:T(256)S(1)} %get-tuple-element.847) | copy-start | bytes 3076
  16.0 98.3 %copy-start.54 = (f32[256]{0:T(256)}, f32[256]{0:T(256)S(1)}, u32[]{:S(2)}) copy-start(f32[256]{0:T(256)S(1)} %get-tuple-element.849) | copy-start | bytes 3076
  16.0 98.3 %copy-start.56 = (f32[256]{0:T(256)}, f32[256]{0:T(256)S(1)}, u32[]{:S(2)}) copy-start(f32[256]{0:T(256)S(1)} %get-tuple-element.848) | copy-start | bytes 3076
  16.1 365.6 %copy-start.23 = (f32[1536]{0:T(1024)}, f32[1536]{0:T(1024)S(1)}, u32[]{:S(2)}) copy-start(f32[1536]{0:T(1024)S(1)} %mul.1015) | copy-start | bytes 18436
  16.2 181.8 %copy-start.33 = (f32[1536]{0:T(1024)}, f32[1536]{0:T(1024)S(1)}, u32[]{:S(2)}) copy-start(f32[1536]{0:T(1024)S(1)} %get-tuple-element.716) | copy-start | bytes 18436
  16.2 181.8 %copy-start.35 = (f32[1536]{0:T(1024)}, f32[1536]{0:T(1024)S(1)}, u32[]{:S(2)}) copy-start(f32[1536]{0:T(1024)S(1)} %get-tuple-element.718) | copy-start | bytes 18436
  16.2 181.8 %copy-start.37 = (f32[1536]{0:T(1024)}, f32[1536]{0:T(1024)S(1)}, u32[]{:S(2)}) copy-start(f32[1536]{0:T(1024)S(1)} %get-tuple-element.717) | copy-start | bytes 18436
  16.2 181.8 %copy-start.39 = (f32[1536]{0:T(1024)}, f32[1536]{0:T(1024)S(1)}, u32[]{:S(2)}) copy-start(f32[1536]{0:T(1024)S(1)} %get-tuple-element.719) | copy-start | bytes 18436
  59.8 55.6 %copy-start.20 = (bf16[1536,24]{0,1:T(8,128)(2,1)}, bf16[1536,24]{0,1:T(8,128)(2,1)S(1)}, u32[]{:S(2)}) copy-start(bf16[1536,24]{0,1:T(8,128)(2,1)S(1)} %reshape.549) | copy-start | bytes 221188
  108.3 89.8 %copy-start.26 = (f32[1024]{0:T(1024)}, f32[1024]{0:T(1024)S(1)}, u32[]{:S(2)}) copy-start(f32[1024]{0:T(1024)S(1)} %get-tuple-element.850) | copy-start | bytes 12292
  108.3 89.8 %copy-start.28 = (f32[1024]{0:T(1024)}, f32[1024]{0:T(1024)S(1)}, u32[]{:S(2)}) copy-start(f32[1024]{0:T(1024)S(1)} %get-tuple-element.851) | copy-start | bytes 12292
  108.3 89.8 %copy-start.30 = (f32[1024]{0:T(1024)}, f32[1024]{0:T(1024)S(1)}, u32[]{:S(2)}) copy-start(f32[1024]{0:T(1024)S(1)} %get-tuple-element.852) | copy-start | bytes 12292
  367.7 14.0 copy-start.48
  428.9 29.9 %copy-start.11 = (f32[256,24]{0,1:T(8,128)}, f32[256,24]{0,1:T(8,128)S(1)}, u32[]{:S(2)}) copy-start(f32[256,24]{0,1:T(8,128)S(1)} %get-tuple-element.1078) | copy-start | bytes 73732 | tf_op jit(solution)/shard_map/transpose(jvp())/while
  490.6 29.9 %copy-start.11 = (f32[256,24]{0,1:T(8,128)}, f32[256,24]{0,1:T(8,128)S(1)}, u32[]{:S(2)}) copy-start(f32[256,24]{0,1:T(8,128)S(1)} %get-tuple-element.1078) | copy-start | bytes 73732 | tf_op jit(solution)/shard_map/transpose(jvp())/while
  500.6 13.2 copy-start.18
  552.4 29.9 %copy-start.11 = (f32[256,24]{0,1:T(8,128)}, f32[256,24]{0,1:T(8,128)S(1)}, u32[]{:S(2)}) copy-start(f32[256,24]{0,1:T(8,128)S(1)} %get-tuple-element.1078) | copy-start | bytes 73732 | tf_op jit(solution)/shard_map/transpose(jvp())/while
  614.1 29.9 %copy-start.11 = (f32[256,24]{0,1:T(8,128)}, f32[256,24]{0,1:T(8,128)S(1)}, u32[]{:S(2)}) copy-start(f32[256,24]{0,1:T(8,128)S(1)} %get-tuple-element.1078) | copy-start | bytes 73732 | tf_op jit(solution)/shard_map/transpose(jvp())/while
  678.4 185.5 %reduce-scatter.13.cloned.1.call-start = ((), (), s32[]{:S(2)}) async-start(), calls=%async_computation.12 | async-start | bytes 835584
  688.2 24.8 %slice-start = ((s8[6291456]{0:T(1024)(128)(4,1)}), s8[2097152]{0:T(1024)(128)(4,1)S(1)}, s32[]{:S(2)}) async-start(s8[6291456]{0:T(1024)(128)(4,1)} %bitcast.465), calls=%async_computation.14 | async-start | bytes 4194304
  699.6 13.3 slice-start.1
  699.6 13.3 copy-start.27
  699.7 13.3 copy-start.29
  740.5 202.8 %reduce-scatter.9.cloned.1.call-start = ((), (), s32[]{:S(2)}) async-start(), calls=%async_computation.9 | async-start | bytes 9437184 | tf_op jit(solution)/shard_map/reduce_scatter | solution.py:223
  754.6 17.5 %copy-start.21 = (bf16[1536,24]{0,1:T(8,128)(2,1)S(1)}, bf16[1536,24]{0,1:T(8,128)(2,1)}, u32[]{:S(2)}) copy-start(bf16[1536,24]{0,1:T(8,128)(2,1)} %copy-done.20) | copy-start | bytes 221188
  778.7 210.9 %reduce-scatter.7.cloned.1.call-start = ((), (), s32[]{:S(2)}) async-start(), calls=%async_computation.7 | async-start | bytes 9437184 | tf_op jit(solution)/shard_map/reduce_scatter | solution.py:169
  790.0 656.7 %all-reduce.37.cloned.1.call-start = ((), (), s32[]{:S(2)}) async-start(), calls=%async_computation.13 | async-start | bytes 40894464
  808.1 24.7 %copy-start.3 = (f32[1024,256]{1,0:T(8,128)S(1)}, f32[1024,256]{1,0:T(8,128)}, u32[]{:S(2)}) copy-start(f32[1024,256]{1,0:T(8,128)} %copy-done.2) | copy-start | bytes 3145732
  808.1 24.7 %copy-start.15 = (f32[1024,256]{1,0:T(8,128)S(1)}, f32[1024,256]{1,0:T(8,128)}, u32[]{:S(2)}) copy-start(f32[1024,256]{1,0:T(8,128)} %get-tuple-element.809) | copy-start | bytes 3145732
  808.1 26.5 %copy-start.57 = (f32[256]{0:T(256)S(1)}, f32[256]{0:T(256)}, u32[]{:S(2)}) copy-start(f32[256]{0:T(256)} %copy-done.56) | copy-start | bytes 3076
  840.5 782.8 %reduce-scatter.11.cloned.1.call-start = ((), (), s32[]{:S(2)}) async-start(), calls=%async_computation.11 | async-start | bytes 10027008 | tf_op jit(solution)/shard_map/reduce_scatter | solution.py:242
  853.0 90.3 %copy-start.8 = (bf16[512,1536]{1,0:T(8,128)(2,1)S(1)}, bf16[512,1536]{1,0:T(8,128)(2,1)}, u32[]{:S(2)}) copy-start(bf16[512,1536]{1,0:T(8,128)(2,1)} %param.20) | copy-start | bytes 4718596
  853.0 90.3 %copy-start.32 = (f32[1536]{0:T(1024)S(1)}, f32[1536]{0:T(1024)}, u32[]{:S(2)}) copy-start(f32[1536]{0:T(1024)} %param.22) | copy-start | bytes 18436
  853.0 90.3 %copy-start.44 = (f32[512]{0:T(512)S(1)}, f32[512]{0:T(512)}, u32[]{:S(2)}) copy-start(f32[512]{0:T(512)} %copy-done.43) | copy-start | bytes 6148
  853.1 136.5 %copy-start.14 = (bf16[512,1536]{1,0:T(8,128)(2,1)S(1)}, bf16[512,1536]{1,0:T(8,128)(2,1)}, u32[]{:S(2)}) copy-start(bf16[512,1536]{1,0:T(8,128)(2,1)} %param.35) | copy-start | bytes 4718596
  853.1 136.5 %copy-start.47 = (f32[512]{0:T(512)S(1)}, f32[512]{0:T(512)}, u32[]{:S(2)}) copy-start(f32[512]{0:T(512)} %copy-done.46) | copy-start | bytes 6148
  853.1 136.5 %copy-start.60 = (f32[512]{0:T(512)S(1)}, f32[512]{0:T(512)}, u32[]{:S(2)}) copy-start(f32[512]{0:T(512)} %get-tuple-element.853) | copy-start | bytes 6148
  (56 other events, 372.5 us)
Sparse Core Ops, SparseCore 0:
  12.9 14.8 all-gather.5
  30.6 133.7 all-gather.7
  166.0 10.2 all-gather.11
  179.0 80.8 all-gather.9
  678.5 18.7 all-reduce.34
  740.6 123.2 reduce-scatter.12
  866.2 13.0 reduce-scatter.8
  881.6 16.0 reduce-scatter.6
  904.1 542.5 all-reduce.36
  1452.8 170.3 reduce-scatter.10
where the time goes:
time: 1640 us; the launch traced here: 1630 us
  waiting for transfers between devices  681 us (42%)
  matrix products  316 us (19%)
  local copies, waits for them, and re-layouts  222 us (14%)
  blocking collectives  216 us (13%)
  other arithmetic  167 us (10%)
    unnamed x12, waiting for transfers between devices  462 us
    reduce_scatter x1, waiting for transfers between devices, shards(): lax.psum_scatter(grad_out_proj, 'dp', scatter_dimension=1, tiled=True)  173 us
    dot_general x12, matrix products, span_step(): within = jnp.einsum('hts,shp->thp', mixing, inner_blk, precision=HIGHEST)  117 us
    psum x1, blocking collectives, shards(): lax.psum((grad_conv_inner, grad_conv_inner_bias, grad_conv_state, grad_co...  77.9 us
    all_gather x1, blocking collectives, shards(): lax.all_gather(in_state, 'dp', axis=0, tiled=True)  48.5 us
    all_gather x1, waiting for transfers between devices, shards(): lax.all_gather(in_gate_inner, 'dp', axis=0, tiled=True)  46.8 us
    unnamed x151, local copies, waits for them, and re-layouts  43.4 us
    all_gather x1, blocking collectives, shards(): lax.all_gather(in_step, 'dp', axis=0, tiled=True)  43.3 us
  transfers between devices with their start and end apart: 10, of which 4 were waited for; matrix products, arithmetic and copies ran while one was open for 24% of the time, Pallas kernels for 0%

commit v1 on v0

--- a/solution.py
+++ b/solution.py
@@ -123,19 +123,28 @@
     own_rows = tokens.astype(jnp.float32)
     row_scale = lax.rsqrt(jnp.mean(own_rows * own_rows, axis=1, keepdims=True) + EPSILON)
     normed_own = (own_rows * row_scale * norm_gain[None, :]).astype(jnp.bfloat16)
-    gate_weights, state_weights, step_weights, out_weights = (
-        lax.all_gather(in_gate_inner, "dp", axis=0, tiled=True),
-        lax.all_gather(in_state, "dp", axis=0, tiled=True),
-        lax.all_gather(in_step, "dp", axis=0, tiled=True),
-        lax.all_gather(out_proj, "dp", axis=1, tiled=True),
-    )
+    packed_in = jnp.concatenate(
+        [
+            in_gate_inner.reshape(in_gate_inner.shape[0], -1),
+            in_state.reshape(in_state.shape[0], -1),
+            in_step,
+            jnp.zeros((in_step.shape[0], -in_step.shape[1] % 128), jnp.bfloat16),
+        ],
+        axis=1,
+    )
+    packed_weights = lax.all_gather(packed_in, "dp", axis=0, tiled=True)
+    out_weights_t = lax.all_gather(out_proj.T, "dp", axis=0, tiled=True)
+    inner_dev = in_gate_inner.shape[2]
+    state_end = 2 * inner_dev + 2 * in_state.shape[2]
+    gate_weights = packed_weights[:, : 2 * inner_dev]
+    state_weights = packed_weights[:, 2 * inner_dev : state_end]
+    step_weights = packed_weights[:, state_end : state_end + in_step.shape[1]]
     normed = lax.all_gather(normed_own, "tensor", axis=0, tiled=True)
-    inner_dev = gate_weights.shape[2]
     gate_inner = jnp.dot(
-        normed, gate_weights.reshape(model_width, 2 * inner_dev), preferred_element_type=jnp.float32
+        normed, gate_weights, preferred_element_type=jnp.float32
     )
     state_proj = jnp.dot(
-        normed, state_weights.reshape(model_width, -1), preferred_element_type=jnp.float32
+        normed, state_weights, preferred_element_type=jnp.float32
     )
     step_proj = jnp.dot(normed, step_weights, preferred_element_type=jnp.float32)
 
@@ -165,23 +174,19 @@
     squares = lax.psum(jnp.sum(gated_values * gated_values, axis=1), "tensor")
     gate_scale = lax.rsqrt(squares / full_inner + EPSILON)[:, None]
     normed_inner = (gated_values * gate_scale * gate_gain[None, :]).astype(jnp.bfloat16)
-    partial_out = jnp.dot(normed_inner, out_weights, preferred_element_type=jnp.float32)
+    partial_out = jnp.einsum(
+        "tc,dc->td", normed_inner, out_weights_t, preferred_element_type=jnp.float32
+    )
     branch_own = lax.psum_scatter(partial_out, "tensor", scatter_dimension=0, tiled=True)
     block_out = (own_rows + own_live * branch_own).astype(jnp.bfloat16)
-    gate_weights, state_weights, step_weights, out_weights = (
-        lax.all_gather(in_gate_inner, "dp", axis=0, tiled=True),
-        lax.all_gather(in_state, "dp", axis=0, tiled=True),
-        lax.all_gather(in_step, "dp", axis=0, tiled=True),
-        lax.all_gather(out_proj, "dp", axis=1, tiled=True),
-    )
     cot_rows = cotangent.astype(jnp.float32)
     branch_grad_own = (own_live * cot_rows).astype(jnp.bfloat16)
     branch_grad = lax.all_gather(branch_grad_own, "tensor", axis=0, tiled=True)
-    grad_out_proj = jnp.einsum(
-        "tc,td->cd", normed_inner, branch_grad, preferred_element_type=jnp.float32
+    grad_out_proj_t = jnp.einsum(
+        "td,tc->dc", branch_grad, normed_inner, preferred_element_type=jnp.float32
     )
     grad_normed_inner = jnp.einsum(
-        "td,cd->tc", branch_grad, out_weights, preferred_element_type=jnp.float32
+        "td,dc->tc", branch_grad, out_weights_t, preferred_element_type=jnp.float32
     )
     grad_gate_gain = jnp.sum(grad_normed_inner * gated_values * gate_scale, axis=0)
     scaled_grad = grad_normed_inner * gate_gain[None, :]
@@ -204,17 +209,37 @@
     low_gate_inner = grad_gate_inner.astype(jnp.bfloat16)
     low_state = grad_state_proj.astype(jnp.bfloat16)
     low_step = grad_step_proj.astype(jnp.bfloat16)
-    grad_in_gate_inner = jnp.einsum(
-        "td,tc->dc", normed, low_gate_inner, preferred_element_type=jnp.float32
-    ).reshape(model_width, 2, inner_dev)
-    grad_in_state = jnp.einsum(
-        "td,tc->dc", normed, low_state, preferred_element_type=jnp.float32
-    ).reshape(model_width, 2, -1)
-    grad_in_step = jnp.einsum("td,th->dh", normed, low_step, preferred_element_type=jnp.float32)
+    grad_gate_half = jnp.einsum(
+        "td,tc->dc", normed, low_gate_inner[:, :inner_dev], preferred_element_type=jnp.float32
+    )
+    early_part = lax.psum_scatter(
+        jnp.concatenate([grad_out_proj_t, grad_gate_half], axis=1).astype(jnp.bfloat16),
+        "dp",
+        scatter_dimension=0,
+        tiled=True,
+    ).astype(jnp.float32)
+    low_late = jnp.concatenate(
+        [
+            low_gate_inner[:, inner_dev:],
+            low_state,
+            low_step,
+            jnp.zeros((low_step.shape[0], -low_step.shape[1] % 128), jnp.bfloat16),
+        ],
+        axis=1,
+    )
+    grad_late = jnp.einsum("td,tc->dc", normed, low_late, preferred_element_type=jnp.float32)
+    late_part = lax.psum_scatter(
+        grad_late.astype(jnp.bfloat16), "dp", scatter_dimension=0, tiled=True
+    ).astype(jnp.float32)
+    grad_out_proj = early_part[:, :inner_dev].T
+    grad_in_gate_inner = jnp.stack([early_part[:, inner_dev:], late_part[:, :inner_dev]], axis=1)
+    late_state = inner_dev + low_state.shape[1]
+    grad_in_state = late_part[:, inner_dev:late_state].reshape(in_state.shape)
+    grad_in_step = late_part[:, late_state : late_state + low_step.shape[1]]
     head_grads = jnp.einsum(
         "tc,dc->td",
         low_gate_inner,
-        gate_weights.reshape(model_width, 2 * inner_dev),
+        gate_weights,
         preferred_element_type=jnp.float32,
     )
     head_grads = head_grads + jnp.einsum(
@@ -225,7 +250,7 @@
     normed_grad_own = normed_grad_own + jnp.einsum(
         "tc,dc->td",
         own_state_grad,
-        state_weights.reshape(model_width, -1),
+        state_weights,
         preferred_element_type=jnp.float32,
     )
     grad_norm_part = jnp.sum(normed_grad_own * own_rows * row_scale, axis=0)
@@ -234,42 +259,51 @@
     grad_tokens = (
         cot_rows + row_scale * scaled_rows - own_rows * row_scale**3 * row_products / model_width
     )
-    grad_norm_gain = lax.psum(grad_norm_part, ("dp", "tensor"))
-    summed_weights = (
-        lax.psum_scatter(grad_in_gate_inner, "dp", scatter_dimension=0, tiled=True),
-        lax.psum_scatter(grad_in_state, "dp", scatter_dimension=0, tiled=True),
-        lax.psum_scatter(grad_in_step, "dp", scatter_dimension=0, tiled=True),
-        lax.psum_scatter(grad_out_proj, "dp", scatter_dimension=1, tiled=True),
-    )
-    summed_small = lax.psum(
-        (
-            grad_conv_inner,
-            grad_conv_inner_bias,
-            grad_conv_state,
-            grad_conv_state_bias,
-            grad_step_bias,
-            grad_decay_log,
-            grad_skip_gain,
-            grad_gate_gain,
-        ),
-        "dp",
-    )
+    split_parts = (
+        grad_conv_inner,
+        grad_conv_inner_bias,
+        grad_step_bias,
+        grad_decay_log,
+        grad_skip_gain,
+        grad_gate_gain,
+    )
+    half_state = 1.0 / lax.axis_size("tensor")
+    whole_parts = (grad_norm_part, grad_conv_state * half_state, grad_conv_state_bias * half_state)
+    split_row = jnp.concatenate([part.reshape(-1) for part in split_parts])
+    split_rows = jnp.zeros((lax.axis_size("tensor"), split_row.shape[0]), jnp.float32)
+    split_rows = lax.dynamic_update_slice(split_rows, split_row[None], (tensor_place, 0))
+    whole_row = jnp.concatenate([part.reshape(-1) for part in whole_parts])
+    summed = lax.psum(jnp.concatenate([split_rows.reshape(-1), whole_row]), ("dp", "tensor"))
+    split_sum = lax.dynamic_slice_in_dim(
+        summed, tensor_place * split_row.shape[0], split_row.shape[0]
+    )
+    whole_sum = summed[split_rows.size :]
+
+    def unpack(row, parts):
+        pieces, start = [], 0
+        for part in parts:
+            pieces.append(row[start : start + part.size].reshape(part.shape))
+            start += part.size
+        return pieces
+
+    split_out = unpack(split_sum, split_parts)
+    whole_out = unpack(whole_sum, whole_parts)
     return (
         block_out,
         grad_tokens,
-        grad_norm_gain,
-        summed_weights[0],
-        summed_weights[1],
-        summed_weights[2],
-        summed_small[0],
-        summed_small[1],
-        summed_small[2],
-        summed_small[3],
-        summed_small[4],
-        summed_small[5],
-        summed_small[6],
-        summed_small[7],
-        summed_weights[3],
+        whole_out[0],
+        grad_in_gate_inner,
+        grad_in_state,
+        grad_in_step,
+        split_out[0],
+        split_out[1],
+        whole_out[1],
+        whole_out[2],
+        split_out[2],
+        split_out[3],
+        split_out[4],
+        split_out[5],
+        grad_out_proj,
     )
 
 

time: 1640 us -> 1280 us (0.78)
  blocking collectives: 216 us -> 5.27 us
  waiting for transfers between devices: 681 us -> 536 us
  other arithmetic: 167 us -> 187 us
    reduce_scatter x1 -> x0, waiting for transfers between devices: 173 us -> none  [shards(): lax.psum_scatter(grad_out_proj, 'dp', scatter_dimension=1, tiled=True)]
    unnamed x12, waiting for transfers between devices: 462 us -> 320 us
    psum x2 -> x0, blocking collectives: 119 us -> none  [the longest x1 77.9 us: shards(): lax.psum((grad_conv_inner, grad_conv_inner_bias, grad_conv_state, grad_co...]
    all_gather x2 -> x0, blocking collectives: 91.8 us -> none  [the longest x1 48.5 us: shards(): lax.all_gather(in_state, 'dp', axis=0, tiled=True)]
    all_gather x2, waiting for transfers between devices: 46.8 us -> 137 us  [the longest x1 137 us: shards(): packed_weights = lax.all_gather(packed_in, 'dp', axis=0, tiled=True)]
    psum x0 -> x1, waiting for transfers between devices: none -> 68.1 us  [shards(): lax.psum(jnp.concatenate([split_rows.reshape(-1), whole_row]), ('dp', 'te...]
    reshape x3 -> x4, local copies, waits for them, and re-layouts: 26.7 us -> 2.06 us  [the longest x2 1.93 us: unpack(): pieces.append(row[start:start + part.size].reshape(part.shape))]
    dynamic_update_slice x20 -> x4, local copies, waits for them, and re-layouts: 21.3 us -> 0.46 us  [mixer(): unused, ssd_out = lax.scan(jax.checkpoint(span_step), initial, scanned)]
  transfers between devices with their start and end apart: 10 -> 10, of which waited for: 4 -> 5; matrix products, arithmetic and copies ran while one was open for 24% -> 31% of each run, Pallas kernels for 0% -> 0%
where the time goes in v1:
time: 1280 us; the launch traced here: 1270 us
  waiting for transfers between devices  536 us (42%)
  matrix products  302 us (24%)
  local copies, waits for them, and re-layouts  209 us (16%)
  other arithmetic  187 us (15%)
  between operations  15.4 us (1%)
    unnamed x12, waiting for transfers between devices  320 us
    all_gather x1, waiting for transfers between devices, shards(): packed_weights = lax.all_gather(packed_in, 'dp', axis=0, tiled=True)  137 us
    dot_general x12, matrix products, span_step(): within = jnp.einsum('hts,shp->thp', mixing, inner_blk, precision=HIGHEST)  116 us
    psum x1, waiting for transfers between devices, shards(): lax.psum(jnp.concatenate([split_rows.reshape(-1), whole_row]), ('dp', 'te...  68.1 us
    unnamed x160, local copies, waits for them, and re-layouts  47.1 us
    dot_general x12, matrix products, span_step(): jnp.einsum('sn,shp->hnp', state_in, inner_blk * to_end[:, :, None], preci...  40.5 us
    reshape x3, local copies, waits for them, and re-layouts, mixer(): heads_inner.reshape(blocks, SPAN, heads_dev, head_size)  31.4 us
    reshape x3, local copies, waits for them, and re-layouts, mixer(): ssd_out.reshape(length, heads_dev, head_size)  30.8 us
  transfers between devices with their start and end apart: 10, of which 5 were waited for; matrix products, arithmetic and copies ran while one was open for 31% of the time, Pallas kernels for 0%

profile of v1, /device:TPU:0, one launch (start us, length us, event | category | flops | bytes accessed | tf_op | source)
XLA Modules:
  0.0 1267.4 jit_solution(6069346290562899713)
XLA Ops:
  17.6 10.3 all-gather.5.cloned.1.call-done
  27.9 137.3 %all-gather.7.cloned.1.call-done = bf16[1536,3456]{1,0:T(8,128)(2,1)} async-done(((bf16[96,3456]{1,0:T(8,128)(2,1)}), bf16[1536,3456]{1,0:T(8,128)(2,1)}) %all-gather.7.cloned.1.call-update) | async-done | bytes 10616848 | tf_op jit(solution)/shard_map/all_gather | solution.py:135
  165.2 13.4 %fusion.113 = f32[1024,3072]{1,0:T(8,128)S(1)} fusion(bf16[1024,1536]{1,0:T(8,128)(2,1)} %all-gather.5.cloned.1.call-done, bf16[1536,3456]{1,0:T(8,128)(2,1)} %all-gather.7.cloned.1.call-done), kind=kOutput, calls=%fused_computation.156 | convolution fusion | flops 9663676416 | bytes 25165824 | tf_op jit(solution)/shard_map/dot_general | solution.py:143
  202.2 15.3 %fusion.120 = (f32[1024,1536]{1,0:T(8,128)}, f32[1024,1536]{1,0:T(8,128)}) fusion(f32[1024]{0:T(1024)S(1)} %get-tuple-element.923, f32[1021,1536]{1,0:T(8,128)} %slice.270, f32[1536]{0:T(1024)S(1)} %get-tuple-element.793, f32[1024]{0:T(1024)S(1)} %get-tuple-element.922, f32[1022,1536]{1,0:T(8,128)} %slice.269, f32[1536]{0:T(1024)S(1)} %get-tuple-element.794, ...), kind=kLoop, calls=%fused_computation.189 | loop fusion | flops 23592960 | bytes 37754880 | tf_op jit(solution)/shard_map/jvp(jit(silu))/mul | solution.py:78
  217.5 10.0 reshape.585
  227.5 9.8 copy.155
  240.7 98.6 %while.45 = (s32[]{:T(128)}, f32[24,128,64]{1,2,0:T(8,128)S(1)}, s32[]{:T(128)}, f32[4,256,24,64]{1,3,2,0:T(8,128)}, f32[4,24,128,64]{2,3,1,0:T(8,128)}, /*index...) while((s32[]{:T(128)}, f32[24,128,64]{1,2,0:T(8,128)S(1)}, ...), condition=%wide.region_4.5_spmd.clone, body=%wide.region_1.4_spmd.clone.sunk | while | flops 2525926400 | bytes 14220909 | solution.py:93
  255.4 9.4 bitcast_dynamic-update-slice_fusion.9
  280.0 9.4 bitcast_dynamic-update-slice_fusion.9
  304.6 9.4 bitcast_dynamic-update-slice_fusion.9
  329.2 9.4 bitcast_dynamic-update-slice_fusion.9
  339.3 9.7 copy.174
  349.0 11.1 reshape.578
  360.1 9.9 multiply_reduce_fusion.12
  372.5 11.5 multiply_reduce_fusion.5
  386.9 18.2 %multiply_reduce_fusion.6 = (f32[1536]{0:T(1024)}, f32[1024,1536]{1,0:T(8,128)}, f32[1024,1536]{1,0:T(8,128)}) fusion(f32[1024,1536]{1,0:T(8,128)} %get-tuple-element.876, f32[1024,3072]{1,0:T(8,128)} %copy-done.1, f32[1024]{0:T(1024)S(1)} %broadcast_multiply_fusion.7, f32[1024,1536]{1,0:T(8,128)} %get-tuple-element.872, f32[1024]{0:T(1024)S(1)} %get-tuple-element.915, ...), kind=kLoop, calls=%fused_computation.175 | loop fusion | flops 39320064 | bytes 44070912 | tf_op jit(solution)/shard_map/transpose(jvp())/reduce_sum | solution.py:95
  405.1 10.0 reshape.579
  415.1 9.7 copy.164
  431.2 234.4 %while.46 = (s32[]{:T(128)}, f32[24,128,64]{1,2,0:T(8,128)S(1)}, f32[4,256,24,64]{1,3,2,0:T(8,128)}, f32[4,256,128]{2,1,0:T(8,128)}, f32[4,256,128]{2,1,0:T(8,12...) while((s32[]{:T(128)}, f32[24,128,64]{1,2,0:T(8,128)S(1)}, ...), condition=%wide.region_23.24_spmd.clone, body=%wide.region_10.23_spmd.clone.sunk | while | flops 5771779072 | bytes 50224940 | solution.py:93
  445.6 4.7 fusion.268
  450.7 12.0 fusion.263
  482.2 7.7 bitcast_dynamic-update-slice_fusion.10
  509.2 12.0 fusion.263
  540.7 7.7 bitcast_dynamic-update-slice_fusion.10
  562.6 4.7 fusion.268
  567.7 12.0 fusion.263
  599.1 7.7 bitcast_dynamic-update-slice_fusion.10
  626.1 12.0 fusion.263
  657.6 7.7 bitcast_dynamic-update-slice_fusion.10
  671.0 10.0 copy.177
  681.0 11.4 reshape.580
  692.4 13.7 %multiply_reduce_fusion.10 = (f32[1536]{0:T(1024)}, f32[1024,1536]{1,0:T(8,128)}, f32[1024,1536]{1,0:T(8,128)S(1)}) fusion(f32[1021,1536]{1,0:T(8,128)} %slice.270, f32[1024]{0:T(1024)S(1)} %copy-done.29, f32[1024,1536]{1,0:T(8,128)} %get-tuple-element.876, f32[1024,1536]{1,0:T(8,128)} %reshape.580, f32[1024,1536]{1,0:T(8,128)} %get-tuple-element.861, ...), kind=kLoop, calls=%fused_computation.179 | loop fusion | flops 22018560 | bytes 37746688 | tf_op jit(solution)/shard_map/transpose(jvp())/reduce_sum | solution.py:27
  706.1 8.7 multiply_reduce_fusion.9
  730.0 10.2 fusion.159
  740.2 8.2 add_convert_fusion
  752.0 14.0 %fusion.121 = f32[1024,1536]{1,0:T(8,128)} fusion(f32[1024,1536]{1,0:T(8,128)S(1)} %fusion.149, bf16[1024,3072]{1,0:T(8,128)(2,1)S(1)} %bitcast.481, bf16[1536,3456]{1,0:T(8,128)(2,1)} %all-gather.7.cloned.1.call-done), kind=kOutput, calls=%fused_computation.191 | convolution fusion | flops 9665249280 | bytes 28311552 | tf_op jit(solution)/shard_map/tc,dc->td/dot_general | solution.py:239
  766.7 10.6 fusion.158
  786.3 6.6 concatenate.59
  792.9 5.8 fusion.134
  799.5 11.2 convolution_convert_fusion.2
  810.8 8.1 convolution_convert_fusion
  818.9 8.7 convolution_convert_fusion.1
  827.5 12.3 pad_maximum_fusion
  839.8 12.7 %copy.178 = bf16[1536,3072]{1,0:T(8,128)(2,1)} copy(bf16[1536,3072]{0,1:T(8,128)(2,1)} %pad_maximum_fusion) | data formatting | bytes 18874368
  853.2 5.5 fusion.125
  858.7 68.1 %all-reduce.33.cloned.1.call-done = f32[21392]{0:T(1024)} async-done(((f32[21392]{0:T(1024)}), f32[21392]{0:T(1024)}) %all-reduce.33.cloned.1.call-update) | async-done | bytes 85584 | tf_op jit(solution)/shard_map/psum | solution.py:276
  933.7 146.3 %reduce-scatter.15.cloned.1.call-done = bf16[96,1920]{1,0:T(8,128)(2,1)} async-done(((bf16[1536,1920]{1,0:T(8,128)(2,1)}), bf16[96,1920]{1,0:T(8,128)(2,1)}) %reduce-scatter.15.cloned.1.call-update) | async-done | bytes 368656
  1082.8 173.2 %reduce-scatter.13.cloned.1.call-done = bf16[96,3072]{1,0:T(8,128)(2,1)} async-done(((bf16[1536,3072]{1,0:T(8,128)(2,1)}), bf16[96,3072]{1,0:T(8,128)(2,1)}) %reduce-scatter.13.cloned.1.call-update) | async-done | bytes 589840
  (595 shorter events, 292.5 us)
Async XLA Ops:
  7.2 20.7 %all-gather.5.cloned.1.call-start = ((), (), s32[]{:S(2)}) async-start(), calls=%async_computation.4 | async-start | bytes 4718592 | tf_op jit(solution)/shard_map/all_gather | solution.py:142
  12.9 152.3 %all-gather.7.cloned.1.call-start = ((), (), s32[]{:S(2)}) async-start(), calls=%async_computation.5 | async-start | bytes 11280384 | tf_op jit(solution)/shard_map/all_gather | solution.py:135
  14.2 358.3 %all-gather.11.cloned.1.call-start = ((), (), s32[]{:S(2)}) async-start(), calls=%async_computation.8 | async-start | bytes 4718592 | tf_op jit(solution)/shard_map/all_gather | solution.py:184
  14.3 164.3 %copy-start.49 = (f32[512]{0:T(512)}, f32[512]{0:T(512)S(1)}, u32[]{:S(2)}) copy-start(f32[512]{0:T(512)S(1)} %fusion.156) | copy-start | bytes 6148
  15.9 356.6 %all-gather.9.cloned.1.call-start = ((), (), s32[]{:S(2)}) async-start(), calls=%async_computation.6 | async-start | bytes 5013504 | tf_op jit(solution)/shard_map/all_gather | solution.py:136
  16.5 766.5 %all-reduce.31.cloned.1.call-start = ((), (), s32[]{:S(2)}) async-start(), calls=%async_computation.10 | async-start | bytes 2097152 | tf_op jit(solution)/shard_map/psum | solution.py:207
  17.1 173.1 %copy-start.70 = (f32[24]{0:T(128)}, f32[24]{0:T(128)S(1)}, u32[]{:S(2)}) copy-start(f32[24]{0:T(128)S(1)} %exponential_negate_fusion) | copy-start | bytes 292
  17.2 180.8 %copy-start.53 = (f32[256]{0:T(256)}, f32[256]{0:T(256)S(1)}, u32[]{:S(2)}) copy-start(f32[256]{0:T(256)S(1)} %get-tuple-element.917) | copy-start | bytes 3076
  17.2 180.8 %copy-start.55 = (f32[256]{0:T(256)}, f32[256]{0:T(256)S(1)}, u32[]{:S(2)}) copy-start(f32[256]{0:T(256)S(1)} %get-tuple-element.918) | copy-start | bytes 3076
  17.2 180.8 %copy-start.57 = (f32[256]{0:T(256)}, f32[256]{0:T(256)S(1)}, u32[]{:S(2)}) copy-start(f32[256]{0:T(256)S(1)} %get-tuple-element.920) | copy-start | bytes 3076
  17.2 180.8 %copy-start.59 = (f32[256]{0:T(256)}, f32[256]{0:T(256)S(1)}, u32[]{:S(2)}) copy-start(f32[256]{0:T(256)S(1)} %get-tuple-element.919) | copy-start | bytes 3076
  17.4 369.5 %copy-start.21 = (f32[1536]{0:T(1024)}, f32[1536]{0:T(1024)S(1)}, u32[]{:S(2)}) copy-start(f32[1536]{0:T(1024)S(1)} %mul.1035) | copy-start | bytes 18436
  17.4 184.7 %copy-start.31 = (f32[1536]{0:T(1024)}, f32[1536]{0:T(1024)S(1)}, u32[]{:S(2)}) copy-start(f32[1536]{0:T(1024)S(1)} %get-tuple-element.791) | copy-start | bytes 18436
  17.4 184.7 %copy-start.33 = (f32[1536]{0:T(1024)}, f32[1536]{0:T(1024)S(1)}, u32[]{:S(2)}) copy-start(f32[1536]{0:T(1024)S(1)} %get-tuple-element.793) | copy-start | bytes 18436
  17.4 184.7 %copy-start.35 = (f32[1536]{0:T(1024)}, f32[1536]{0:T(1024)S(1)}, u32[]{:S(2)}) copy-start(f32[1536]{0:T(1024)S(1)} %get-tuple-element.792) | copy-start | bytes 18436
  17.5 184.7 %copy-start.37 = (f32[1536]{0:T(1024)}, f32[1536]{0:T(1024)S(1)}, u32[]{:S(2)}) copy-start(f32[1536]{0:T(1024)S(1)} %get-tuple-element.794) | copy-start | bytes 18436
  17.5 184.6 %copy-start.24 = (f32[1024]{0:T(1024)}, f32[1024]{0:T(1024)S(1)}, u32[]{:S(2)}) copy-start(f32[1024]{0:T(1024)S(1)} %get-tuple-element.921) | copy-start | bytes 12292
  17.6 184.6 %copy-start.26 = (f32[1024]{0:T(1024)}, f32[1024]{0:T(1024)S(1)}, u32[]{:S(2)}) copy-start(f32[1024]{0:T(1024)S(1)} %get-tuple-element.922) | copy-start | bytes 12292
  17.6 184.6 %copy-start.28 = (f32[1024]{0:T(1024)}, f32[1024]{0:T(1024)S(1)}, u32[]{:S(2)}) copy-start(f32[1024]{0:T(1024)S(1)} %get-tuple-element.923) | copy-start | bytes 12292
  360.1 12.4 copy-start.61
  372.4 14.4 %copy-start.51 = (f32[1024]{0:T(1024)}, f32[1024]{0:T(1024)S(1)}, u32[]{:S(2)}) copy-start(f32[1024]{0:T(1024)S(1)} %get-tuple-element.916) | copy-start | bytes 12292
  444.8 20.5 %copy-start.19 = (f32[24]{0:T(128)}, f32[24]{0:T(128)S(1)}, u32[]{:S(2)}) copy-start(f32[24]{0:T(128)S(1)} %get-tuple-element.1156) | copy-start | bytes 292 | tf_op jit(solution)/shard_map/transpose(jvp())/while
  445.6 17.1 %copy-start.13 = (pred[256,256]{1,0:T(8,128)(4,1)}, pred[256,256]{1,0:T(8,128)(4,1)S(1)}, u32[]{:S(2)}) copy-start(pred[256,256]{1,0:T(8,128)(4,1)S(1)} %fusion.262) | copy-start | bytes 196612 | tf_op jit(solution)/shard_map/transpose(jvp())/while
  450.7 12.0 copy-start.9
  450.7 12.0 copy-start
  477.8 12.1 copy-start.78
  503.3 20.5 %copy-start.19 = (f32[24]{0:T(128)}, f32[24]{0:T(128)S(1)}, u32[]{:S(2)}) copy-start(f32[24]{0:T(128)S(1)} %get-tuple-element.1156) | copy-start | bytes 292 | tf_op jit(solution)/shard_map/transpose(jvp())/while
  504.1 17.1 %copy-start.13 = (pred[256,256]{1,0:T(8,128)(4,1)}, pred[256,256]{1,0:T(8,128)(4,1)S(1)}, u32[]{:S(2)}) copy-start(pred[256,256]{1,0:T(8,128)(4,1)S(1)} %fusion.262) | copy-start | bytes 196612 | tf_op jit(solution)/shard_map/transpose(jvp())/while
  509.2 12.0 copy-start.9
  509.2 12.0 copy-start
  536.3 12.1 copy-start.78
  561.8 20.5 %copy-start.19 = (f32[24]{0:T(128)}, f32[24]{0:T(128)S(1)}, u32[]{:S(2)}) copy-start(f32[24]{0:T(128)S(1)} %get-tuple-element.1156) | copy-start | bytes 292 | tf_op jit(solution)/shard_map/transpose(jvp())/while
  562.6 17.1 %copy-start.13 = (pred[256,256]{1,0:T(8,128)(4,1)}, pred[256,256]{1,0:T(8,128)(4,1)S(1)}, u32[]{:S(2)}) copy-start(pred[256,256]{1,0:T(8,128)(4,1)S(1)} %fusion.262) | copy-start | bytes 196612 | tf_op jit(solution)/shard_map/transpose(jvp())/while
  567.7 12.0 copy-start.9
  567.7 12.0 copy-start
  594.7 12.1 copy-start.78
  620.3 20.5 %copy-start.19 = (f32[24]{0:T(128)}, f32[24]{0:T(128)S(1)}, u32[]{:S(2)}) copy-start(f32[24]{0:T(128)S(1)} %get-tuple-element.1156) | copy-start | bytes 292 | tf_op jit(solution)/shard_map/transpose(jvp())/while
  621.0 17.1 %copy-start.13 = (pred[256,256]{1,0:T(8,128)(4,1)}, pred[256,256]{1,0:T(8,128)(4,1)S(1)}, u32[]{:S(2)}) copy-start(pred[256,256]{1,0:T(8,128)(4,1)S(1)} %fusion.262) | copy-start | bytes 196612 | tf_op jit(solution)/shard_map/transpose(jvp())/while
  626.1 12.0 copy-start.9
  626.1 12.0 copy-start
  653.2 12.1 copy-start.78
  670.9 122.0 %reduce-scatter.11.cloned.1.call-start = ((), (), s32[]{:S(2)}) async-start(), calls=%async_computation.9 | async-start | bytes 9437184 | tf_op jit(solution)/shard_map/reduce_scatter | solution.py:248
  692.4 13.8 %copy-start.25 = (f32[1024]{0:T(1024)S(1)}, f32[1024]{0:T(1024)}, u32[]{:S(2)}) copy-start(f32[1024]{0:T(1024)} %copy-done.24) | copy-start | bytes 12292
  692.4 13.8 %copy-start.27 = (f32[1024]{0:T(1024)S(1)}, f32[1024]{0:T(1024)}, u32[]{:S(2)}) copy-start(f32[1024]{0:T(1024)} %copy-done.26) | copy-start | bytes 12292
  766.0 86.6 %reduce-scatter.9.cloned.1.call-start = ((), (), s32[]{:S(2)}) async-start(), calls=%async_computation.7 | async-start | bytes 9437184 | tf_op jit(solution)/shard_map/reduce_scatter | solution.py:180
  777.4 149.3 %all-reduce.33.cloned.1.call-start = ((), (), s32[]{:S(2)}) async-start(), calls=%async_computation.11 | async-start | bytes 172032 | tf_op jit(solution)/shard_map/psum | solution.py:276
  799.4 280.6 %reduce-scatter.15.cloned.1.call-start = ((), (), s32[]{:S(2)}) async-start(), calls=%async_computation.13 | async-start | bytes 6266880
  810.7 445.3 %reduce-scatter.13.cloned.1.call-start = ((), (), s32[]{:S(2)}) async-start(), calls=%async_computation.12 | async-start | bytes 10027008
  (79 other events, 453.3 us)
Sparse Core Ops, SparseCore 0:
  13.0 14.8 all-gather.4
  31.3 133.8 all-gather.6
  166.7 10.2 all-gather.10
  179.7 80.8 all-gather.8
  671.0 18.0 all-reduce.30
  766.1 12.4 reduce-scatter.10
  780.9 16.0 reduce-scatter.8
  803.2 123.5 all-reduce.32
  932.1 147.8 reduce-scatter.14
  1085.5 170.4 reduce-scatter.12

commit v2 on v1

v2 whole, which is shorter than its diff:
```python
from functools import partial

import jax
import jax.numpy as jnp
from jax import lax
from jax.experimental import pallas as pl
from jax.experimental.pallas import tpu as pltpu
from jax.sharding import PartitionSpec as P

EPSILON = 1e-05
HIGHEST = lax.Precision.HIGHEST
CHUNK = 128
HEADS_STEP = 8
F32 = jnp.float32
BF16 = jnp.bfloat16


def shift_down(values, steps_back, filler):
    leading = jnp.full((steps_back,) + values.shape[1:], filler, values.dtype)
    return jnp.concatenate([leading, values[: values.shape[0] - steps_back]], axis=0)


def causal_conv(values, conv_taps, conv_bias, segment):
    taps_count = conv_taps.shape[0]
    result = conv_bias[None, :] + conv_taps[taps_count - 1][None, :] * values
    for steps_back in range(1, taps_count):
        earlier = shift_down(values, steps_back, 0.0)
        same_seq = (shift_down(segment, steps_back, -2) == segment).astype(values.dtype)
        result = (
            result + conv_taps[taps_count - 1 - steps_back][None, :] * earlier * same_seq[:, None]
        )
    return result


def dot(a, b):
    return jnp.dot(a, b, preferred_element_type=F32)


def dot_nt(a, b):
    return lax.dot_general(a, b, (((1,), (1,)), ((), ())), preferred_element_type=F32)


def spread_heads(columns, pair, head_size):
    lane = lax.broadcasted_iota(jnp.int32, (columns.shape[0], 2 * head_size), 1)
    first = columns[:, 2 * pair : 2 * pair + 1]
    second = columns[:, 2 * pair + 1 : 2 * pair + 2]
    return jnp.where(lane < head_size, first, second)


def conv_pair(xr, taps, bias, masks, rows, before, lanes):
    current = xr[rows, lanes]
    joined = jnp.concatenate([xr[before, lanes], current], axis=0)
    count = taps.shape[0]
    value = bias[0:1, lanes] + taps[count - 1 : count, lanes] * current
    shifted = []
    for back in range(1, count):
        piece = pltpu.roll(joined, back, 0)[8:] * masks[back - 1, rows, :]
        shifted.append(piece)
        value = value + taps[count - 1 - back : count - back, lanes] * piece
    return current, shifted, value


def ssd_forward_kernel(
    xr, taps, bias, skip, masks, score, cs, bst, dt, cumc, reach, toend, cumr, kept,
    y_out, states_out, state,
):
    width = xr.shape[1]
    head_size = width // dt.shape[2]
    pair_width = 2 * head_size
    chunks = xr.shape[0] // CHUNK
    state[...] = jnp.zeros_like(state)

    def chunk_body(place, unused):
        start = pl.multiple_of(place * CHUNK, CHUNK)
        rows = pl.ds(start, CHUNK)
        before = pl.ds(pl.multiple_of(jnp.maximum(start - 8, 0), 8), 8)
        dt_cols, cum_cols = dt[0, rows, :], cumc[0, rows, :]
        reach_cols, end_cols = reach[0, rows, :], toend[0, rows, :]
        score_now, cs_now, bst_now = score[rows, :], cs[rows, :], bst[:, rows]
        lane = lax.broadcasted_iota(jnp.int32, (CHUNK, pair_width), 1)
        row_of = pl.ds(pl.multiple_of(place * 8, 8), 8)
        for pair in range(width // pair_width):
            lanes = slice(pair * pair_width, (pair + 1) * pair_width)
            unused_cur, unused_shift, value = conv_pair(
                xr, taps, bias, masks, rows, before, lanes
            )
            x = value * jax.nn.sigmoid(value)
            xdt = x * spread_heads(dt_cols, pair, head_size)
            xb = xdt.astype(BF16)
            held = state[:, lanes]
            held_low = held.astype(BF16)
            states_out[rows, lanes] = held_low
            halves = []
            for head in (2 * pair, 2 * pair + 1):
                spread = cum_cols[:, head : head + 1] - cumr[0, head : head + 1, rows]
                mixing = score_now * jnp.exp(jnp.minimum(spread, 0.0))
                halves.append(dot(mixing.astype(BF16), xb))
            y = jnp.where(lane < head_size, halves[0], halves[1])
            y = y + spread_heads(reach_cols, pair, head_size) * dot(cs_now, held_low)
            y_out[rows, lanes] = y + skip[0:1, lanes] * x
            fresh = dot(bst_now, (xdt * spread_heads(end_cols, pair, head_size)).astype(BF16))
            state[:, lanes] = fresh + kept[0, row_of, lanes][0:1] * held
        return unused

    lax.fori_loop(0, chunks, chunk_body, 0)


def ssd_backward_kernel(
    xr, taps, bias, skip, masks, score_t, cs, bs, cst, pick, dt, cumc, reach, toend, cumr, kept,
    states, dy,
    dxr_out, dscore_out, dbs_out, dcs_out, cols_out, rows_out, span_out, sums_out,
    dstate, dvalue_next,
):
    width = xr.shape[1]
    head_size = width // dt.shape[2]
    pair_width = 2 * head_size
    length = xr.shape[0]
    chunks = length // CHUNK
    count = taps.shape[0]
    dstate[...] = jnp.zeros_like(dstate)
    dvalue_next[...] = jnp.zeros_like(dvalue_next)
    sums_out[...] = jnp.zeros_like(sums_out)

    @pl.when(pl.program_id(0) == 0)
    def clear():
        dscore_out[...] = jnp.zeros_like(dscore_out)
        dbs_out[...] = jnp.zeros_like(dbs_out)
        dcs_out[...] = jnp.zeros_like(dcs_out)

    def chunk_body(step, unused):
        place = chunks - 1 - step
        start = pl.multiple_of(place * CHUNK, CHUNK)
        rows = pl.ds(start, CHUNK)
        before = pl.ds(pl.multiple_of(jnp.maximum(start - 8, 0), 8), 8)
        after = pl.ds(pl.multiple_of(jnp.minimum(start + CHUNK, length - 8), 8), 8)
        dt_cols, cum_cols = dt[0, rows, :], cumc[0, rows, :]
        reach_cols, end_cols = reach[0, rows, :], toend[0, rows, :]
        score_now, cs_now, bs_now, cst_now = score_t[rows, :], cs[rows, :], bs[rows, :], cst[:, rows]
        lane = lax.broadcasted_iota(jnp.int32, (CHUNK, pair_width), 1)
        row_of = pl.ds(pl.multiple_of(place * 8, 8), 8)
        dscore = jnp.zeros((CHUNK, CHUNK), F32)
        dbs = jnp.zeros((CHUNK, bs_now.shape[1]), F32)
        dcs = jnp.zeros((CHUNK, bs_now.shape[1]), F32)
        columns = jnp.zeros((CHUNK, cols_out.shape[2]), F32)
        column_lane = lax.broadcasted_iota(jnp.int32, columns.shape, 1)
        for pair in range(width // pair_width):
            lanes = slice(pair * pair_width, (pair + 1) * pair_width)
            current, shifted, value = conv_pair(xr, taps, bias, masks, rows, before, lanes)
            gate = jax.nn.sigmoid(value)
            x = value * gate
            dt_now = spread_heads(dt_cols, pair, head_size)
            end_now = spread_heads(end_cols, pair, head_size)
            xdt = x * dt_now
            xb = xdt.astype(BF16)
            dy_now = dy[rows, lanes]
            dyb = dy_now.astype(BF16)
            held_low = states[rows, lanes]
            dheld = dstate[:, lanes]
            dheld_low = dheld.astype(BF16)
            dyr = dy_now * spread_heads(reach_cols, pair, head_size)
            dyr_low = dyr.astype(BF16)
            from_state = dyr * dot(cs_now, held_low)
            dcs = dcs + dot_nt(dyr_low, held_low)
            dxdt_end = end_now * dot(bs_now, dheld_low)
            dbs = dbs + dot_nt((xdt * end_now).astype(BF16), dheld_low)
            halves = []
            for side in (0, 1):
                head = 2 * pair + side
                spread = cumr[0, head : head + 1, rows] - cum_cols[:, head : head + 1]
                decay = jnp.exp(jnp.minimum(spread, 0.0))
                weight = score_now * decay
                own = (lane < head_size) if side == 0 else (lane >= head_size)
                pairs = dot_nt(jnp.where(own, xdt, 0.0).astype(BF16), dyb)
                dscore = dscore + pairs * decay
                share = pairs * weight
                columns = columns - jnp.where(
                    column_lane == head, jnp.sum(share, axis=1, keepdims=True), 0.0
                )
                rows_out[0, head : head + 1, rows] = jnp.sum(share, axis=0, keepdims=True)
                halves.append(dot(weight.astype(BF16), dyb))
            dxdt = jnp.where(lane < head_size, halves[0], halves[1]) + dxdt_end
            picked = jnp.concatenate(
                [
                    from_state.astype(BF16),
                    (xdt * dxdt_end).astype(BF16),
                    (x * dxdt).astype(BF16),
                ],
                axis=1,
            )
            columns = columns + dot(picked, pick[pair])
            dx = skip[0:1, lanes] * dy_now + dt_now * dxdt
            kept_row = kept[0, row_of, lanes][0:1]
            span_row = kept_row * jnp.sum(dheld * held_low.astype(F32), axis=0, keepdims=True)
            span_out[0, row_of, lanes] = jnp.broadcast_to(span_row, (8, pair_width))
            dstate[:, lanes] = kept_row * dheld + dot(cst_now, dyr_low)
            dvalue = dx * (gate * (1.0 + value * (1.0 - gate)))
            dxr = taps[count - 1 : count, lanes] * dvalue
            next_rows = dvalue_next[:, lanes]
            sums = [jnp.sum(dvalue * current, axis=0, keepdims=True)]
            for back in range(1, count):
                masked = dvalue * masks[back - 1, rows, :]
                joined = jnp.concatenate(
                    [masked, next_rows * masks[back - 1, after, :]], axis=0
                )
                lifted = pltpu.roll(joined, CHUNK + 8 - back, 0)[:CHUNK]
                dxr = dxr + taps[count - 1 - back : count - back, lanes] * lifted
                sums.append(jnp.sum(dvalue * shifted[back - 1], axis=0, keepdims=True))
            dvalue_next[:, lanes] = dvalue[:8]
            sums.append(jnp.sum(dvalue, axis=0, keepdims=True))
            sums.append(jnp.sum(dy_now * x, axis=0, keepdims=True))
            for slot, row in enumerate(sums):
                sums_out[slot : slot + 1, lanes] += row
            dxr_out[rows, lanes] = dxr.astype(dxr_out.dtype)
        dscore_out[rows, :] += dscore
        dbs_out[rows, :] += dbs
        dcs_out[rows, :] += dcs
        cols_out[0, rows, :] = columns
        return unused

    lax.fori_loop(0, chunks, chunk_body, 0)


def chunk_terms(step_size, log_decay, segment, head_size):
    length, heads = step_size.shape
    chunks, groups = length // CHUNK, heads // HEADS_STEP
    parted = segment.reshape(chunks, CHUNK)
    places = jnp.arange(CHUNK)
    lower = (places[:, None] >= places[None, :]).astype(F32)
    allowed = (
        (parted[:, :, None] == parted[:, None, :]) & (places[:, None] >= places[None, :])[None]
    ).astype(F32)
    cumulative = jnp.einsum(
        "ts,csh->cth", lower, log_decay.reshape(chunks, CHUNK, heads), precision=HIGHEST
    )
    last = jnp.concatenate([jnp.full((1,), -2, segment.dtype), parted[:-1, CHUNK - 1]])
    carried = (parted == last[:, None]).astype(F32)
    final = parted[:, CHUNK - 1]
    at_end = (parted == final[:, None]).astype(F32)
    total = cumulative[:, CHUNK - 1]
    reach = jnp.exp(cumulative) * carried[:, :, None]
    to_end = jnp.exp(total[:, None, :] - cumulative) * at_end[:, :, None]
    kept = jnp.exp(total) * (final == last).astype(F32)[:, None]

    def by_group(array):
        return array.reshape(length, groups, HEADS_STEP).transpose(1, 0, 2)

    columns = tuple(by_group(a.reshape(length, heads)) for a in (step_size, cumulative, reach, to_end))
    cum_rows = cumulative.reshape(length, heads).T.reshape(groups, HEADS_STEP, length)
    kept_rows = jnp.repeat(kept, head_size, axis=1).reshape(chunks, groups, -1).transpose(1, 0, 2)
    kept_rows = jnp.repeat(kept_rows, 8, axis=1)
    masks = jnp.stack(
        [
            jnp.broadcast_to(
                (shift_down(segment, back, -2) == segment).astype(F32)[:, None],
                (length, 2 * head_size),
            )
            for back in (1, 2, 3)
        ]
    )
    return allowed, columns, cum_rows, kept_rows, masks


def whole_spec(array):
    zeros = (0,) * array.ndim
    return pl.BlockSpec(array.shape, lambda g: zeros)


def group_spec(array):
    rest = (0,) * (array.ndim - 1)
    return pl.BlockSpec((1,) + array.shape[1:], lambda g: (g,) + rest)


def lanes_spec(array, width):
    return pl.BlockSpec((array.shape[0], width), lambda g: (0, g))


def ssd_forward(xr, taps, bias, skip_row, terms, bs_low, cs_low):
    allowed, columns, cum_rows, kept_rows, masks = terms
    length, inner = xr.shape
    groups = cum_rows.shape[0]
    width = inner // groups
    state_dim = bs_low.shape[1]
    chunks = length // CHUNK
    score = (
        jnp.einsum(
            "ctn,csn->cts",
            cs_low.reshape(chunks, CHUNK, state_dim),
            bs_low.reshape(chunks, CHUNK, state_dim),
            preferred_element_type=F32,
        )
        * allowed
    )
    shared = (masks, score.reshape(length, CHUNK), cs_low, bs_low.T)
    grouped = (*columns, cum_rows, kept_rows)
    y, states = pl.pallas_call(
        ssd_forward_kernel,
        grid=(groups,),
        in_specs=[lanes_spec(a, width) for a in (xr, taps, bias, skip_row)]
        + [whole_spec(a) for a in shared]
        + [group_spec(a) for a in grouped],
        out_specs=[
            pl.BlockSpec((length, width), lambda g: (0, g)),
            pl.BlockSpec((chunks * state_dim, width), lambda g: (0, g)),
        ],
        out_shape=[
            jax.ShapeDtypeStruct((length, inner), F32),
            jax.ShapeDtypeStruct((chunks * state_dim, inner), BF16),
        ],
        scratch_shapes=[pltpu.VMEM((state_dim, width), F32)],
        cost_estimate=pl.CostEstimate(
            flops=8 * length * inner * CHUNK, bytes_accessed=12 * length * inner, transcendentals=0
        ),
        name="ssd_forward",
    )(xr, taps, bias, skip_row, *shared, *grouped)
    return y, states, score


def ssd_backward(xr, taps, bias, skip_row, terms, score, bs_low, cs_low, states, dy):
    allowed, columns, cum_rows, kept_rows, masks = terms
    length, inner = xr.shape
    groups, heads_step = cum_rows.shape[:2]
    width = inner // groups
    head_size = width // heads_step
    state_dim = bs_low.shape[1]
    chunks = length // CHUNK
    lane = jnp.arange(2 * head_size) // head_size
    pick = jnp.stack(
        [
            jnp.concatenate(
                [
                    (
                        (2 * pair + lane + slot * heads_step)[:, None] == jnp.arange(CHUNK)[None, :]
                    ).astype(BF16)
                    for slot in range(3)
                ]
            )
            for pair in range(heads_step // 2)
        ]
    )
    score_t = score.transpose(0, 2, 1).reshape(length, CHUNK)
    shared = (masks, score_t, cs_low, bs_low, cs_low.T, pick)
    grouped = (*columns, cum_rows, kept_rows)
    fixed = pl.BlockSpec((length, CHUNK), lambda g: (0, 0))
    out = pl.pallas_call(
        ssd_backward_kernel,
        grid=(groups,),
        in_specs=[lanes_spec(a, width) for a in (xr, taps, bias, skip_row)]
        + [whole_spec(a) for a in shared]
        + [group_spec(a) for a in grouped]
        + [lanes_spec(a, width) for a in (states, dy)],
        out_specs=[
            pl.BlockSpec((length, width), lambda g: (0, g)),
            fixed,
            pl.BlockSpec((length, state_dim), lambda g: (0, 0)),
            pl.BlockSpec((length, state_dim), lambda g: (0, 0)),
            pl.BlockSpec((1, length, CHUNK), lambda g: (g, 0, 0)),
            pl.BlockSpec((1, heads_step, length), lambda g: (g, 0, 0)),
            pl.BlockSpec((1, 8 * chunks, width), lambda g: (g, 0, 0)),
            pl.BlockSpec((8, width), lambda g: (0, g)),
        ],
        out_shape=[
            jax.ShapeDtypeStruct((length, inner), BF16),
            jax.ShapeDtypeStruct((length, CHUNK), F32),
            jax.ShapeDtypeStruct((length, state_dim), F32),
            jax.ShapeDtypeStruct((length, state_dim), F32),
            jax.ShapeDtypeStruct((groups, length, CHUNK), F32),
            jax.ShapeDtypeStruct((groups, heads_step, length), F32),
            jax.ShapeDtypeStruct((groups, 8 * chunks, width), F32),
            jax.ShapeDtypeStruct((8, inner), F32),
        ],
        scratch_shapes=[pltpu.VMEM((state_dim, width), F32), pltpu.VMEM((8, width), F32)],
        cost_estimate=pl.CostEstimate(
            flops=24 * length * inner * CHUNK, bytes_accessed=16 * length * inner, transcendentals=0
        ),
        name="ssd_backward",
    )(xr, taps, bias, skip_row, *shared, *grouped, states, dy)
    dxr, dscore_t, dbs, dcs, cols, rows, span, sums = out
    dscore_t = (dscore_t.reshape(chunks, CHUNK, CHUNK) * allowed.transpose(0, 2, 1)).astype(BF16)
    parted_c = cs_low.reshape(chunks, CHUNK, state_dim)
    parted_b = bs_low.reshape(chunks, CHUNK, state_dim)
    dbs = dbs + jnp.einsum(
        "cst,ctn->csn", dscore_t, parted_c, preferred_element_type=F32
    ).reshape(length, state_dim)
    dcs = dcs + jnp.einsum(
        "cst,csn->ctn", dscore_t, parted_b, preferred_element_type=F32
    ).reshape(length, state_dim)
    heads = groups * heads_step

    def from_columns(slot):
        part = cols[:, :, slot * heads_step : (slot + 1) * heads_step]
        return part.transpose(1, 0, 2).reshape(length, heads)

    upward = from_columns(0) + rows.reshape(heads, length).T
    onward = from_columns(1)
    dstep = from_columns(2)
    spans = jnp.sum(span[:, ::8].reshape(groups, chunks, heads_step, head_size), axis=3)
    spans = spans.transpose(1, 0, 2).reshape(chunks, 1, heads)
    places = jnp.arange(CHUNK)
    at_or_after = (places[None, :] >= places[:, None]).astype(F32)
    ahead = (places[None, :] < places[:, None]).astype(F32)
    dlog = (
        jnp.einsum(
            "rt,cth->crh", at_or_after, upward.reshape(chunks, CHUNK, heads), precision=HIGHEST
        )
        + jnp.einsum("rs,csh->crh", ahead, onward.reshape(chunks, CHUNK, heads), precision=HIGHEST)
        + spans
    ).reshape(length, heads)
    return dxr, dbs, dcs, dstep, dlog, sums


def swap_pair(values):
    return lax.ppermute(values, "tensor", [(0, 1), (1, 0)])


def gather_pair(own, place):
    joined = jnp.concatenate([own, swap_pair(own), own], axis=0)
    return lax.dynamic_slice_in_dim(joined, place * own.shape[0], 2 * own.shape[0])


def scatter_pair(values, place):
    half = values.shape[0] // 2
    sent = lax.dynamic_slice_in_dim(values, (1 - place) * half, half)
    kept = lax.dynamic_slice_in_dim(values, place * half, half)
    return kept + swap_pair(sent)


def stage_orders(size):
    bits = size.bit_length() - 1
    if bits == 4:
        return ((0, 1, 2, 3), (1, 2, 3, 0), (2, 0, 1, 3))
    return tuple(tuple((bit + turn) % bits for bit in range(bits)) for turn in range(3))


def partner(values, bit):
    size = lax.axis_size("dp")
    return lax.ppermute(values, "dp", [(i, i ^ (1 << bit)) for i in range(size)])


def place_kernel(table, *refs):
    out = refs[-1]
    start = 0
    for ref in refs[:-1]:
        width = ref.shape[2]
        out[:, start : start + width] = ref[0]
        start += width


def gather_rows(shard):
    size, index = lax.axis_size("dp"), lax.axis_index("dp")
    orders = stage_orders(size)
    rows, width = shard.shape[0], shard.shape[1] // len(orders)
    targets = jnp.arange(size, dtype=jnp.int32) ^ index.astype(jnp.int32)
    pieces = [shard[None, :, turn * width : (turn + 1) * width] for turn in range(len(orders))]
    tables = []
    for order in orders:
        stages = order[::-1]
        tables.append(sum(((targets >> bit) & 1) << stage for stage, bit in enumerate(stages)))
    for stage in range(size.bit_length() - 1):
        pieces = [
            jnp.concatenate([piece, partner(piece, order[::-1][stage])], axis=0)
            for piece, order in zip(pieces, orders)
        ]

    def piece_spec(turn):
        return pl.BlockSpec((1, rows, width), lambda d, table: (table[turn, d], 0, 0))

    return pl.pallas_call(
        place_kernel,
        grid_spec=pltpu.PrefetchScalarGridSpec(
            num_scalar_prefetch=1,
            grid=(size,),
            in_specs=[piece_spec(turn) for turn in range(len(orders))],
            out_specs=pl.BlockSpec((rows, shard.shape[1]), lambda d, table: (d, 0)),
        ),
        out_shape=jax.ShapeDtypeStruct((size * rows, shard.shape[1]), shard.dtype),
        cost_estimate=pl.CostEstimate(
            flops=0, bytes_accessed=4 * size * shard.size, transcendentals=0
        ),
        name="place_rows",
    )(jnp.stack(tables), *pieces)


def scatter_rows(values):
    size, index = lax.axis_size("dp"), lax.axis_index("dp")
    bits = size.bit_length() - 1
    orders = stage_orders(size)
    width = values.shape[1] // len(orders)
    rows = values.shape[0] // size
    held, left = [], []
    for turn in range(len(orders)):
        piece = values[:, turn * width : (turn + 1) * width]
        held.append(piece.reshape((2,) * bits + (rows, width)))
        left.append(list(range(bits - 1, -1, -1)))
    for stage in range(bits):
        for turn, order in enumerate(orders):
            bit = order[stage]
            axis = left[turn].index(bit)
            mine = (index >> bit) & 1
            sent = lax.dynamic_index_in_dim(held[turn], 1 - mine, axis, keepdims=False)
            kept = lax.dynamic_index_in_dim(held[turn], mine, axis, keepdims=False)
            got = partner(sent.astype(BF16), bit)
            held[turn] = kept.astype(F32) + got.astype(F32)
            left[turn].pop(axis)
    return jnp.concatenate(held, axis=1)


def sum_small(values):
    for bit in range(lax.axis_size("dp").bit_length() - 1):
        values = values + partner(values, bit)
    return values


def shards(
    tokens,
    segment_ids,
    norm_gain,
    in_gate_inner,
    in_state,
    in_step,
    conv_inner,
    conv_inner_bias,
    conv_state,
    conv_state_bias,
    step_bias,
    decay_log,
    skip_gain,
    gate_gain,
    out_proj,
    cotangent,
):
    half_rows = tokens.shape[0]
    model_width = tokens.shape[1]
    tensor_place = lax.axis_index("tensor")
    own_segment = lax.dynamic_slice_in_dim(segment_ids, tensor_place * half_rows, half_rows)
    own_live = (own_segment >= 0).astype(F32)[:, None]
    own_rows = tokens.astype(F32)
    row_scale = lax.rsqrt(jnp.mean(own_rows * own_rows, axis=1, keepdims=True) + EPSILON)
    normed_own = (own_rows * row_scale * norm_gain[None, :]).astype(BF16)
    width, _, inner_dev = in_gate_inner.shape
    state_dim = in_state.shape[2]
    heads_dev = in_step.shape[1]
    head_size = inner_dev // heads_dev
    step_pad = -heads_dev % 128
    first_shard = jnp.concatenate(
        [
            in_gate_inner[:, 1],
            in_state.reshape(width, -1),
            in_step,
            jnp.zeros((width, step_pad), BF16),
        ],
        axis=1,
    )
    first_weights = gather_rows(first_shard)
    later_shard = jnp.concatenate([in_gate_inner[:, 0], out_proj.T], axis=1)
    later_weights = gather_rows(later_shard)
    normed = gather_pair(normed_own, tensor_place)
    first_proj = dot(normed, first_weights)
    state_end = inner_dev + 2 * state_dim
    inner_proj = first_proj[:, :inner_dev]
    state_proj = first_proj[:, inner_dev:state_end]
    step_proj = first_proj[:, state_end : state_end + heads_dev]

    def state_piece(state_values, conv_taps, conv_bias):
        return jax.nn.silu(
            causal_conv(
                state_values,
                conv_taps.reshape(conv_taps.shape[0], -1),
                conv_bias.reshape(-1),
                segment_ids,
            )
        )

    state_act, state_back = jax.vjp(state_piece, state_proj, conv_state, conv_state_bias)
    bs_low = state_act[:, :state_dim].astype(BF16)
    cs_low = state_act[:, state_dim:].astype(BF16)
    step_size = jax.nn.softplus(step_proj + step_bias[None, :])
    decay_rate = -jnp.exp(decay_log)
    log_decay = step_size * decay_rate[None, :]
    terms = chunk_terms(step_size, log_decay, segment_ids, head_size)
    skip_row = jnp.repeat(skip_gain, head_size)[None]
    bias_row = conv_inner_bias[None]
    mixed, states, score = ssd_forward(
        inner_proj, conv_inner, bias_row, skip_row, terms, bs_low, cs_low
    )
    gate_weights = later_weights[:, :inner_dev]
    out_weights_t = later_weights[:, inner_dev:]
    gate_proj = dot(normed, gate_weights)
    gate_sigmoid = jax.nn.sigmoid(gate_proj)
    gated_values = mixed * (gate_proj * gate_sigmoid)
    full_inner = inner_dev * lax.axis_size("tensor")
    squares = lax.psum(jnp.sum(gated_values * gated_values, axis=1), "tensor")
    gate_scale = lax.rsqrt(squares / full_inner + EPSILON)[:, None]
    normed_inner = (gated_values * gate_scale * gate_gain[None, :]).astype(BF16)
    partial_out = jnp.einsum(
        "tc,dc->td", normed_inner, out_weights_t, preferred_element_type=F32
    )
    branch_own = scatter_pair(partial_out, tensor_place)
    block_out = (own_rows + own_live * branch_own).astype(BF16)
    cot_rows = cotangent.astype(F32)
    branch_grad_own = (own_live * cot_rows).astype(BF16)
    branch_grad = gather_pair(branch_grad_own, tensor_place)
    grad_out_proj_t = jnp.einsum(
        "td,tc->dc", branch_grad, normed_inner, preferred_element_type=F32
    )
    grad_normed_inner = jnp.einsum(
        "td,dc->tc", branch_grad, out_weights_t, preferred_element_type=F32
    )
    grad_gate_gain = jnp.sum(grad_normed_inner * gated_values * gate_scale, axis=0)
    scaled_grad = grad_normed_inner * gate_gain[None, :]
    products = lax.psum(jnp.sum(scaled_grad * gated_values, axis=1), "tensor")
    grad_gated = (
        gate_scale * scaled_grad - gated_values * gate_scale**3 * (products / full_inner)[:, None]
    )
    low_gate = (
        grad_gated * mixed * (gate_sigmoid * (1.0 + gate_proj * (1.0 - gate_sigmoid)))
    ).astype(BF16)
    grad_mixed = grad_gated * (gate_proj * gate_sigmoid)
    grad_gate_half = jnp.einsum(
        "td,tc->dc", normed, low_gate, preferred_element_type=F32
    ).astype(BF16)
    grad_out_low = grad_out_proj_t.astype(BF16)
    grad_mixed, grad_gate_half, grad_out_low = lax.optimization_barrier(
        (grad_mixed, grad_gate_half, grad_out_low)
    )
    gate_part = scatter_rows(grad_gate_half)
    out_part = scatter_rows(grad_out_low)
    low_inner, grad_bs, grad_cs, grad_step_size, grad_log, inner_sums = ssd_backward(
        inner_proj, conv_inner, bias_row, skip_row, terms, score, bs_low, cs_low, states, grad_mixed
    )
    taps_count = conv_inner.shape[0]
    grad_conv_inner = inner_sums[:taps_count][::-1]
    grad_conv_inner_bias = inner_sums[taps_count]
    grad_skip_gain = jnp.sum(inner_sums[taps_count + 1].reshape(heads_dev, head_size), axis=1)
    grad_decay_log = jnp.sum(grad_log * log_decay, axis=0)
    grad_step_proj = (grad_step_size + grad_log * decay_rate[None, :]) * jax.nn.sigmoid(
        step_proj + step_bias[None, :]
    )
    grad_step_bias = jnp.sum(grad_step_proj, axis=0)
    grad_state_part = jnp.concatenate([grad_bs, grad_cs], axis=1)
    grad_state_act = grad_state_part + swap_pair(grad_state_part)
    grad_state_proj, grad_conv_state, grad_conv_state_bias = state_back(grad_state_act)
    low_state = grad_state_proj.astype(BF16)
    low_step = grad_step_proj.astype(BF16)
    own_state = low_state * (tensor_place == 0).astype(BF16)
    low_pad = jnp.zeros((low_step.shape[0], step_pad), BF16)
    low_first = jnp.concatenate([low_inner, low_state, low_step, low_pad], axis=1)
    grad_first = jnp.einsum(
        "td,tc->dc", normed, low_first, preferred_element_type=F32
    ).astype(BF16)
    first_part = scatter_rows(grad_first)
    grad_out_proj = out_part.T
    grad_in_gate_inner = jnp.stack([gate_part, first_part[:, :inner_dev]], axis=1)
    grad_in_state = first_part[:, inner_dev:state_end].reshape(in_state.shape)
    grad_in_step = first_part[:, state_end : state_end + heads_dev]
    low_heads = jnp.concatenate([low_inner, own_state, low_step, low_pad], axis=1)
    head_grads = dot_nt(low_gate, gate_weights) + dot_nt(low_heads, first_weights)
    normed_grad_own = scatter_pair(head_grads, tensor_place)
    grad_norm_part = jnp.sum(normed_grad_own * own_rows * row_scale, axis=0)
    scaled_rows = normed_grad_own * norm_gain[None, :]
    row_products = jnp.sum(scaled_rows * own_rows, axis=1, keepdims=True)
    grad_tokens = (
        cot_rows + row_scale * scaled_rows - own_rows * row_scale**3 * row_products / model_width
    )
    small_parts = (
        grad_norm_part + swap_pair(grad_norm_part),
        grad_conv_inner,
        grad_conv_inner_bias,
        grad_conv_state,
        grad_conv_state_bias,
        grad_step_bias,
        grad_decay_log,
        grad_skip_gain,
        grad_gate_gain,
    )
    summed = sum_small(jnp.concatenate([part.reshape(-1) for part in small_parts]))
    small, start = [], 0
    for part in small_parts:
        small.append(summed[start : start + part.size].reshape(part.shape))
        start += part.size
    return (
        block_out,
        grad_tokens,
        small[0],
        grad_in_gate_inner,
        grad_in_state,
        grad_in_step,
        *small[1:],
        grad_out_proj,
    )


def solution(mesh):
    in_specs = (
        P(("dp", "tensor"), None),
        P("dp"),
        P(),
        P("dp", None, "tensor"),
        P("dp", None, None),
        P("dp", "tensor"),
        P(None, "tensor"),
        P("tensor"),
        P(),
        P(),
        P("tensor"),
        P("tensor"),
        P("tensor"),
        P("tensor"),
        P("tensor", "dp"),
        P(("dp", "tensor"), None),
    )
    out_specs = (
        P(("dp", "tensor"), None),
        P(("dp", "tensor"), None),
        P(),
        P("dp", None, "tensor"),
        P("dp", None, None),
        P("dp", "tensor"),
        P(None, "tensor"),
        P("tensor"),
        P(),
        P(),
        P("tensor"),
        P("tensor"),
        P("tensor"),
        P("tensor"),
        P("tensor", "dp"),
    )
    return jax.shard_map(shards, mesh=mesh, in_specs=in_specs, out_specs=out_specs, check_vma=False)
```

time: 1280 us -> 727 us (0.57)
  waiting for transfers between devices: 536 us -> 180 us
  matrix products: 302 us -> 87.7 us
  Pallas kernels: 0 us -> 109 us
  local copies, waits for them, and re-layouts: 209 us -> 143 us
  starting transfers between devices: 0.41 us -> 64.5 us
  other arithmetic: 187 us -> 126 us
    unnamed x12 -> x0, waiting for transfers between devices: 320 us -> none
    dot_general x56 -> x12, matrix products: 256 us -> 57.4 us  [the longest x2 21.5 us: dot(): return jnp.dot(a, b, preferred_element_type=F32)]
    ppermute x0 -> x70, waiting for transfers between devices: none -> 180 us  [the longest x64 179 us: partner(): return lax.ppermute(values, 'dp', [(i, i ^ 1 << bit) for i in range(size)])]
    all_gather x4 -> x0, waiting for transfers between devices: 148 us -> none  [the longest x1 137 us: shards(): packed_weights = lax.all_gather(packed_in, 'dp', axis=0, tiled=True)]
    pallas_call x0 -> x4, Pallas kernels: none -> 109 us  [the longest x1 58.2 us: ssd_backward(): pl.pallas_call(ssd_backward_kernel, grid=(groups,), in_specs=[lanes_spec(...]
    psum x2 -> x0, waiting for transfers between devices: 68.1 us -> none  [the longest x1 68.1 us: shards(): lax.psum(jnp.concatenate([split_rows.reshape(-1), whole_row]), ('dp', 'te...]
    ppermute x0 -> x70, starting transfers between devices: none -> 64.5 us  [the longest x64 63.3 us: partner(): return lax.ppermute(values, 'dp', [(i, i ^ 1 << bit) for i in range(size)])]
    reshape x19 -> x14, local copies, waits for them, and re-layouts: 67.9 us -> 9.62 us  [the longest x1 1.65 us: by_group(): return array.reshape(length, groups, HEADS_STEP).transpose(1, 0, 2)]
  transfers between devices with their start and end apart: 10 -> 70, of which waited for: 5 -> 35; matrix products, arithmetic and copies ran while one was open for 31% -> 37% of each run, Pallas kernels for 0% -> 5%
where the time goes in v2:
time: 727 us; the launch traced here: 717 us
  waiting for transfers between devices  180 us (25%)
  local copies, waits for them, and re-layouts  143 us (20%)
  other arithmetic  126 us (17%)
  Pallas kernels  109 us (15%)
  matrix products  87.7 us (12%)
  starting transfers between devices  64.5 us (9%)
    ppermute x64, waiting for transfers between devices, partner(): return lax.ppermute(values, 'dp', [(i, i ^ 1 << bit) for i in range(size)])  179 us
    ppermute x64, starting transfers between devices, partner(): return lax.ppermute(values, 'dp', [(i, i ^ 1 << bit) for i in range(size)])  63.3 us
    pallas_call x1, Pallas kernels, ssd_backward(): pl.pallas_call(ssd_backward_kernel, grid=(groups,), in_specs=[lanes_spec(...  58.2 us
    unnamed x246, local copies, waits for them, and re-layouts  35.1 us
    pallas_call x1, Pallas kernels, ssd_forward(): pl.pallas_call(ssd_forward_kernel, grid=(groups,), in_specs=[lanes_spec(a...  25.7 us
    pallas_call x2, Pallas kernels, gather_rows(): pl.pallas_call(place_kernel, grid_spec=pltpu.PrefetchScalarGridSpec(num_s...  25.1 us
    dot_general x2, matrix products, dot(): return jnp.dot(a, b, preferred_element_type=F32)  21.5 us
    dot_general x2, matrix products, dot_nt(): lax.dot_general(a, b, (((1,), (1,)), ((), ())), preferred_element_type=F32)  17.2 us
  transfers between devices with their start and end apart: 70, of which 35 were waited for; matrix products, arithmetic and copies ran while one was open for 37% of the time, Pallas kernels for 5%

profile of v2, /device:TPU:0, one launch (start us, length us, event | category | flops | bytes accessed | tf_op | source)
XLA Modules:
  0.0 717.2 jit_solution(7299148226537292738)
XLA Ops:
  8.0 3.6 collective-permute-start.1
  83.6 5.3 collective-permute-done.6
  93.8 4.5 collective-permute-done.14
  99.4 5.2 collective-permute-done.18
  120.1 5.0 collective-permute-done.15
  140.9 7.3 %fusion.13 = bf16[1024,1536]{1,0:T(8,128)(2,1)} fusion(s32[]{:T(128)S(6)} %select_n.186, bf16[512,1536]{1,0:T(8,128)(2,1)S(1)} %fusion.16, bf16[512,1536]{1,0:T(8,128)(2,1)} %collective-permute-done), kind=kLoop, calls=%fused_computation.38 | loop fusion | flops 9437184 | bytes 6291460 | tf_op jit(solution)/shard_map/concatenate | solution.py:416
  149.7 6.8 fusion.11
  161.7 12.1 %place_rows.2 = bf16[1536,1920]{1,0:T(8,128)(2,1)} custom-call(s32[3,16]{1,0:T(4,128)} %pad_add_fusion.table, bf16[16,96,640]{2,1,0:T(8,128)(2,1)} %copy-done.52, bf16[16,96,640]{2,1,0:T(8,128)(2,1)} %copy-done.50, bf16[16,96,640]{2,1,0:T(8,128)(2,1)} %constant_dynamic-update-slice_fusion.10.refs_2_), custom_call_target="tpu_custom_call" | custom-call | bytes 11796480 | tf_op jit(solution)/shard_map/place_rows/pallas_call | solution.py:467
  173.9 9.0 %fusion.92 = f32[1024,1920]{1,0:T(8,128)S(1)} fusion(bf16[1024,1536]{1,0:T(8,128)(2,1)S(1)} %copy-done.40, bf16[1536,1920]{1,0:T(8,128)(2,1)} %place_rows.2), kind=kOutput, calls=%fused_computation.373 | convolution fusion | flops 6039797760 | bytes 16908288 | tf_op jit(solution)/shard_map/dot_general | solution.py:36
  183.1 2.9 copy-done.1
  191.0 3.8 multiply_convert_fusion.2
  201.4 5.9 slice.242.xr
  218.3 25.7 %ssd_forward.1 = (f32[1024,1536]{1,0:T(8,128)}, bf16[1024,1536]{1,0:T(8,128)(2,1)}) custom-call(f32[1024,1536]{1,0:T(8,128)} %slice.242.xr, f32[4,1536]{1,0:T(4,128)} %taps.3, f32[1,1536]{1,0:T(1,128)} %broadcast_in_dim.28.bias, f32[1,1536]{1,0:T(1,128)} %broadcast_in_dim_reshape.2.skip, f32[3,1024,128]{2,1,0:T(8,128)} %pad_maximum_fusion.masks, ...), custom_call_target="tpu_custom_call" | custom-call | flops 1610612736 | bytes 18874368 | tf_op jit(solution)/shard_map/ssd_forward/pallas_call | solution.py:295
  252.1 13.0 %place_rows.3 = bf16[1536,3072]{1,0:T(8,128)(2,1)} custom-call(s32[3,16]{1,0:T(4,128)} %pad_add_fusion.table, bf16[16,96,1024]{2,1,0:T(8,128)(2,1)} %constant_dynamic-update-slice_fusion.15.refs_0_, bf16[16,96,1024]{2,1,0:T(8,128)(2,1)} %constant_dynamic-update-slice_fusion.20.refs_1_, bf16[16,96,1024]{2,1,0:T(8,128)(2,1)} %constant_dynamic-update-slice_fusion.25.refs_2_), custom_call_target="tpu_custom_call" | custom-call | bytes 18874368 | tf_op jit(solution)/shard_map/place_rows/pallas_call | solution.py:467
  265.1 12.6 %multiply_reduce_fusion.2 = (f32[1024]{0:T(1024)S(1)}, f32[1024,1536]{1,0:T(8,128)}, f32[1024,1536]{1,0:T(8,128)}) fusion(f32[1024,1536]{1,0:T(8,128)} %get-tuple-element.28, bf16[1024,1536]{1,0:T(8,128)(2,1)} %fusion.13, bf16[1536,3072]{1,0:T(8,128)(2,1)} %place_rows.3), kind=kOutput, calls=%fused_computation.14 | convolution fusion | flops 4842847232 | bytes 26742784 | tf_op jit(solution)/shard_map/dot_general | solution.py:36
  280.2 11.8 %multiply_reduce_fusion = (f32[1536]{0:T(1024)}, f32[1024]{0:T(1024)S(1)}, f32[1024,1536]{1,0:T(8,128)}) fusion(f32[1024,1536]{1,0:T(8,128)} %get-tuple-element.152, f32[1024]{0:T(1024)S(1)} %get-tuple-element.211, f32[1536]{0:T(1024)S(1)} %copy-done.92, bf16[1024,1536]{1,0:T(8,128)(2,1)} %fusion.11, bf16[1536,3072]{1,0:T(8,128)(2,1)} %place_rows.3), kind=kOutput, calls=%fused_computation.9 | convolution fusion | flops 4841272832 | bytes 20467712 | tf_op jit(solution)/shard_map/td,dc->tc/dot_general | solution.py:605
  292.0 7.4 %convolution_convert_fusion = bf16[1536,1536]{1,0:T(8,128)(2,1)} fusion(bf16[1024,1536]{1,0:T(8,128)(2,1)S(1)} %copy-done.43, f32[1024,1536]{1,0:T(8,128)S(1)} %copy-done.17, f32[1536]{0:T(1024)S(1)} %copy-done.92, f32[1024]{0:T(1024)S(1)} %get-tuple-element.211), kind=kOutput, calls=%fused_computation | convolution fusion | flops 4838916096 | bytes 14166016 | tf_op jit(solution)/shard_map/td,tc->dc/dot_general | solution.py:602
  301.9 13.1 %multiply_convert_fusion = (bf16[1024,1536]{1,0:T(8,128)(2,1)S(1)}, f32[1024,1536]{1,0:T(8,128)}) fusion(f32[1024,1536]{1,0:T(8,128)} %get-tuple-element.227, f32[1024,1536]{1,0:T(8,128)} %get-tuple-element.28, f32[1024]{0:T(1024)S(1)} %broadcast_multiply_fusion.5, f32[1024,1536]{1,0:T(8,128)} %get-tuple-element.152, f32[1024,1536]{1,0:T(8,128)} %get-tuple-element.228, ...), kind=kLoop, calls=%fused_computation.10 | loop fusion | flops 26738688 | bytes 34621440 | tf_op jit(solution)/shard_map/convert_element_type | solution.py:616
  315.0 6.9 convolution_convert_fusion.1
  321.8 58.2 %ssd_backward.1 = (bf16[1024,1536]{1,0:T(8,128)(2,1)}, f32[1024,128]{1,0:T(8,128)}, f32[1024,128]{1,0:T(8,128)}, f32[1024,128]{1,0:T(8,128)}, f32[3,1024,128]{2,...) custom-call(f32[1024,1536]{1,0:T(8,128)} %slice.242.xr, f32[4,1536]{1,0:T(4,128)} %taps.3, ...), custom_call_target="tpu_custom_call" | custom-call | flops 4831838208 | bytes 25165824 | tf_op jit(solution)/shard_map/ssd_backward/pallas_call | solution.py:344
  382.0 11.1 %fusion.3 = f32[1024,1536]{1,0:T(8,128)} fusion(bf16[1536,3072]{1,0:T(8,128)(2,1)} %place_rows.3, f32[1024,1536]{1,0:T(8,128)} %get-tuple-element.152, f32[1536]{0:T(1024)S(1)} %copy-done.92, f32[1024]{0:T(1024)S(1)} %get-tuple-element.211), kind=kOutput, calls=%fused_computation.26 | convolution fusion | flops 4836556800 | bytes 17311744 | tf_op jit(solution)/shard_map/tc,dc->td/dot_general | solution.py:594
  402.7 3.1 slice_bitcast_fusion
  413.8 3.8 constant_dynamic-slice_fusion.11
  429.1 3.8 fusion.86
  442.4 4.6 collective-permute-done.34
  454.4 10.8 %collective-permute-done.66 = bf16[2,2,2,96,512]{4,3,0,1,2:T(8,128)(2,1)S(1)} collective-permute-done((bf16[2,2,2,96,512]{4,3,0,1,2:T(8,128)(2,1)S(1)}, bf16[2,2,2,96,512]{4,3,0,1,2:T(8,128)(2,1)S(1)}, u32[]{:S(2)}, u32[]{:S(2)}) %collective-permute-start.66) | collective-permute-done | bytes 786464 | tf_op jit(solution)/shard_map/ppermute | solution.py:436
  483.5 5.7 concatenate.207
  489.2 10.2 %fusion.94 = f32[1024,1536]{1,0:T(8,128)S(1)} fusion(bf16[1024,1920]{1,0:T(8,128)(2,1)} %concatenate.207, bf16[1536,1920]{1,0:T(8,128)(2,1)} %place_rows.2), kind=kOutput, calls=%fused_computation.375 | convolution fusion | flops 6039797760 | bytes 16121856 | tf_op jit(solution)/shard_map/dot_general | solution.py:40
  499.5 7.0 convolution_add_fusion
  512.1 5.7 concatenate.210
  517.7 9.8 %convolution_convert_fusion.2 = bf16[1536,1920]{1,0:T(8,128)(2,1)S(1)} fusion(bf16[1024,1536]{1,0:T(8,128)(2,1)} %fusion.13, bf16[1024,1920]{1,0:T(8,128)(2,1)} %concatenate.210), kind=kOutput, calls=%fused_computation.2 | convolution fusion | flops 6042746880 | bytes 12976128 | tf_op jit(solution)/shard_map/td,tc->dc/dot_general | solution.py:647
  540.7 24.9 %collective-permute-done.44 = bf16[2,96,512]{2,1,0:T(8,128)(2,1)S(1)} collective-permute-done((bf16[2,96,512]{2,1,0:T(8,128)(2,1)S(1)}, bf16[2,96,512]{2,1,0:T(8,128)(2,1)S(1)}, u32[]{:S(2)}, u32[]{:S(2)}) %collective-permute-start.44) | collective-permute-done | bytes 196640 | tf_op jit(solution)/shard_map/ppermute | solution.py:436
  566.7 4.9 collective-permute-done.36
  572.5 9.5 %collective-permute-done.40 = bf16[2,96,512]{2,1,0:T(8,128)(2,1)S(1)} collective-permute-done((bf16[2,96,512]{2,1,0:T(8,128)(2,1)S(1)}, bf16[2,96,512]{2,1,0:T(8,128)(2,1)S(1)}, u32[]{:S(2)}, u32[]{:S(2)}) %collective-permute-start.40) | collective-permute-done | bytes 196640 | tf_op jit(solution)/shard_map/ppermute | solution.py:436
  583.6 4.7 collective-permute-done.68
  588.4 9.1 %collective-permute-done.64 = bf16[2,96,512]{2,1,0:T(8,128)(2,1)S(1)} collective-permute-done((bf16[2,96,512]{2,1,0:T(8,128)(2,1)S(1)}, bf16[2,96,512]{2,1,0:T(8,128)(2,1)S(1)}, u32[]{:S(2)}, u32[]{:S(2)}) %collective-permute-start.64) | collective-permute-done | bytes 196640 | tf_op jit(solution)/shard_map/ppermute | solution.py:436
  597.6 6.7 collective-permute-done.60
  605.9 5.4 collective-permute-done.45
  611.5 4.3 collective-permute-done.41
  615.9 6.1 collective-permute-done.37
  622.1 5.6 collective-permute-done.69
  627.8 4.5 collective-permute-done.65
  632.3 5.5 collective-permute-done.61
  642.3 19.7 %collective-permute-done.46 = bf16[2,2,2,96,640]{4,3,2,1,0:T(8,128)(2,1)S(1)} collective-permute-done((bf16[2,2,2,96,640]{4,3,2,1,0:T(8,128)(2,1)S(1)}, bf16[2,2,2,96,640]{4,3,2,1,0:T(8,128)(2,1)S(1)}, u32[]{:S(2)}, u32[]{:S(2)}) %collective-permute-start.46) | collective-permute-done | bytes 983072 | tf_op jit(solution)/shard_map/ppermute | solution.py:436
  663.9 3.4 collective-permute-done.55
  675.6 8.3 %collective-permute-done.52 = bf16[2,96,640]{2,1,0:T(8,128)(2,1)S(1)} collective-permute-done((bf16[2,96,640]{2,1,0:T(8,128)(2,1)S(1)}, bf16[2,96,640]{2,1,0:T(8,128)(2,1)S(1)}, u32[]{:S(2)}, u32[]{:S(2)}) %collective-permute-start.52) | collective-permute-done | bytes 245792 | tf_op jit(solution)/shard_map/ppermute | solution.py:436
  686.1 3.3 fusion.22
  707.9 6.0 fusion.9
  (619 shorter events, 286.8 us)
Async XLA Ops:
  5.0 134.4 %collective-permute-start = (bf16[512,1536]{1,0:T(8,128)(2,1)S(1)}, bf16[512,1536]{1,0:T(8,128)(2,1)}, u32[]{:S(2)}, u32[]{:S(2)}) collective-permute-start(bf16[512,1536]{1,0:T(8,128)(2,1)S(1)} %fusion.16), channel_id=1, source_target_pairs={{0,1},{1,0},{2,3},{3,2},{4,5},{5,4},{6,7},{7,6},{8,9},{9,8},{10,11... | collective-permute-start | bytes 4718600 | tf_op jit(solution)/shard_map/ppermute | solution.py:412
  8.0 55.0 %collective-permute-start.1 = (bf16[1,96,640]{2,1,0:T(8,128)(2,1)}, bf16[1,96,640]{2,1,0:T(8,128)(2,1)}, u32[]{:S(2)}, u32[]{:S(2)}) collective-permute-start(bf16[1,96,640]{2,1,0:T(8,128)(2,1)} %get-tuple-element.197), channel_id=1, source_target_pairs={{0,16},{2,18},{4,20},{6,22},{8,24},{10,26},{12,28},{14,30},{16,0},... | collective-permute-start | bytes 368648 | tf_op jit(solution)/shard_map/ppermute | solution.py:436
  11.6 54.5 %collective-permute-start.5 = (bf16[1,96,640]{2,1,0:T(8,128)(2,1)}, bf16[1,96,640]{2,1,0:T(8,128)(2,1)}, u32[]{:S(2)}, u32[]{:S(2)}) collective-permute-start(bf16[1,96,640]{2,1,0:T(8,128)(2,1)} %get-tuple-element.196), channel_id=1, source_target_pairs={{0,2},{2,0},{4,6},{6,4},{8,10},{10,8},{12,14},{14,12},{16,18},{18,... | collective-permute-start | bytes 368648 | tf_op jit(solution)/shard_map/ppermute | solution.py:436
  16.3 50.8 %collective-permute-start.9 = (bf16[1,96,640]{2,1,0:T(8,128)(2,1)}, bf16[1,96,640]{2,1,0:T(8,128)(2,1)}, u32[]{:S(2)}, u32[]{:S(2)}) collective-permute-start(bf16[1,96,640]{2,1,0:T(8,128)(2,1)} %slice_bitcast_fusion.5), channel_id=1, source_target_pairs={{0,16},{2,18},{4,20},{6,22},{8,24},{10,26},{12,28},{14,30},{16,0},... | collective-permute-start | bytes 368648 | tf_op jit(solution)/shard_map/ppermute | solution.py:436
  19.2 54.2 %collective-permute-start.13 = (bf16[1,96,1024]{2,1,0:T(8,128)(2,1)}, bf16[1,96,1024]{2,1,0:T(8,128)(2,1)}, u32[]{:S(2)}, u32[]{:S(2)}) collective-permute-start(bf16[1,96,1024]{2,1,0:T(8,128)(2,1)} %slice_bitcast_fusion.4), channel_id=1, source_target_pairs={{0,16},{2,18},{4,20},{6,22},{8,24},{10,26},{12,28},{14,30},{16,0},... | collective-permute-start | bytes 589832 | tf_op jit(solution)/shard_map/ppermute | solution.py:436
  63.0 14.6 %collective-permute-start.17 = (bf16[1,96,1024]{2,1,0:T(8,128)(2,1)S(1)}, bf16[1,96,1024]{2,1,0:T(8,128)(2,1)S(1)}, u32[]{:S(2)}, u32[]{:S(2)}) collective-permute-start(bf16[1,96,1024]{2,1,0:T(8,128)(2,1)S(1)} %get-tuple-element.158), channel_id=1, source_target_pairs={{0,2},{2,0},{4,6},{6,4},{8,10},{10,8},{12,14},{14,12},{16,18},{18,... | collective-permute-start | bytes 589832 | tf_op jit(solution)/shard_map/ppermute | solution.py:436
  66.1 14.7 %collective-permute-start.21 = (bf16[1,96,1024]{2,1,0:T(8,128)(2,1)S(1)}, bf16[1,96,1024]{2,1,0:T(8,128)(2,1)S(1)}, u32[]{:S(2)}, u32[]{:S(2)}) collective-permute-start(bf16[1,96,1024]{2,1,0:T(8,128)(2,1)S(1)} %slice_bitcast_fusion.3), channel_id=1, source_target_pairs={{0,16},{2,18},{4,20},{6,22},{8,24},{10,26},{12,28},{14,30},{16,0},... | collective-permute-start | bytes 589832 | tf_op jit(solution)/shard_map/ppermute | solution.py:436
  67.1 15.1 %collective-permute-start.2 = (bf16[2,96,640]{2,1,0:T(8,128)(2,1)S(1)}, bf16[2,96,640]{2,1,0:T(8,128)(2,1)S(1)}, u32[]{:S(2)}, u32[]{:S(2)}) collective-permute-start(bf16[2,96,640]{2,1,0:T(8,128)(2,1)S(1)} %pad_maximum_fusion.20), channel_id=1, source_target_pairs={{0,8},{2,10},{4,12},{6,14},{8,0},{10,2},{12,4},{14,6},{16,24},{18,... | collective-permute-start | bytes 737288 | tf_op jit(solution)/shard_map/ppermute | solution.py:436
  73.3 15.5 %collective-permute-start.6 = (bf16[2,96,640]{2,1,0:T(8,128)(2,1)S(1)}, bf16[2,96,640]{2,1,0:T(8,128)(2,1)S(1)}, u32[]{:S(2)}, u32[]{:S(2)}) collective-permute-start(bf16[2,96,640]{2,1,0:T(8,128)(2,1)S(1)} %pad_maximum_fusion.21), channel_id=1, source_target_pairs={{0,16},{2,18},{4,20},{6,22},{8,24},{10,26},{12,28},{14,30},{16,0},... | collective-permute-start | bytes 737288 | tf_op jit(solution)/shard_map/ppermute | solution.py:436
  77.6 14.0 %collective-permute-start.10 = (bf16[2,96,640]{2,1,0:T(8,128)(2,1)S(1)}, bf16[2,96,640]{2,1,0:T(8,128)(2,1)S(1)}, u32[]{:S(2)}, u32[]{:S(2)}) collective-permute-start(bf16[2,96,640]{2,1,0:T(8,128)(2,1)S(1)} %pad_maximum_fusion.22), channel_id=1, source_target_pairs={{0,4},{2,6},{4,0},{6,2},{8,12},{10,14},{12,8},{14,10},{16,20},{18,... | collective-permute-start | bytes 737288 | tf_op jit(solution)/shard_map/ppermute | solution.py:436
  80.8 17.5 %collective-permute-start.14 = (bf16[2,96,1024]{2,1,0:T(8,128)(2,1)S(1)}, bf16[2,96,1024]{2,1,0:T(8,128)(2,1)S(1)}, u32[]{:S(2)}, u32[]{:S(2)}) collective-permute-start(bf16[2,96,1024]{2,1,0:T(8,128)(2,1)S(1)} %pad_maximum_fusion.17), channel_id=1, source_target_pairs={{0,8},{2,10},{4,12},{6,14},{8,0},{10,2},{12,4},{14,6},{16,24},{18,... | collective-permute-start | bytes 1179656 | tf_op jit(solution)/shard_map/ppermute | solution.py:436
  82.2 22.5 %collective-permute-start.18 = (bf16[2,96,1024]{2,1,0:T(8,128)(2,1)S(1)}, bf16[2,96,1024]{2,1,0:T(8,128)(2,1)S(1)}, u32[]{:S(2)}, u32[]{:S(2)}) collective-permute-start(bf16[2,96,1024]{2,1,0:T(8,128)(2,1)S(1)} %pad_maximum_fusion.18), channel_id=1, source_target_pairs={{0,16},{2,18},{4,20},{6,22},{8,24},{10,26},{12,28},{14,30},{16,0},... | collective-permute-start | bytes 1179656 | tf_op jit(solution)/shard_map/ppermute | solution.py:436
  88.9 18.1 %collective-permute-start.22 = (bf16[2,96,1024]{2,1,0:T(8,128)(2,1)S(1)}, bf16[2,96,1024]{2,1,0:T(8,128)(2,1)S(1)}, u32[]{:S(2)}, u32[]{:S(2)}) collective-permute-start(bf16[2,96,1024]{2,1,0:T(8,128)(2,1)S(1)} %pad_maximum_fusion.19), channel_id=1, source_target_pairs={{0,4},{2,6},{4,0},{6,2},{8,12},{10,14},{12,8},{14,10},{16,20},{18,... | collective-permute-start | bytes 1179656 | tf_op jit(solution)/shard_map/ppermute | solution.py:436
  91.5 18.7 %collective-permute-start.3 = (bf16[4,96,640]{2,1,0:T(8,128)(2,1)S(1)}, bf16[4,96,640]{2,1,0:T(8,128)(2,1)S(1)}, u32[]{:S(2)}, u32[]{:S(2)}) collective-permute-start(bf16[4,96,640]{2,1,0:T(8,128)(2,1)S(1)} %pad_maximum_fusion.14), channel_id=1, source_target_pairs={{0,4},{2,6},{4,0},{6,2},{8,12},{10,14},{12,8},{14,10},{16,20},{18,... | collective-permute-start | bytes 1474568 | tf_op jit(solution)/shard_map/ppermute | solution.py:436
  98.3 15.5 %collective-permute-start.7 = (bf16[4,96,640]{2,1,0:T(8,128)(2,1)S(1)}, bf16[4,96,640]{2,1,0:T(8,128)(2,1)S(1)}, u32[]{:S(2)}, u32[]{:S(2)}) collective-permute-start(bf16[4,96,640]{2,1,0:T(8,128)(2,1)S(1)} %pad_maximum_fusion.15), channel_id=1, source_target_pairs={{0,8},{2,10},{4,12},{6,14},{8,0},{10,2},{12,4},{14,6},{16,24},{18,... | collective-permute-start | bytes 1474568 | tf_op jit(solution)/shard_map/ppermute | solution.py:436
  104.7 12.0 %collective-permute-start.11 = (bf16[4,96,640]{2,1,0:T(8,128)(2,1)S(1)}, bf16[4,96,640]{2,1,0:T(8,128)(2,1)S(1)}, u32[]{:S(2)}, u32[]{:S(2)}) collective-permute-start(bf16[4,96,640]{2,1,0:T(8,128)(2,1)S(1)} %pad_maximum_fusion.16), channel_id=1, source_target_pairs={{0,2},{2,0},{4,6},{6,4},{8,10},{10,8},{12,14},{14,12},{16,18},{18,... | collective-permute-start | bytes 1474568 | tf_op jit(solution)/shard_map/ppermute | solution.py:436
  107.0 18.1 %collective-permute-start.15 = (bf16[4,96,1024]{2,1,0:T(8,128)(2,1)S(1)}, bf16[4,96,1024]{2,1,0:T(8,128)(2,1)S(1)}, u32[]{:S(2)}, u32[]{:S(2)}) collective-permute-start(bf16[4,96,1024]{2,1,0:T(8,128)(2,1)S(1)} %pad_maximum_fusion.9), channel_id=1, source_target_pairs={{0,4},{2,6},{4,0},{6,2},{8,12},{10,14},{12,8},{14,10},{16,20},{18,... | collective-permute-start | bytes 2359304 | tf_op jit(solution)/shard_map/ppermute | solution.py:436
  110.2 19.1 %collective-permute-start.19 = (bf16[4,96,1024]{2,1,0:T(8,128)(2,1)S(1)}, bf16[4,96,1024]{2,1,0:T(8,128)(2,1)S(1)}, u32[]{:S(2)}, u32[]{:S(2)}) collective-permute-start(bf16[4,96,1024]{2,1,0:T(8,128)(2,1)S(1)} %pad_maximum_fusion.10), channel_id=1, source_target_pairs={{0,8},{2,10},{4,12},{6,14},{8,0},{10,2},{12,4},{14,6},{16,24},{18,... | collective-permute-start | bytes 2359304 | tf_op jit(solution)/shard_map/ppermute | solution.py:436
  113.8 34.3 %collective-permute-start.26 = (bf16[512,1536]{1,0:T(8,128)(2,1)S(1)}, bf16[512,1536]{1,0:T(8,128)(2,1)S(1)}, u32[]{:S(2)}, u32[]{:S(2)}) collective-permute-start(bf16[512,1536]{1,0:T(8,128)(2,1)S(1)} %copy-done.16), channel_id=1, source_target_pairs={{0,1},{1,0},{2,3},{3,2},{4,5},{5,4},{6,7},{7,6},{8,9},{9,8},{10,11... | collective-permute-start | bytes 4718600 | tf_op jit(solution)/shard_map/ppermute | solution.py:412
  116.7 20.4 %collective-permute-start.23 = (bf16[4,96,1024]{2,1,0:T(8,128)(2,1)S(1)}, bf16[4,96,1024]{2,1,0:T(8,128)(2,1)S(1)}, u32[]{:S(2)}, u32[]{:S(2)}) collective-permute-start(bf16[4,96,1024]{2,1,0:T(8,128)(2,1)S(1)} %pad_maximum_fusion.11), channel_id=1, source_target_pairs={{0,2},{2,0},{4,6},{6,4},{8,10},{10,8},{12,14},{14,12},{16,18},{18,... | collective-permute-start | bytes 2359304 | tf_op jit(solution)/shard_map/ppermute | solution.py:436
  125.1 33.1 %collective-permute-start.4 = (bf16[8,96,640]{2,1,0:T(8,128)(2,1)S(1)}, bf16[8,96,640]{2,1,0:T(8,128)(2,1)S(1)}, u32[]{:S(2)}, u32[]{:S(2)}) collective-permute-start(bf16[8,96,640]{2,1,0:T(8,128)(2,1)S(1)} %pad_maximum_fusion.6), channel_id=1, source_target_pairs={{0,2},{2,0},{4,6},{6,4},{8,10},{10,8},{12,14},{14,12},{16,18},{18,... | collective-permute-start | bytes 2949128 | tf_op jit(solution)/shard_map/ppermute | solution.py:436
  129.3 29.4 %collective-permute-start.8 = (bf16[8,96,640]{2,1,0:T(8,128)(2,1)S(1)}, bf16[8,96,640]{2,1,0:T(8,128)(2,1)S(1)}, u32[]{:S(2)}, u32[]{:S(2)}) collective-permute-start(bf16[8,96,640]{2,1,0:T(8,128)(2,1)S(1)} %pad_maximum_fusion.7), channel_id=1, source_target_pairs={{0,4},{2,6},{4,0},{6,2},{8,12},{10,14},{12,8},{14,10},{16,20},{18,... | collective-permute-start | bytes 2949128 | tf_op jit(solution)/shard_map/ppermute | solution.py:436
  137.1 21.8 %collective-permute-start.12 = (bf16[8,96,640]{2,1,0:T(8,128)(2,1)S(1)}, bf16[8,96,640]{2,1,0:T(8,128)(2,1)S(1)}, u32[]{:S(2)}, u32[]{:S(2)}) collective-permute-start(bf16[8,96,640]{2,1,0:T(8,128)(2,1)S(1)} %pad_maximum_fusion.8), channel_id=1, source_target_pairs={{0,8},{2,10},{4,12},{6,14},{8,0},{10,2},{12,4},{14,6},{16,24},{18,... | collective-permute-start | bytes 2949128 | tf_op jit(solution)/shard_map/ppermute | solution.py:436
  139.4 104.7 %collective-permute-start.16 = (bf16[8,96,1024]{2,1,0:T(8,128)(2,1)}, bf16[8,96,1024]{2,1,0:T(8,128)(2,1)}, u32[]{:S(2)}, u32[]{:S(2)}) collective-permute-start(bf16[8,96,1024]{2,1,0:T(8,128)(2,1)} %pad_maximum_fusion.1), channel_id=1, source_target_pairs={{0,2},{2,0},{4,6},{6,4},{8,10},{10,8},{12,14},{14,12},{16,18},{18,... | collective-permute-start | bytes 4718600 | tf_op jit(solution)/shard_map/ppermute | solution.py:436
  148.2 98.6 %collective-permute-start.20 = (bf16[8,96,1024]{2,1,0:T(8,128)(2,1)}, bf16[8,96,1024]{2,1,0:T(8,128)(2,1)}, u32[]{:S(2)}, u32[]{:S(2)}) collective-permute-start(bf16[8,96,1024]{2,1,0:T(8,128)(2,1)} %pad_maximum_fusion.2), channel_id=1, source_target_pairs={{0,4},{2,6},{4,0},{6,2},{8,12},{10,14},{12,8},{14,10},{16,20},{18,... | collective-permute-start | bytes 4718600 | tf_op jit(solution)/shard_map/ppermute | solution.py:436
  158.2 91.3 %collective-permute-start.24 = (bf16[8,96,1024]{2,1,0:T(8,128)(2,1)}, bf16[8,96,1024]{2,1,0:T(8,128)(2,1)}, u32[]{:S(2)}, u32[]{:S(2)}) collective-permute-start(bf16[8,96,1024]{2,1,0:T(8,128)(2,1)} %pad_maximum_fusion.3), channel_id=1, source_target_pairs={{0,8},{2,10},{4,12},{6,14},{8,0},{10,2},{12,4},{14,6},{16,24},{18,... | collective-permute-start | bytes 4718600 | tf_op jit(solution)/shard_map/ppermute | solution.py:436
  402.5 71.3 %collective-permute-start.27 = (f32[1024,256]{0,1:T(8,128)}, f32[1024,256]{0,1:T(8,128)}, u32[]{:S(2)}, u32[]{:S(2)}) collective-permute-start(f32[1024,256]{0,1:T(8,128)} %pad_maximum_fusion.5), channel_id=1, source_target_pairs={{0,1},{1,0},{2,3},{3,2},{4,5},{5,4},{6,7},{7,6},{8,9},{9,8},{10,11... | collective-permute-start | bytes 3145736 | tf_op jit(solution)/shard_map/ppermute | solution.py:412
  417.6 290.3 %collective-permute-start.25 = (f32[512,1536]{1,0:T(8,128)}, f32[512,1536]{1,0:T(8,128)}, u32[]{:S(2)}, u32[]{:S(2)}) collective-permute-start(f32[512,1536]{1,0:T(8,128)} %constant_dynamic-slice_fusion.11), channel_id=1, source_target_pairs={{0,1},{1,0},{2,3},{3,2},{4,5},{5,4},{6,7},{7,6},{8,9},{9,8},{10,11... | collective-permute-start | bytes 9437192 | tf_op jit(solution)/shard_map/ppermute | solution.py:412
  422.2 26.5 %collective-permute-start.42 = (bf16[2,2,2,96,512]{4,3,2,1,0:T(8,128)(2,1)}, bf16[2,2,2,96,512]{4,3,2,1,0:T(8,128)(2,1)}, u32[]{:S(2)}, u32[]{:S(2)}) collective-permute-start(bf16[2,2,2,96,512]{4,3,2,1,0:T(8,128)(2,1)} %get-tuple-element.178), channel_id=1, source_target_pairs={{0,8},{2,10},{4,12},{6,14},{8,0},{10,2},{12,4},{14,6},{16,24},{18,... | collective-permute-start | bytes 2359304 | tf_op jit(solution)/shard_map/ppermute | solution.py:436
  425.1 25.6 %collective-permute-start.38 = (bf16[2,2,2,96,512]{4,3,2,1,0:T(8,128)(2,1)}, bf16[2,2,2,96,512]{4,3,2,1,0:T(8,128)(2,1)}, u32[]{:S(2)}, u32[]{:S(2)}) collective-permute-start(bf16[2,2,2,96,512]{4,3,2,1,0:T(8,128)(2,1)} %get-tuple-element.176), channel_id=1, source_target_pairs={{0,4},{2,6},{4,0},{6,2},{8,12},{10,14},{12,8},{14,10},{16,20},{18,... | collective-permute-start | bytes 2359304 | tf_op jit(solution)/shard_map/ppermute | solution.py:436
  427.6 19.4 %collective-permute-start.34 = (bf16[2,2,2,96,512]{4,3,2,1,0:T(8,128)(2,1)}, bf16[2,2,2,96,512]{4,3,2,1,0:T(8,128)(2,1)}, u32[]{:S(2)}, u32[]{:S(2)}) collective-permute-start(bf16[2,2,2,96,512]{4,3,2,1,0:T(8,128)(2,1)} %dynamic-slice_bitcast_fusion.5), channel_id=1, source_target_pairs={{0,2},{2,0},{4,6},{6,4},{8,10},{10,8},{12,14},{14,12},{16,18},{18,... | collective-permute-start | bytes 2359304 | tf_op jit(solution)/shard_map/ppermute | solution.py:436
  447.0 18.2 %collective-permute-start.66 = (bf16[2,2,2,96,512]{4,3,0,1,2:T(8,128)(2,1)S(1)}, bf16[2,2,2,96,512]{4,3,0,1,2:T(8,128)(2,1)S(1)}, u32[]{:S(2)}, u32[]{:S(2)}) collective-permute-start(bf16[2,2,2,96,512]{4,3,0,1,2:T(8,128)(2,1)S(1)} %bitcast.418), channel_id=1, source_target_pairs={{0,8},{2,10},{4,12},{6,14},{8,0},{10,2},{12,4},{14,6},{16,24},{18,... | collective-permute-start | bytes 2359304 | tf_op jit(solution)/shard_map/ppermute | solution.py:436
  448.7 20.8 %collective-permute-start.62 = (bf16[2,2,2,96,512]{4,3,2,0,1:T(8,128)(2,1)S(1)}, bf16[2,2,2,96,512]{4,3,2,0,1:T(8,128)(2,1)S(1)}, u32[]{:S(2)}, u32[]{:S(2)}) collective-permute-start(bf16[2,2,2,96,512]{4,3,2,0,1:T(8,128)(2,1)S(1)} %bitcast.417), channel_id=1, source_target_pairs={{0,4},{2,6},{4,0},{6,2},{8,12},{10,14},{12,8},{14,10},{16,20},{18,... | collective-permute-start | bytes 2359304 | tf_op jit(solution)/shard_map/ppermute | solution.py:436
  450.8 20.5 %collective-permute-start.58 = (bf16[2,2,2,96,512]{4,3,0,1,2:T(8,128)(2,1)S(1)}, bf16[2,2,2,96,512]{4,3,0,1,2:T(8,128)(2,1)S(1)}, u32[]{:S(2)}, u32[]{:S(2)}) collective-permute-start(bf16[2,2,2,96,512]{4,3,0,1,2:T(8,128)(2,1)S(1)} %bitcast.416), channel_id=1, source_target_pairs={{0,2},{2,0},{4,6},{6,4},{8,10},{10,8},{12,14},{14,12},{16,18},{18,... | collective-permute-start | bytes 2359304 | tf_op jit(solution)/shard_map/ppermute | solution.py:436
  465.2 63.2 %collective-permute-start.43 = (bf16[2,2,96,512]{3,2,0,1:T(8,128)(2,1)}, bf16[2,2,96,512]{3,2,0,1:T(8,128)(2,1)}, u32[]{:S(2)}, u32[]{:S(2)}) collective-permute-start(bf16[2,2,96,512]{3,2,0,1:T(8,128)(2,1)} %fusion.38), channel_id=1, source_target_pairs={{0,2},{2,0},{4,6},{6,4},{8,10},{10,8},{12,14},{14,12},{16,18},{18,... | collective-permute-start | bytes 1179656 | tf_op jit(solution)/shard_map/ppermute | solution.py:436
  469.5 62.6 %collective-permute-start.39 = (bf16[2,2,96,512]{3,2,1,0:T(8,128)(2,1)}, bf16[2,2,96,512]{3,2,1,0:T(8,128)(2,1)}, u32[]{:S(2)}, u32[]{:S(2)}) collective-permute-start(bf16[2,2,96,512]{3,2,1,0:T(8,128)(2,1)} %fusion.37), channel_id=1, source_target_pairs={{0,8},{2,10},{4,12},{6,14},{8,0},{10,2},{12,4},{14,6},{16,24},{18,... | collective-permute-start | bytes 1179656 | tf_op jit(solution)/shard_map/ppermute | solution.py:436
  471.3 62.6 %collective-permute-start.35 = (bf16[2,2,96,512]{3,2,1,0:T(8,128)(2,1)}, bf16[2,2,96,512]{3,2,1,0:T(8,128)(2,1)}, u32[]{:S(2)}, u32[]{:S(2)}) collective-permute-start(bf16[2,2,96,512]{3,2,1,0:T(8,128)(2,1)} %fusion.36), channel_id=1, source_target_pairs={{0,4},{2,6},{4,0},{6,2},{8,12},{10,14},{12,8},{14,10},{16,20},{18,... | collective-permute-start | bytes 1179656 | tf_op jit(solution)/shard_map/ppermute | solution.py:436
  473.8 61.3 %collective-permute-start.67 = (bf16[2,2,96,512]{3,2,0,1:T(8,128)(2,1)}, bf16[2,2,96,512]{3,2,0,1:T(8,128)(2,1)}, u32[]{:S(2)}, u32[]{:S(2)}) collective-permute-start(bf16[2,2,96,512]{3,2,0,1:T(8,128)(2,1)} %fusion.41), channel_id=1, source_target_pairs={{0,2},{2,0},{4,6},{6,4},{8,10},{10,8},{12,14},{14,12},{16,18},{18,... | collective-permute-start | bytes 1179656 | tf_op jit(solution)/shard_map/ppermute | solution.py:436
  533.9 152.2 %collective-permute-start.28 = (f32[512,1536]{1,0:T(8,128)S(1)}, f32[512,1536]{1,0:T(8,128)S(1)}, u32[]{:S(2)}, u32[]{:S(2)}) collective-permute-start(f32[512,1536]{1,0:T(8,128)S(1)} %copy-done.42), channel_id=1, source_target_pairs={{0,1},{1,0},{2,3},{3,2},{4,5},{5,4},{6,7},{7,6},{8,9},{9,8},{10,11... | collective-permute-start | bytes 9437192 | tf_op jit(solution)/shard_map/ppermute | solution.py:412
  535.2 104.6 %collective-permute-start.54 = (bf16[2,2,2,96,640]{4,3,2,1,0:T(8,128)(2,1)S(1)}, bf16[2,2,2,96,640]{4,3,2,1,0:T(8,128)(2,1)S(1)}, u32[]{:S(2)}, u32[]{:S(2)}) collective-permute-start(bf16[2,2,2,96,640]{4,3,2,1,0:T(8,128)(2,1)S(1)} %dynamic-slice_bitcast_fusion), channel_id=1, source_target_pairs={{0,8},{2,10},{4,12},{6,14},{8,0},{10,2},{12,4},{14,6},{16,24},{18,... | collective-permute-start | bytes 2949128 | tf_op jit(solution)/shard_map/ppermute | solution.py:436
  537.5 104.4 %collective-permute-start.50 = (bf16[2,2,2,96,640]{4,3,2,1,0:T(8,128)(2,1)S(1)}, bf16[2,2,2,96,640]{4,3,2,1,0:T(8,128)(2,1)S(1)}, u32[]{:S(2)}, u32[]{:S(2)}) collective-permute-start(bf16[2,2,2,96,640]{4,3,2,1,0:T(8,128)(2,1)S(1)} %dynamic-slice_bitcast_fusion.1), channel_id=1, source_target_pairs={{0,4},{2,6},{4,0},{6,2},{8,12},{10,14},{12,8},{14,10},{16,20},{18,... | collective-permute-start | bytes 2949128 | tf_op jit(solution)/shard_map/ppermute | solution.py:436
  540.0 25.6 %collective-permute-start.44 = (bf16[2,96,512]{2,1,0:T(8,128)(2,1)S(1)}, bf16[2,96,512]{2,1,0:T(8,128)(2,1)S(1)}, u32[]{:S(2)}, u32[]{:S(2)}) collective-permute-start(bf16[2,96,512]{2,1,0:T(8,128)(2,1)S(1)} %fusion.47), channel_id=1, source_target_pairs={{0,4},{2,6},{4,0},{6,2},{8,12},{10,14},{12,8},{14,10},{16,20},{18,... | collective-permute-start | bytes 589832 | tf_op jit(solution)/shard_map/ppermute | solution.py:436
  637.8 24.2 %collective-permute-start.46 = (bf16[2,2,2,96,640]{4,3,2,1,0:T(8,128)(2,1)S(1)}, bf16[2,2,2,96,640]{4,3,2,1,0:T(8,128)(2,1)S(1)}, u32[]{:S(2)}, u32[]{:S(2)}) collective-permute-start(bf16[2,2,2,96,640]{4,3,2,1,0:T(8,128)(2,1)S(1)} %dynamic-slice_bitcast_fusion.2), channel_id=1, source_target_pairs={{0,2},{2,0},{4,6},{6,4},{8,10},{10,8},{12,14},{14,12},{16,18},{18,... | collective-permute-start | bytes 2949128 | tf_op jit(solution)/shard_map/ppermute | solution.py:436
  640.0 27.2 %collective-permute-start.55 = (bf16[2,2,96,640]{3,2,1,0:T(8,128)(2,1)S(1)}, bf16[2,2,96,640]{3,2,1,0:T(8,128)(2,1)S(1)}, u32[]{:S(2)}, u32[]{:S(2)}) collective-permute-start(bf16[2,2,96,640]{3,2,1,0:T(8,128)(2,1)S(1)} %fusion.35), channel_id=1, source_target_pairs={{0,2},{2,0},{4,6},{6,4},{8,10},{10,8},{12,14},{14,12},{16,18},{18,... | collective-permute-start | bytes 1474568 | tf_op jit(solution)/shard_map/ppermute | solution.py:436
  642.2 26.8 %collective-permute-start.51 = (bf16[2,2,96,640]{3,2,1,0:T(8,128)(2,1)S(1)}, bf16[2,2,96,640]{3,2,1,0:T(8,128)(2,1)S(1)}, u32[]{:S(2)}, u32[]{:S(2)}) collective-permute-start(bf16[2,2,96,640]{3,2,1,0:T(8,128)(2,1)S(1)} %fusion.34), channel_id=1, source_target_pairs={{0,8},{2,10},{4,12},{6,14},{8,0},{10,2},{12,4},{14,6},{16,24},{18,... | collective-permute-start | bytes 1474568 | tf_op jit(solution)/shard_map/ppermute | solution.py:436
  669.1 14.7 %collective-permute-start.52 = (bf16[2,96,640]{2,1,0:T(8,128)(2,1)S(1)}, bf16[2,96,640]{2,1,0:T(8,128)(2,1)S(1)}, u32[]{:S(2)}, u32[]{:S(2)}) collective-permute-start(bf16[2,96,640]{2,1,0:T(8,128)(2,1)S(1)} %fusion.43), channel_id=1, source_target_pairs={{0,16},{2,18},{4,20},{6,22},{8,24},{10,26},{12,28},{14,30},{16,0},... | collective-permute-start | bytes 737288 | tf_op jit(solution)/shard_map/ppermute | solution.py:436
  672.5 12.7 %collective-permute-start.48 = (bf16[2,96,640]{2,1,0:T(8,128)(2,1)S(1)}, bf16[2,96,640]{2,1,0:T(8,128)(2,1)S(1)}, u32[]{:S(2)}, u32[]{:S(2)}) collective-permute-start(bf16[2,96,640]{2,1,0:T(8,128)(2,1)S(1)} %fusion.42), channel_id=1, source_target_pairs={{0,8},{2,10},{4,12},{6,14},{8,0},{10,2},{12,4},{14,6},{16,24},{18,... | collective-permute-start | bytes 737288 | tf_op jit(solution)/shard_map/ppermute | solution.py:436
  675.0 10.9 %collective-permute-start.57 = (bf16[96,640]{1,0:T(8,128)(2,1)S(1)}, bf16[96,640]{1,0:T(8,128)(2,1)S(1)}, u32[]{:S(2)}, u32[]{:S(2)}) collective-permute-start(bf16[96,640]{1,0:T(8,128)(2,1)S(1)} %fusion.54), channel_id=1, source_target_pairs={{0,16},{2,18},{4,20},{6,22},{8,24},{10,26},{12,28},{14,30},{16,0},... | collective-permute-start | bytes 368648 | tf_op jit(solution)/shard_map/ppermute | solution.py:436
  (129 other events, 1039.7 us)

commit v3 on v2

--- a/solution.py
+++ b/solution.py
@@ -1,11 +1,10 @@
-from functools import partial
-
 import jax
 import jax.numpy as jnp
 from jax import lax
 from jax.experimental import pallas as pl
 from jax.experimental.pallas import tpu as pltpu
 from jax.sharding import PartitionSpec as P
+
 
 EPSILON = 1e-05
 HIGHEST = lax.Precision.HIGHEST
@@ -81,7 +80,7 @@
         row_of = pl.ds(pl.multiple_of(place * 8, 8), 8)
         for pair in range(width // pair_width):
             lanes = slice(pair * pair_width, (pair + 1) * pair_width)
-            unused_cur, unused_shift, value = conv_pair(
+            _, _, value = conv_pair(
                 xr, taps, bias, masks, rows, before, lanes
             )
             x = value * jax.nn.sigmoid(value)
@@ -308,7 +307,7 @@
         ],
         scratch_shapes=[pltpu.VMEM((state_dim, width), F32)],
         cost_estimate=pl.CostEstimate(
-            flops=8 * length * inner * CHUNK, bytes_accessed=12 * length * inner, transcendentals=0
+            flops=130 * length * inner * CHUNK, bytes_accessed=12 * length * inner, transcendentals=0
         ),
         name="ssd_forward",
     )(xr, taps, bias, skip_row, *shared, *grouped)
@@ -370,7 +369,7 @@
         ],
         scratch_shapes=[pltpu.VMEM((state_dim, width), F32), pltpu.VMEM((8, width), F32)],
         cost_estimate=pl.CostEstimate(
-            flops=24 * length * inner * CHUNK, bytes_accessed=16 * length * inner, transcendentals=0
+            flops=290 * length * inner * CHUNK, bytes_accessed=16 * length * inner, transcendentals=0
         ),
         name="ssd_backward",
     )(xr, taps, bias, skip_row, *shared, *grouped, states, dy)
@@ -378,12 +377,10 @@
     dscore_t = (dscore_t.reshape(chunks, CHUNK, CHUNK) * allowed.transpose(0, 2, 1)).astype(BF16)
     parted_c = cs_low.reshape(chunks, CHUNK, state_dim)
     parted_b = bs_low.reshape(chunks, CHUNK, state_dim)
-    dbs = dbs + jnp.einsum(
-        "cst,ctn->csn", dscore_t, parted_c, preferred_element_type=F32
-    ).reshape(length, state_dim)
-    dcs = dcs + jnp.einsum(
-        "cst,csn->ctn", dscore_t, parted_b, preferred_element_type=F32
-    ).reshape(length, state_dim)
+    from_score_b = jnp.einsum("cst,ctn->csn", dscore_t, parted_c, preferred_element_type=F32)
+    from_score_c = jnp.einsum("cst,csn->ctn", dscore_t, parted_b, preferred_element_type=F32)
+    dbs = dbs + from_score_b.reshape(length, state_dim)
+    dcs = dcs + from_score_c.reshape(length, state_dim)
     heads = groups * heads_step
 
     def from_columns(slot):
@@ -437,59 +434,103 @@
 
 
 def place_kernel(table, *refs):
-    out = refs[-1]
-    start = 0
-    for ref in refs[:-1]:
-        width = ref.shape[2]
-        out[:, start : start + width] = ref[0]
-        start += width
-
-
-def gather_rows(shard):
+    sources, (out, buffer, arrived, left) = refs[:-4], refs[-4:]
+    turns, size = len(sources) // 2, out.shape[0]
+    half = size // 2
+    width = sources[0].shape[2]
+
+    def arrival(turn, source, block, target):
+        lanes = pl.ds(turn * width, width)
+        return pltpu.make_async_copy(
+            source.at[block], buffer.at[target, :, lanes], arrived.at[turn, target]
+        )
+
+    def start_in(target, unused):
+        for turn in range(turns):
+            block = table[turn, target]
+
+            @pl.when(block < half)
+            def from_own():
+                arrival(turn, sources[2 * turn], block, target).start()
+
+            @pl.when(block >= half)
+            def from_other():
+                arrival(turn, sources[2 * turn + 1], block - half, target).start()
+
+        return unused
+
+    def start_out(target, unused):
+        for turn in range(turns):
+            arrival(turn, sources[2 * turn], 0, target).wait()
+        pltpu.make_async_copy(buffer.at[target], out.at[target], left.at[target]).start()
+        return unused
+
+    def finish(target, unused):
+        pltpu.make_async_copy(buffer.at[target], out.at[target], left.at[target]).wait()
+        return unused
+
+    lax.fori_loop(0, size, start_in, 0)
+    lax.fori_loop(0, size, start_out, 0)
+    lax.fori_loop(0, size, finish, 0)
+
+
+def gather_stages(pieces, first_stage, last_stage):
+    orders = stage_orders(lax.axis_size("dp"))
+    for stage in range(first_stage, last_stage):
+        joined = []
+        for piece, order in zip(pieces, orders):
+            other = partner(piece, order[::-1][stage])
+            if stage == len(order) - 1:
+                joined.append((piece, other))
+            else:
+                joined.append(jnp.concatenate([piece, other], axis=0))
+        pieces = joined
+    return pieces
+
+
+def split_shard(shard):
+    turns = len(stage_orders(lax.axis_size("dp")))
+    width = shard.shape[1] // turns
+    return [shard[None, :, turn * width : (turn + 1) * width] for turn in range(turns)]
+
+
+def place_rows(pieces):
     size, index = lax.axis_size("dp"), lax.axis_index("dp")
     orders = stage_orders(size)
-    rows, width = shard.shape[0], shard.shape[1] // len(orders)
     targets = jnp.arange(size, dtype=jnp.int32) ^ index.astype(jnp.int32)
-    pieces = [shard[None, :, turn * width : (turn + 1) * width] for turn in range(len(orders))]
-    tables = []
-    for order in orders:
-        stages = order[::-1]
-        tables.append(sum(((targets >> bit) & 1) << stage for stage, bit in enumerate(stages)))
-    for stage in range(size.bit_length() - 1):
-        pieces = [
-            jnp.concatenate([piece, partner(piece, order[::-1][stage])], axis=0)
-            for piece, order in zip(pieces, orders)
-        ]
-
-    def piece_spec(turn):
-        return pl.BlockSpec((1, rows, width), lambda d, table: (table[turn, d], 0, 0))
-
-    return pl.pallas_call(
+    tables = [
+        sum(((targets >> bit) & 1) << stage for stage, bit in enumerate(order[::-1]))
+        for order in orders
+    ]
+    _, rows, width = pieces[0][0].shape
+    sources = [part for pair in pieces for part in pair]
+    shape = (size, rows, width * len(orders))
+    placed = pl.pallas_call(
         place_kernel,
-        grid_spec=pltpu.PrefetchScalarGridSpec(
-            num_scalar_prefetch=1,
-            grid=(size,),
-            in_specs=[piece_spec(turn) for turn in range(len(orders))],
-            out_specs=pl.BlockSpec((rows, shard.shape[1]), lambda d, table: (d, 0)),
-        ),
-        out_shape=jax.ShapeDtypeStruct((size * rows, shard.shape[1]), shard.dtype),
+        in_specs=[pl.BlockSpec(memory_space=pltpu.SMEM)]
+        + [pl.BlockSpec(memory_space=pl.ANY)] * len(sources),
+        out_specs=pl.BlockSpec(memory_space=pl.ANY),
+        out_shape=jax.ShapeDtypeStruct(shape, BF16),
+        scratch_shapes=[
+            pltpu.VMEM(shape, BF16),
+            pltpu.SemaphoreType.DMA((len(orders), size)),
+            pltpu.SemaphoreType.DMA((size,)),
+        ],
         cost_estimate=pl.CostEstimate(
-            flops=0, bytes_accessed=4 * size * shard.size, transcendentals=0
+            flops=0, bytes_accessed=4 * size * rows * shape[2], transcendentals=0
         ),
         name="place_rows",
-    )(jnp.stack(tables), *pieces)
-
-
-def scatter_rows(values):
+    )(jnp.stack(tables), *sources)
+    return placed.reshape(size * rows, shape[2])
+
+
+def scatter_rows(pieces):
     size, index = lax.axis_size("dp"), lax.axis_index("dp")
     bits = size.bit_length() - 1
     orders = stage_orders(size)
-    width = values.shape[1] // len(orders)
-    rows = values.shape[0] // size
     held, left = [], []
-    for turn in range(len(orders)):
-        piece = values[:, turn * width : (turn + 1) * width]
-        held.append(piece.reshape((2,) * bits + (rows, width)))
+    for piece in pieces:
+        held.append(piece.reshape((2,) * bits + (piece.shape[0] // size, piece.shape[1])))
         left.append(list(range(bits - 1, -1, -1)))
     for stage in range(bits):
         for turn, order in enumerate(orders):
@@ -501,7 +542,12 @@
             got = partner(sent.astype(BF16), bit)
             held[turn] = kept.astype(F32) + got.astype(F32)
             left[turn].pop(axis)
-    return jnp.concatenate(held, axis=1)
+    return held
+
+
+def column_thirds(values):
+    width = values.shape[1] // 3
+    return [values[:, turn * width : (turn + 1) * width] for turn in range(3)]
 
 
 def sum_small(values):
@@ -550,9 +596,13 @@
         ],
         axis=1,
     )
-    first_weights = gather_rows(first_shard)
+    bits = lax.axis_size("dp").bit_length() - 1
+    first_pieces = gather_stages(split_shard(first_shard), 0, bits)
     later_shard = jnp.concatenate([in_gate_inner[:, 0], out_proj.T], axis=1)
-    later_weights = gather_rows(later_shard)
+    later_pieces = gather_stages(split_shard(later_shard), 0, 2)
+    first_pieces, later_pieces = lax.optimization_barrier((first_pieces, later_pieces))
+    later_pieces = gather_stages(later_pieces, 2, bits)
+    first_weights = place_rows(first_pieces)
     normed = gather_pair(normed_own, tensor_place)
     first_proj = dot(normed, first_weights)
     state_end = inner_dev + 2 * state_dim
@@ -582,6 +632,7 @@
     mixed, states, score = ssd_forward(
         inner_proj, conv_inner, bias_row, skip_row, terms, bs_low, cs_low
     )
+    later_weights = place_rows(later_pieces)
     gate_weights = later_weights[:, :inner_dev]
     out_weights_t = later_weights[:, inner_dev:]
     gate_proj = dot(normed, gate_weights)
@@ -622,11 +673,29 @@
     grad_mixed, grad_gate_half, grad_out_low = lax.optimization_barrier(
         (grad_mixed, grad_gate_half, grad_out_low)
     )
-    gate_part = scatter_rows(grad_gate_half)
-    out_part = scatter_rows(grad_out_low)
-    low_inner, grad_bs, grad_cs, grad_step_size, grad_log, inner_sums = ssd_backward(
-        inner_proj, conv_inner, bias_row, skip_row, terms, score, bs_low, cs_low, states, grad_mixed
-    )
+    cut = 2 * inner_dev // 3
+    early_parts = scatter_rows(
+        [
+            grad_gate_half[:, :cut],
+            jnp.concatenate([grad_gate_half[:, cut:], grad_out_low[:, : 2 * cut - inner_dev]], axis=1),
+            grad_out_low[:, 2 * cut - inner_dev :],
+        ],
+    )
+    early_part = jnp.concatenate(early_parts, axis=1)
+    gate_part, out_part = early_part[:, :inner_dev], early_part[:, inner_dev:]
+    scan_back = ssd_backward(
+        inner_proj,
+        conv_inner,
+        bias_row,
+        skip_row,
+        terms,
+        score,
+        bs_low,
+        cs_low,
+        states,
+        grad_mixed,
+    )
+    low_inner, grad_bs, grad_cs, grad_step_size, grad_log, inner_sums = scan_back
     taps_count = conv_inner.shape[0]
     grad_conv_inner = inner_sums[:taps_count][::-1]
     grad_conv_inner_bias = inner_sums[taps_count]
@@ -644,10 +713,9 @@
     own_state = low_state * (tensor_place == 0).astype(BF16)
     low_pad = jnp.zeros((low_step.shape[0], step_pad), BF16)
     low_first = jnp.concatenate([low_inner, low_state, low_step, low_pad], axis=1)
-    grad_first = jnp.einsum(
-        "td,tc->dc", normed, low_first, preferred_element_type=F32
-    ).astype(BF16)
-    first_part = scatter_rows(grad_first)
+    grad_first = jnp.einsum("td,tc->dc", normed, low_first, preferred_element_type=F32).astype(BF16)
+    grad_first, low_inner, low_gate = lax.optimization_barrier((grad_first, low_inner, low_gate))
+    first_part = jnp.concatenate(scatter_rows(column_thirds(grad_first)), axis=1)
     grad_out_proj = out_part.T
     grad_in_gate_inner = jnp.stack([gate_part, first_part[:, :inner_dev]], axis=1)
     grad_in_state = first_part[:, inner_dev:state_end].reshape(in_state.shape)
@@ -725,4 +793,5 @@
         P("tensor"),
         P("tensor", "dp"),
     )
+
     return jax.shard_map(shards, mesh=mesh, in_specs=in_specs, out_specs=out_specs, check_vma=False)

time: 727 us -> 623 us (0.86)
  waiting for transfers between devices: 180 us -> 123 us
  local copies, waits for them, and re-layouts: 143 us -> 116 us
  Pallas kernels: 109 us -> 99.1 us
    ppermute x64 -> x52, waiting for transfers between devices: 179 us -> 123 us  [partner(): return lax.ppermute(values, 'dp', [(i, i ^ 1 << bit) for i in range(size)])]
    unnamed x246 -> x239, local copies, waits for them, and re-layouts: 35.1 us -> 21.3 us
    pallas_call x2, Pallas kernels: 25.1 us -> 15.1 us  [place_rows(): pl.pallas_call(place_kernel, in_specs=[pl.BlockSpec(memory_space=pltpu.SM...]
    ppermute x64 -> x52, starting transfers between devices: 63.3 us -> 59.6 us  [partner(): return lax.ppermute(values, 'dp', [(i, i ^ 1 << bit) for i in range(size)])]
    concatenate x18 -> x16, other arithmetic: 16.6 us -> 15.6 us  [the longest x15 15.3 us: gather_stages(): joined.append(jnp.concatenate([piece, other], axis=0))]
  transfers between devices with their start and end apart: 70 -> 58, of which waited for: 35 -> 26; matrix products, arithmetic and copies ran while one was open for 37% -> 35% of each run, Pallas kernels for 5% -> 4%
where the time goes in v3:
time: 623 us; the launch traced here: 615 us
  waiting for transfers between devices  123 us (20%)
  other arithmetic  119 us (19%)
  local copies, waits for them, and re-layouts  116 us (19%)
  Pallas kernels  99.1 us (16%)
  matrix products  89.7 us (14%)
  starting transfers between devices  60.7 us (10%)
    ppermute x52, waiting for transfers between devices, partner(): return lax.ppermute(values, 'dp', [(i, i ^ 1 << bit) for i in range(size)])  123 us
    ppermute x52, starting transfers between devices, partner(): return lax.ppermute(values, 'dp', [(i, i ^ 1 << bit) for i in range(size)])  59.6 us
    pallas_call x1, Pallas kernels, ssd_backward(): pl.pallas_call(ssd_backward_kernel, grid=(groups,), in_specs=[lanes_spec(...  58 us
    pallas_call x1, Pallas kernels, ssd_forward(): pl.pallas_call(ssd_forward_kernel, grid=(groups,), in_specs=[lanes_spec(a...  25.9 us
    unnamed x239, local copies, waits for them, and re-layouts  21.3 us
    dot_general x2, matrix products, dot(): return jnp.dot(a, b, preferred_element_type=F32)  21 us
    dot_general x2, matrix products, dot_nt(): lax.dot_general(a, b, (((1,), (1,)), ((), ())), preferred_element_type=F32)  17.4 us
    concatenate x15, other arithmetic, gather_stages(): joined.append(jnp.concatenate([piece, other], axis=0))  15.3 us
  transfers between devices with their start and end apart: 58, of which 26 were waited for; matrix products, arithmetic and copies ran while one was open for 35% of the time, Pallas kernels for 4%

profile of v3, /device:TPU:0, one launch (start us, length us, event | category | flops | bytes accessed | tf_op | source)
XLA Modules:
  0.0 615.5 jit_solution(10188999028105465292)
XLA Ops:
  7.9 3.6 collective-permute-start.1
  18.5 2.6 collective-permute-start.13
  54.0 2.7 collective-permute-start.6
  59.2 3.9 collective-permute-done.17
  66.7 6.1 collective-permute-done.6
  76.5 4.6 collective-permute-done.14
  82.1 6.5 %collective-permute-done.16 = bf16[2,96,1024]{2,1,0:T(8,128)(2,1)S(1)} collective-permute-done((bf16[2,96,1024]{2,1,0:T(8,128)(2,1)S(1)}, bf16[2,96,1024]{2,1,0:T(8,128)(2,1)S(1)}, u32[]{:S(2)}, u32[]{:S(2)}) %collective-permute-start.16) | collective-permute-done | bytes 393248 | tf_op jit(solution)/shard_map/ppermute | solution.py:433
  98.8 3.9 collective-permute-done.11
  106.5 7.3 %fusion.13 = bf16[1024,1536]{1,0:T(8,128)(2,1)} fusion(s32[]{:T(128)S(6)} %select_n.162, bf16[512,1536]{1,0:T(8,128)(2,1)S(1)} %fusion.16, bf16[512,1536]{1,0:T(8,128)(2,1)} %collective-permute-done), kind=kLoop, calls=%fused_computation.38 | loop fusion | flops 9437184 | bytes 6291460 | tf_op jit(solution)/shard_map/concatenate | solution.py:413
  113.8 6.9 %fusion.11 = bf16[1024,1536]{1,0:T(8,128)(2,1)} fusion(s32[]{:T(128)S(6)} %select_n.162, bf16[512,1536]{1,0:T(8,128)(2,1)S(1)} %copy-done.15, bf16[512,1536]{1,0:T(8,128)(2,1)S(1)} %collective-permute-done.26), kind=kLoop, calls=%fused_computation.36 | loop fusion | flops 9437184 | bytes 6291460 | tf_op jit(solution)/shard_map/concatenate | solution.py:413
  124.8 6.3 %place_rows.2 = bf16[16,96,1920]{2,1,0:T(8,128)(2,1)} custom-call(s32[3,16]{1,0:T(4,128)} %pad_add_fusion.table, bf16[8,96,640]{2,1,0:T(8,128)(2,1)} %copy-done.27, bf16[8,96,640]{2,1,0:T(8,128)(2,1)} %copy-done.50, bf16[8,96,640]{2,1,0:T(8,128)(2,1)} %copy-done.28, bf16[8,96,640]{2,1,0:T(8,128)(2,1)} %copy-done.51, bf16[8,96,640]{2,1,0:T(8,128)(2,1)} %copy-done.29, ...), custom_call_target="tpu_custom_call" | custom-call | bytes 11796480 | tf_op jit(solution)/shard_map/place_rows/pallas_call | solution.py:508
  131.2 9.0 %fusion.82 = f32[1024,1920]{1,0:T(8,128)S(1)} fusion(bf16[1024,1536]{1,0:T(8,128)(2,1)S(1)} %copy-done.34, bf16[1536,1920]{1,0:T(8,128)(2,1)} %bitcast.308), kind=kOutput, calls=%fused_computation.317 | convolution fusion | flops 6039797760 | bytes 16908288 | tf_op jit(solution)/shard_map/dot_general | solution.py:35
  140.4 2.9 copy-done.1
  148.4 3.6 multiply_convert_fusion.2
  166.5 5.9 slice.246.xr
  195.3 25.9 %ssd_forward.1 = (f32[1024,1536]{1,0:T(8,128)}, bf16[1024,1536]{1,0:T(8,128)(2,1)}) custom-call(f32[1024,1536]{1,0:T(8,128)} %slice.246.xr, f32[4,1536]{1,0:T(4,128)} %taps.3, f32[1,1536]{1,0:T(1,128)} %broadcast_in_dim.31.bias, f32[1,1536]{1,0:T(1,128)} %broadcast_in_dim_reshape.2.skip, f32[3,1024,128]{2,1,0:T(8,128)} %pad_maximum_fusion.1.masks, ...), custom_call_target="tpu_custom_call" | custom-call | flops 26172456960 | bytes 18874368 | tf_op jit(solution)/shard_map/ssd_forward/pallas_call | solution.py:294
  225.9 8.8 %place_rows.3 = bf16[16,96,3072]{2,1,0:T(8,128)(2,1)} custom-call(s32[3,16]{1,0:T(4,128)} %pad_add_fusion.table, bf16[8,96,1024]{2,1,0:T(8,128)(2,1)} %constant_dynamic-update-slice_fusion.refs_0_, bf16[8,96,1024]{2,1,0:T(8,128)(2,1)} %collective-permute-done.20.refs_1_, bf16[8,96,1024]{2,1,0:T(8,128)(2,1)} %copy-done.31, ...), custom_call_target="tpu_custom_call" | custom-call | bytes 18874368 | tf_op jit(solution)/shard_map/place_rows/pallas_call | solution.py:508
  234.7 12.0 %multiply_reduce_fusion.2 = (f32[1024]{0:T(1024)S(1)}, f32[1024,1536]{1,0:T(8,128)}, f32[1024,1536]{1,0:T(8,128)}) fusion(f32[1024,1536]{1,0:T(8,128)} %get-tuple-element.46, bf16[1024,1536]{1,0:T(8,128)(2,1)S(1)} %copy-done.35, bf16[1536,3072]{1,0:T(8,128)(2,1)} %bitcast.301), kind=kOutput, calls=%fused_computation.14 | convolution fusion | flops 4842847232 | bytes 26742784 | tf_op jit(solution)/shard_map/dot_general | solution.py:35
  249.2 11.8 %multiply_reduce_fusion = (f32[1536]{0:T(1024)}, f32[1024]{0:T(1024)S(1)}, f32[1024,1536]{1,0:T(8,128)}) fusion(f32[1024,1536]{1,0:T(8,128)} %get-tuple-element.176, f32[1024]{0:T(1024)S(1)} %get-tuple-element.230, f32[1536]{0:T(1024)S(1)} %copy-done.96, bf16[1024,1536]{1,0:T(8,128)(2,1)} %fusion.11, bf16[1536,3072]{1,0:T(8,128)(2,1)} %bitcast.302), kind=kOutput, calls=%fused_computation.9 | convolution fusion | flops 4841272832 | bytes 20467712 | tf_op jit(solution)/shard_map/td,dc->tc/dot_general | solution.py:656
  261.1 7.5 %convolution_convert_fusion = bf16[1536,1536]{1,0:T(8,128)(2,1)} fusion(bf16[1024,1536]{1,0:T(8,128)(2,1)S(1)} %copy-done.36, f32[1024,1536]{1,0:T(8,128)S(1)} %copy-done.19, f32[1536]{0:T(1024)S(1)} %copy-done.96, f32[1024]{0:T(1024)S(1)} %get-tuple-element.230), kind=kOutput, calls=%fused_computation | convolution fusion | flops 4838916096 | bytes 14166016 | tf_op jit(solution)/shard_map/td,tc->dc/dot_general | solution.py:653
  271.0 13.0 %multiply_convert_fusion = (bf16[1024,1536]{1,0:T(8,128)(2,1)S(1)}, f32[1024,1536]{1,0:T(8,128)}) fusion(f32[1024,1536]{1,0:T(8,128)} %get-tuple-element.246, f32[1024,1536]{1,0:T(8,128)} %get-tuple-element.46, f32[1024]{0:T(1024)S(1)} %broadcast_multiply_fusion.5, f32[1024,1536]{1,0:T(8,128)} %get-tuple-element.176, f32[1024,1536]{1,0:T(8,128)} %get-tuple-element.247, ...), kind=kLoop, calls=%fused_computation.10 | loop fusion | flops 26738688 | bytes 34621440 | tf_op jit(solution)/shard_map/convert_element_type | solution.py:667
  284.0 6.8 %convolution_convert_fusion.1 = bf16[1536,1536]{1,0:T(8,128)(2,1)} fusion(bf16[1024,1536]{1,0:T(8,128)(2,1)S(1)} %copy-done.35, bf16[1024,1536]{1,0:T(8,128)(2,1)S(1)} %get-tuple-element.59), kind=kOutput, calls=%fused_computation.1 | convolution fusion | flops 4834197504 | bytes 11010048 | tf_op jit(solution)/shard_map/td,tc->dc/dot_general | solution.py:669
  290.9 58.0 %ssd_backward.1 = (bf16[1024,1536]{1,0:T(8,128)(2,1)}, f32[1024,128]{1,0:T(8,128)}, f32[1024,128]{1,0:T(8,128)}, f32[1024,128]{1,0:T(8,128)}, f32[3,1024,128]{2,...) custom-call(f32[1024,1536]{1,0:T(8,128)} %slice.246.xr, f32[4,1536]{1,0:T(4,128)} %taps.3, ...), custom_call_target="tpu_custom_call" | custom-call | flops 58384711680 | bytes 25165824 | tf_op jit(solution)/shard_map/ssd_backward/pallas_call | solution.py:343
  351.7 11.0 %fusion.3 = f32[1024,1536]{1,0:T(8,128)} fusion(bf16[1536,3072]{1,0:T(8,128)(2,1)} %bitcast.303, f32[1024,1536]{1,0:T(8,128)} %get-tuple-element.176, f32[1536]{0:T(1024)S(1)} %copy-done.96, f32[1024]{0:T(1024)S(1)} %get-tuple-element.230), kind=kOutput, calls=%fused_computation.26 | convolution fusion | flops 4836556800 | bytes 17311744 | tf_op jit(solution)/shard_map/tc,dc->td/dot_general | solution.py:645
  369.3 2.6 slice_bitcast_fusion
  377.0 3.8 constant_dynamic-slice_fusion.13
  389.4 2.7 copy.436
  402.7 2.5 fusion.73
  413.6 5.7 concatenate.178
  419.4 11.3 %convolution_convert_fusion.2 = bf16[1536,1920]{1,0:T(8,128)(2,1)} fusion(bf16[1024,1536]{1,0:T(8,128)(2,1)} %fusion.13, bf16[1024,1920]{1,0:T(8,128)(2,1)} %concatenate.178), kind=kOutput, calls=%fused_computation.2 | convolution fusion | flops 6042746880 | bytes 12976128 | tf_op jit(solution)/shard_map/td,tc->dc/dot_general | solution.py:716
  432.7 5.7 concatenate.179
  438.4 10.1 %fusion.84 = f32[1024,1536]{1,0:T(8,128)S(1)} fusion(bf16[1024,1920]{1,0:T(8,128)(2,1)} %concatenate.179, bf16[1536,1920]{1,0:T(8,128)(2,1)} %bitcast.309), kind=kOutput, calls=%fused_computation.319 | convolution fusion | flops 6039797760 | bytes 16121856 | tf_op jit(solution)/shard_map/dot_general | solution.py:39
  448.5 7.3 %convolution_add_fusion = f32[1024,1536]{1,0:T(8,128)S(1)} fusion(f32[1024,1536]{1,0:T(8,128)S(1)} %fusion.84, bf16[1024,1536]{1,0:T(8,128)(2,1)S(1)} %copy-done.33, bf16[1536,3072]{1,0:T(8,128)(2,1)} %bitcast.304), kind=kOutput, calls=%fused_computation.23 | convolution fusion | flops 4833411072 | bytes 20447232 | tf_op jit(solution)/shard_map/dot_general | solution.py:39
  471.5 14.2 %collective-permute-done.50 = bf16[2,2,2,96,640]{4,3,0,1,2:T(8,128)(2,1)S(1)} collective-permute-done((bf16[2,2,2,96,640]{4,3,0,1,2:T(8,128)(2,1)S(1)}, bf16[2,2,2,96,640]{4,3,0,1,2:T(8,128)(2,1)S(1)}, u32[]{:S(2)}, u32[]{:S(2)}) %collective-permute-start.50) | collective-permute-done | bytes 983072 | tf_op jit(solution)/shard_map/ppermute | solution.py:433
  486.5 2.5 collective-permute-done.46
  490.1 2.9 collective-permute-done.42
  494.1 14.9 %collective-permute-done.55 = bf16[2,2,96,1024]{3,2,0,1:T(8,128)(2,1)S(1)} collective-permute-done((bf16[2,2,96,1024]{3,2,0,1:T(8,128)(2,1)S(1)}, bf16[2,2,96,1024]{3,2,0,1:T(8,128)(2,1)S(1)}, u32[]{:S(2)}, u32[]{:S(2)}) %collective-permute-start.55) | collective-permute-done | bytes 786464 | tf_op jit(solution)/shard_map/ppermute | solution.py:433
  512.4 9.1 %collective-permute-done.51 = bf16[2,2,96,640]{3,2,0,1:T(8,128)(2,1)S(1)} collective-permute-done((bf16[2,2,96,640]{3,2,0,1:T(8,128)(2,1)S(1)}, bf16[2,2,96,640]{3,2,0,1:T(8,128)(2,1)S(1)}, u32[]{:S(2)}, u32[]{:S(2)}) %collective-permute-start.51) | collective-permute-done | bytes 491552 | tf_op jit(solution)/shard_map/ppermute | solution.py:433
  526.4 4.7 collective-permute-done.56
  532.2 10.3 %collective-permute-done.36 = bf16[2,96,1024]{2,1,0:T(8,128)(2,1)S(1)} collective-permute-done((bf16[2,96,1024]{2,1,0:T(8,128)(2,1)S(1)}, bf16[2,96,1024]{2,1,0:T(8,128)(2,1)S(1)}, u32[]{:S(2)}, u32[]{:S(2)}) %collective-permute-start.36) | collective-permute-done | bytes 393248 | tf_op jit(solution)/shard_map/ppermute | solution.py:433
  545.0 2.9 collective-permute-start.57
  548.0 11.7 %collective-permute-done.48 = bf16[2,96,640]{2,1,0:T(8,128)(2,1)S(1)} collective-permute-done((bf16[2,96,640]{2,1,0:T(8,128)(2,1)S(1)}, bf16[2,96,640]{2,1,0:T(8,128)(2,1)S(1)}, u32[]{:S(2)}, u32[]{:S(2)}) %collective-permute-start.48) | collective-permute-done | bytes 245792 | tf_op jit(solution)/shard_map/ppermute | solution.py:433
  562.5 4.4 collective-permute-done.53
  569.2 2.9 collective-permute-done.49
  573.2 7.9 %collective-permute-done.45 = bf16[96,640]{1,0:T(8,128)(2,1)S(1)} collective-permute-done((bf16[96,640]{1,0:T(8,128)(2,1)}, bf16[96,640]{1,0:T(8,128)(2,1)S(1)}, u32[]{:S(2)}, u32[]{:S(2)}) %collective-permute-start.45) | collective-permute-done | bytes 122912 | tf_op jit(solution)/shard_map/ppermute | solution.py:433
  584.0 5.6 fusion.22
  599.9 3.3 collective-permute-start.32
  607.1 5.0 fusion.9
  (566 shorter events, 227.6 us)
Async XLA Ops:
  5.0 101.5 %collective-permute-start = (bf16[512,1536]{1,0:T(8,128)(2,1)S(1)}, bf16[512,1536]{1,0:T(8,128)(2,1)}, u32[]{:S(2)}, u32[]{:S(2)}) collective-permute-start(bf16[512,1536]{1,0:T(8,128)(2,1)S(1)} %fusion.16), channel_id=1, source_target_pairs={{0,1},{1,0},{2,3},{3,2},{4,5},{5,4},{6,7},{7,6},{8,9},{9,8},{10,11... | collective-permute-start | bytes 4718600 | tf_op jit(solution)/shard_map/ppermute | solution.py:409
  7.9 40.4 %collective-permute-start.1 = (bf16[1,96,640]{2,1,0:T(8,128)(2,1)}, bf16[1,96,640]{2,1,0:T(8,128)(2,1)}, u32[]{:S(2)}, u32[]{:S(2)}) collective-permute-start(bf16[1,96,640]{2,1,0:T(8,128)(2,1)} %get-tuple-element.220), channel_id=1, source_target_pairs={{0,16},{2,18},{4,20},{6,22},{8,24},{10,26},{12,28},{14,30},{16,0},... | collective-permute-start | bytes 368648 | tf_op jit(solution)/shard_map/ppermute | solution.py:433
  11.5 38.4 %collective-permute-start.5 = (bf16[1,96,640]{2,1,0:T(8,128)(2,1)}, bf16[1,96,640]{2,1,0:T(8,128)(2,1)}, u32[]{:S(2)}, u32[]{:S(2)}) collective-permute-start(bf16[1,96,640]{2,1,0:T(8,128)(2,1)} %get-tuple-element.219), channel_id=1, source_target_pairs={{0,2},{2,0},{4,6},{6,4},{8,10},{10,8},{12,14},{14,12},{16,18},{18,... | collective-permute-start | bytes 368648 | tf_op jit(solution)/shard_map/ppermute | solution.py:433
  16.3 34.8 %collective-permute-start.9 = (bf16[1,96,640]{2,1,0:T(8,128)(2,1)S(1)}, bf16[1,96,640]{2,1,0:T(8,128)(2,1)}, u32[]{:S(2)}, u32[]{:S(2)}) collective-permute-start(bf16[1,96,640]{2,1,0:T(8,128)(2,1)S(1)} %slice_bitcast_fusion.5), channel_id=1, source_target_pairs={{0,16},{2,18},{4,20},{6,22},{8,24},{10,26},{12,28},{14,30},{16,0},... | collective-permute-start | bytes 368648 | tf_op jit(solution)/shard_map/ppermute | solution.py:433
  18.5 35.4 %collective-permute-start.13 = (bf16[1,96,1024]{2,1,0:T(8,128)(2,1)}, bf16[1,96,1024]{2,1,0:T(8,128)(2,1)}, u32[]{:S(2)}, u32[]{:S(2)}) collective-permute-start(bf16[1,96,1024]{2,1,0:T(8,128)(2,1)} %get-tuple-element.218), channel_id=1, source_target_pairs={{0,16},{2,18},{4,20},{6,22},{8,24},{10,26},{12,28},{14,30},{16,0},... | collective-permute-start | bytes 589832 | tf_op jit(solution)/shard_map/ppermute | solution.py:433
  50.0 13.1 %collective-permute-start.17 = (bf16[1,96,1024]{2,1,0:T(8,128)(2,1)S(1)}, bf16[1,96,1024]{2,1,0:T(8,128)(2,1)S(1)}, u32[]{:S(2)}, u32[]{:S(2)}) collective-permute-start(bf16[1,96,1024]{2,1,0:T(8,128)(2,1)S(1)} %get-tuple-element.216), channel_id=1, source_target_pairs={{0,16},{2,18},{4,20},{6,22},{8,24},{10,26},{12,28},{14,30},{16,0},... | collective-permute-start | bytes 589832 | tf_op jit(solution)/shard_map/ppermute | solution.py:433
  51.1 14.2 %collective-permute-start.2 = (bf16[2,96,640]{2,1,0:T(8,128)(2,1)S(1)}, bf16[2,96,640]{2,1,0:T(8,128)(2,1)S(1)}, u32[]{:S(2)}, u32[]{:S(2)}) collective-permute-start(bf16[2,96,640]{2,1,0:T(8,128)(2,1)S(1)} %pad_maximum_fusion.20), channel_id=1, source_target_pairs={{0,8},{2,10},{4,12},{6,14},{8,0},{10,2},{12,4},{14,6},{16,24},{18,... | collective-permute-start | bytes 737288 | tf_op jit(solution)/shard_map/ppermute | solution.py:433
  54.0 18.9 %collective-permute-start.6 = (bf16[2,96,640]{2,1,0:T(8,128)(2,1)S(1)}, bf16[2,96,640]{2,1,0:T(8,128)(2,1)S(1)}, u32[]{:S(2)}, u32[]{:S(2)}) collective-permute-start(bf16[2,96,640]{2,1,0:T(8,128)(2,1)S(1)} %pad_maximum_fusion.21), channel_id=1, source_target_pairs={{0,16},{2,18},{4,20},{6,22},{8,24},{10,26},{12,28},{14,30},{16,0},... | collective-permute-start | bytes 737288 | tf_op jit(solution)/shard_map/ppermute | solution.py:433
  57.7 23.4 %collective-permute-start.14 = (bf16[2,96,1024]{2,1,0:T(8,128)(2,1)S(1)}, bf16[2,96,1024]{2,1,0:T(8,128)(2,1)S(1)}, u32[]{:S(2)}, u32[]{:S(2)}) collective-permute-start(bf16[2,96,1024]{2,1,0:T(8,128)(2,1)S(1)} %pad_maximum_fusion.17), channel_id=1, source_target_pairs={{0,8},{2,10},{4,12},{6,14},{8,0},{10,2},{12,4},{14,6},{16,24},{18,... | collective-permute-start | bytes 1179656 | tf_op jit(solution)/shard_map/ppermute | solution.py:433
  63.1 10.8 %collective-permute-start.10 = (bf16[2,96,640]{2,1,0:T(8,128)(2,1)S(1)}, bf16[2,96,640]{2,1,0:T(8,128)(2,1)S(1)}, u32[]{:S(2)}, u32[]{:S(2)}) collective-permute-start(bf16[2,96,640]{2,1,0:T(8,128)(2,1)S(1)} %pad_maximum_fusion.22), channel_id=1, source_target_pairs={{0,4},{2,6},{4,0},{6,2},{8,12},{10,14},{12,8},{14,10},{16,20},{18,... | collective-permute-start | bytes 737288 | tf_op jit(solution)/shard_map/ppermute | solution.py:433
  65.2 23.4 %collective-permute-start.16 = (bf16[2,96,1024]{2,1,0:T(8,128)(2,1)S(1)}, bf16[2,96,1024]{2,1,0:T(8,128)(2,1)S(1)}, u32[]{:S(2)}, u32[]{:S(2)}) collective-permute-start(bf16[2,96,1024]{2,1,0:T(8,128)(2,1)S(1)} %pad_maximum_fusion.18), channel_id=1, source_target_pairs={{0,16},{2,18},{4,20},{6,22},{8,24},{10,26},{12,28},{14,30},{16,0},... | collective-permute-start | bytes 1179656 | tf_op jit(solution)/shard_map/ppermute | solution.py:433
  72.8 40.9 %collective-permute-start.26 = (bf16[512,1536]{1,0:T(8,128)(2,1)S(1)}, bf16[512,1536]{1,0:T(8,128)(2,1)S(1)}, u32[]{:S(2)}, u32[]{:S(2)}) collective-permute-start(bf16[512,1536]{1,0:T(8,128)(2,1)S(1)} %copy-done.15), channel_id=1, source_target_pairs={{0,1},{1,0},{2,3},{3,2},{4,5},{5,4},{6,7},{7,6},{8,9},{9,8},{10,11... | collective-permute-start | bytes 4718600 | tf_op jit(solution)/shard_map/ppermute | solution.py:409
  73.9 19.2 %collective-permute-start.3 = (bf16[4,96,640]{2,1,0:T(8,128)(2,1)S(1)}, bf16[4,96,640]{2,1,0:T(8,128)(2,1)S(1)}, u32[]{:S(2)}, u32[]{:S(2)}) collective-permute-start(bf16[4,96,640]{2,1,0:T(8,128)(2,1)S(1)} %pad_maximum_fusion.14), channel_id=1, source_target_pairs={{0,4},{2,6},{4,0},{6,2},{8,12},{10,14},{12,8},{14,10},{16,20},{18,... | collective-permute-start | bytes 1474568 | tf_op jit(solution)/shard_map/ppermute | solution.py:433
  81.1 15.4 %collective-permute-start.7 = (bf16[4,96,640]{2,1,0:T(8,128)(2,1)S(1)}, bf16[4,96,640]{2,1,0:T(8,128)(2,1)S(1)}, u32[]{:S(2)}, u32[]{:S(2)}) collective-permute-start(bf16[4,96,640]{2,1,0:T(8,128)(2,1)S(1)} %pad_maximum_fusion.15), channel_id=1, source_target_pairs={{0,8},{2,10},{4,12},{6,14},{8,0},{10,2},{12,4},{14,6},{16,24},{18,... | collective-permute-start | bytes 1474568 | tf_op jit(solution)/shard_map/ppermute | solution.py:433
  88.6 14.1 %collective-permute-start.11 = (bf16[4,96,640]{2,1,0:T(8,128)(2,1)S(1)}, bf16[4,96,640]{2,1,0:T(8,128)(2,1)S(1)}, u32[]{:S(2)}, u32[]{:S(2)}) collective-permute-start(bf16[4,96,640]{2,1,0:T(8,128)(2,1)S(1)} %pad_maximum_fusion.16), channel_id=1, source_target_pairs={{0,2},{2,0},{4,6},{6,4},{8,10},{10,8},{12,14},{14,12},{16,18},{18,... | collective-permute-start | bytes 1474568 | tf_op jit(solution)/shard_map/ppermute | solution.py:433
  93.1 12.2 %collective-permute-start.18 = (bf16[2,96,1024]{2,1,0:T(8,128)(2,1)S(1)}, bf16[2,96,1024]{2,1,0:T(8,128)(2,1)S(1)}, u32[]{:S(2)}, u32[]{:S(2)}) collective-permute-start(bf16[2,96,1024]{2,1,0:T(8,128)(2,1)S(1)} %pad_maximum_fusion.19), channel_id=1, source_target_pairs={{0,4},{2,6},{4,0},{6,2},{8,12},{10,14},{12,8},{14,10},{16,20},{18,... | collective-permute-start | bytes 1179656 | tf_op jit(solution)/shard_map/ppermute | solution.py:433
  96.5 25.2 %collective-permute-start.4 = (bf16[8,96,640]{2,1,0:T(8,128)(2,1)S(1)}, bf16[8,96,640]{2,1,0:T(8,128)(2,1)S(1)}, u32[]{:S(2)}, u32[]{:S(2)}) collective-permute-start(bf16[8,96,640]{2,1,0:T(8,128)(2,1)S(1)} %pad_maximum_fusion.4.refs_0_), channel_id=1, source_target_pairs={{0,2},{2,0},{4,6},{6,4},{8,10},{10,8},{12,14},{14,12},{16,18},{18,... | collective-permute-start | bytes 2949128 | tf_op jit(solution)/shard_map/ppermute | solution.py:433
  102.7 21.1 %collective-permute-start.8 = (bf16[8,96,640]{2,1,0:T(8,128)(2,1)S(1)}, bf16[8,96,640]{2,1,0:T(8,128)(2,1)S(1)}, u32[]{:S(2)}, u32[]{:S(2)}) collective-permute-start(bf16[8,96,640]{2,1,0:T(8,128)(2,1)S(1)} %pad_maximum_fusion.5.refs_2_), channel_id=1, source_target_pairs={{0,4},{2,6},{4,0},{6,2},{8,12},{10,14},{12,8},{14,10},{16,20},{18,... | collective-permute-start | bytes 2949128 | tf_op jit(solution)/shard_map/ppermute | solution.py:433
  105.3 19.5 %collective-permute-start.12 = (bf16[8,96,640]{2,1,0:T(8,128)(2,1)S(1)}, bf16[8,96,640]{2,1,0:T(8,128)(2,1)}, u32[]{:S(2)}, u32[]{:S(2)}) collective-permute-start(bf16[8,96,640]{2,1,0:T(8,128)(2,1)S(1)} %pad_maximum_fusion.6.refs_4_), channel_id=1, source_target_pairs={{0,8},{2,10},{4,12},{6,14},{8,0},{10,2},{12,4},{14,6},{16,24},{18,... | collective-permute-start | bytes 2949128 | tf_op jit(solution)/shard_map/ppermute | solution.py:433
  157.6 29.3 %collective-permute-start.19 = (bf16[4,96,1024]{2,1,0:T(8,128)(2,1)}, bf16[4,96,1024]{2,1,0:T(8,128)(2,1)}, u32[]{:S(2)}, u32[]{:S(2)}) collective-permute-start(bf16[4,96,1024]{2,1,0:T(8,128)(2,1)} %pad_maximum_fusion.7), channel_id=1, source_target_pairs={{0,4},{2,6},{4,0},{6,2},{8,12},{10,14},{12,8},{14,10},{16,20},{18,... | collective-permute-start | bytes 2359304 | tf_op jit(solution)/shard_map/ppermute | solution.py:433
  159.1 31.1 %collective-permute-start.21 = (bf16[4,96,1024]{2,1,0:T(8,128)(2,1)}, bf16[4,96,1024]{2,1,0:T(8,128)(2,1)}, u32[]{:S(2)}, u32[]{:S(2)}) collective-permute-start(bf16[4,96,1024]{2,1,0:T(8,128)(2,1)} %pad_maximum_fusion.8), channel_id=1, source_target_pairs={{0,8},{2,10},{4,12},{6,14},{8,0},{10,2},{12,4},{14,6},{16,24},{18,... | collective-permute-start | bytes 2359304 | tf_op jit(solution)/shard_map/ppermute | solution.py:433
  159.1 33.2 %collective-permute-start.23 = (bf16[4,96,1024]{2,1,0:T(8,128)(2,1)}, bf16[4,96,1024]{2,1,0:T(8,128)(2,1)}, u32[]{:S(2)}, u32[]{:S(2)}) collective-permute-start(bf16[4,96,1024]{2,1,0:T(8,128)(2,1)} %pad_maximum_fusion.9), channel_id=1, source_target_pairs={{0,2},{2,0},{4,6},{6,4},{8,10},{10,8},{12,14},{14,12},{16,18},{18,... | collective-permute-start | bytes 2359304 | tf_op jit(solution)/shard_map/ppermute | solution.py:433
  189.0 33.8 %collective-permute-start.20 = (bf16[8,96,1024]{2,1,0:T(8,128)(2,1)}, bf16[8,96,1024]{2,1,0:T(8,128)(2,1)}, u32[]{:S(2)}, u32[]{:S(2)}) collective-permute-start(bf16[8,96,1024]{2,1,0:T(8,128)(2,1)} %constant_dynamic-update-slice_fusion.refs_0_), channel_id=1, source_target_pairs={{0,2},{2,0},{4,6},{6,4},{8,10},{10,8},{12,14},{14,12},{16,18},{18,... | collective-permute-start | bytes 4718600 | tf_op jit(solution)/shard_map/ppermute | solution.py:433
  191.4 32.7 %collective-permute-start.22 = (bf16[8,96,1024]{2,1,0:T(8,128)(2,1)S(1)}, bf16[8,96,1024]{2,1,0:T(8,128)(2,1)}, u32[]{:S(2)}, u32[]{:S(2)}) collective-permute-start(bf16[8,96,1024]{2,1,0:T(8,128)(2,1)S(1)} %constant_dynamic-update-slice_fusion.2.refs_2_), channel_id=1, source_target_pairs={{0,4},{2,6},{4,0},{6,2},{8,12},{10,14},{12,8},{14,10},{16,20},{18,... | collective-permute-start | bytes 4718600 | tf_op jit(solution)/shard_map/ppermute | solution.py:433
  193.5 32.3 %collective-permute-start.24 = (bf16[8,96,1024]{2,1,0:T(8,128)(2,1)S(1)}, bf16[8,96,1024]{2,1,0:T(8,128)(2,1)}, u32[]{:S(2)}, u32[]{:S(2)}) collective-permute-start(bf16[8,96,1024]{2,1,0:T(8,128)(2,1)S(1)} %constant_dynamic-update-slice_fusion.4.refs_4_), channel_id=1, source_target_pairs={{0,8},{2,10},{4,12},{6,14},{8,0},{10,2},{12,4},{14,6},{16,24},{18,... | collective-permute-start | bytes 4718600 | tf_op jit(solution)/shard_map/ppermute | solution.py:433
  369.1 36.1 %collective-permute-start.27 = (f32[1024,256]{0,1:T(8,128)}, f32[1024,256]{0,1:T(8,128)}, u32[]{:S(2)}, u32[]{:S(2)}) collective-permute-start(f32[1024,256]{0,1:T(8,128)} %pad_maximum_fusion.3), channel_id=1, source_target_pairs={{0,1},{1,0},{2,3},{3,2},{4,5},{5,4},{6,7},{7,6},{8,9},{9,8},{10,11... | collective-permute-start | bytes 3145736 | tf_op jit(solution)/shard_map/ppermute | solution.py:409
  380.7 226.4 %collective-permute-start.25 = (f32[512,1536]{1,0:T(8,128)}, f32[512,1536]{1,0:T(8,128)}, u32[]{:S(2)}, u32[]{:S(2)}) collective-permute-start(f32[512,1536]{1,0:T(8,128)} %constant_dynamic-slice_fusion.13), channel_id=1, source_target_pairs={{0,1},{1,0},{2,3},{3,2},{4,5},{5,4},{6,7},{7,6},{8,9},{9,8},{10,11... | collective-permute-start | bytes 9437192 | tf_op jit(solution)/shard_map/ppermute | solution.py:409
  392.1 69.4 %collective-permute-start.54 = (bf16[2,2,2,96,1024]{4,3,0,1,2:T(8,128)(2,1)}, bf16[2,2,2,96,1024]{4,3,0,1,2:T(8,128)(2,1)}, u32[]{:S(2)}, u32[]{:S(2)}) collective-permute-start(bf16[2,2,2,96,1024]{4,3,0,1,2:T(8,128)(2,1)} %bitcast.288), channel_id=1, source_target_pairs={{0,8},{2,10},{4,12},{6,14},{8,0},{10,2},{12,4},{14,6},{16,24},{18,... | collective-permute-start | bytes 4718600 | tf_op jit(solution)/shard_map/ppermute | solution.py:433
  397.0 67.7 %collective-permute-start.38 = (bf16[2,2,2,96,1024]{4,3,2,0,1:T(8,128)(2,1)}, bf16[2,2,2,96,1024]{4,3,2,0,1:T(8,128)(2,1)}, u32[]{:S(2)}, u32[]{:S(2)}) collective-permute-start(bf16[2,2,2,96,1024]{4,3,2,0,1:T(8,128)(2,1)} %bitcast.289), channel_id=1, source_target_pairs={{0,4},{2,6},{4,0},{6,2},{8,12},{10,14},{12,8},{14,10},{16,20},{18,... | collective-permute-start | bytes 4718600 | tf_op jit(solution)/shard_map/ppermute | solution.py:433
  401.1 67.1 %collective-permute-start.34 = (bf16[2,2,2,96,1024]{4,3,0,1,2:T(8,128)(2,1)}, bf16[2,2,2,96,1024]{4,3,0,1,2:T(8,128)(2,1)}, u32[]{:S(2)}, u32[]{:S(2)}) collective-permute-start(bf16[2,2,2,96,1024]{4,3,0,1,2:T(8,128)(2,1)} %bitcast.290), channel_id=1, source_target_pairs={{0,2},{2,0},{4,6},{6,4},{8,10},{10,8},{12,14},{14,12},{16,18},{18,... | collective-permute-start | bytes 4718600 | tf_op jit(solution)/shard_map/ppermute | solution.py:433
  459.4 124.6 %collective-permute-start.28 = (f32[512,1536]{1,0:T(8,128)}, f32[512,1536]{1,0:T(8,128)}, u32[]{:S(2)}, u32[]{:S(2)}) collective-permute-start(f32[512,1536]{1,0:T(8,128)} %constant_dynamic-slice_fusion.12), channel_id=1, source_target_pairs={{0,1},{1,0},{2,3},{3,2},{4,5},{5,4},{6,7},{7,6},{8,9},{9,8},{10,11... | collective-permute-start | bytes 9437192 | tf_op jit(solution)/shard_map/ppermute | solution.py:409
  461.5 24.2 %collective-permute-start.50 = (bf16[2,2,2,96,640]{4,3,0,1,2:T(8,128)(2,1)S(1)}, bf16[2,2,2,96,640]{4,3,0,1,2:T(8,128)(2,1)S(1)}, u32[]{:S(2)}, u32[]{:S(2)}) collective-permute-start(bf16[2,2,2,96,640]{4,3,0,1,2:T(8,128)(2,1)S(1)} %bitcast.331), channel_id=1, source_target_pairs={{0,8},{2,10},{4,12},{6,14},{8,0},{10,2},{12,4},{14,6},{16,24},{18,... | collective-permute-start | bytes 2949128 | tf_op jit(solution)/shard_map/ppermute | solution.py:433
  464.7 24.2 %collective-permute-start.46 = (bf16[2,2,2,96,640]{4,3,2,0,1:T(8,128)(2,1)S(1)}, bf16[2,2,2,96,640]{4,3,2,0,1:T(8,128)(2,1)S(1)}, u32[]{:S(2)}, u32[]{:S(2)}) collective-permute-start(bf16[2,2,2,96,640]{4,3,2,0,1:T(8,128)(2,1)S(1)} %bitcast.330), channel_id=1, source_target_pairs={{0,4},{2,6},{4,0},{6,2},{8,12},{10,14},{12,8},{14,10},{16,20},{18,... | collective-permute-start | bytes 2949128 | tf_op jit(solution)/shard_map/ppermute | solution.py:433
  468.2 24.7 %collective-permute-start.42 = (bf16[2,2,2,96,640]{4,3,0,1,2:T(8,128)(2,1)S(1)}, bf16[2,2,2,96,640]{4,3,0,1,2:T(8,128)(2,1)S(1)}, u32[]{:S(2)}, u32[]{:S(2)}) collective-permute-start(bf16[2,2,2,96,640]{4,3,0,1,2:T(8,128)(2,1)S(1)} %bitcast.329), channel_id=1, source_target_pairs={{0,2},{2,0},{4,6},{6,4},{8,10},{10,8},{12,14},{14,12},{16,18},{18,... | collective-permute-start | bytes 2949128 | tf_op jit(solution)/shard_map/ppermute | solution.py:433
  485.7 23.3 %collective-permute-start.55 = (bf16[2,2,96,1024]{3,2,0,1:T(8,128)(2,1)S(1)}, bf16[2,2,96,1024]{3,2,0,1:T(8,128)(2,1)S(1)}, u32[]{:S(2)}, u32[]{:S(2)}) collective-permute-start(bf16[2,2,96,1024]{3,2,0,1:T(8,128)(2,1)S(1)} %fusion.31), channel_id=1, source_target_pairs={{0,2},{2,0},{4,6},{6,4},{8,10},{10,8},{12,14},{14,12},{16,18},{18,... | collective-permute-start | bytes 2359304 | tf_op jit(solution)/shard_map/ppermute | solution.py:433
  488.9 21.0 %collective-permute-start.39 = (bf16[2,2,96,1024]{3,2,1,0:T(8,128)(2,1)S(1)}, bf16[2,2,96,1024]{3,2,1,0:T(8,128)(2,1)S(1)}, u32[]{:S(2)}, u32[]{:S(2)}) collective-permute-start(bf16[2,2,96,1024]{3,2,1,0:T(8,128)(2,1)S(1)} %fusion.30), channel_id=1, source_target_pairs={{0,8},{2,10},{4,12},{6,14},{8,0},{10,2},{12,4},{14,6},{16,24},{18,... | collective-permute-start | bytes 2359304 | tf_op jit(solution)/shard_map/ppermute | solution.py:433
  492.9 18.1 %collective-permute-start.35 = (bf16[2,2,96,1024]{3,2,0,1:T(8,128)(2,1)S(1)}, bf16[2,2,96,1024]{3,2,0,1:T(8,128)(2,1)S(1)}, u32[]{:S(2)}, u32[]{:S(2)}) collective-permute-start(bf16[2,2,96,1024]{3,2,0,1:T(8,128)(2,1)S(1)} %fusion.29), channel_id=1, source_target_pairs={{0,4},{2,6},{4,0},{6,2},{8,12},{10,14},{12,8},{14,10},{16,20},{18,... | collective-permute-start | bytes 2359304 | tf_op jit(solution)/shard_map/ppermute | solution.py:433
  509.0 12.5 %collective-permute-start.51 = (bf16[2,2,96,640]{3,2,0,1:T(8,128)(2,1)S(1)}, bf16[2,2,96,640]{3,2,0,1:T(8,128)(2,1)S(1)}, u32[]{:S(2)}, u32[]{:S(2)}) collective-permute-start(bf16[2,2,96,640]{3,2,0,1:T(8,128)(2,1)S(1)} %fusion.40), channel_id=1, source_target_pairs={{0,2},{2,0},{4,6},{6,4},{8,10},{10,8},{12,14},{14,12},{16,18},{18,... | collective-permute-start | bytes 1474568 | tf_op jit(solution)/shard_map/ppermute | solution.py:433
  510.0 12.5 %collective-permute-start.47 = (bf16[2,2,96,640]{3,2,1,0:T(8,128)(2,1)S(1)}, bf16[2,2,96,640]{3,2,1,0:T(8,128)(2,1)S(1)}, u32[]{:S(2)}, u32[]{:S(2)}) collective-permute-start(bf16[2,2,96,640]{3,2,1,0:T(8,128)(2,1)S(1)} %fusion.39), channel_id=1, source_target_pairs={{0,8},{2,10},{4,12},{6,14},{8,0},{10,2},{12,4},{14,6},{16,24},{18,... | collective-permute-start | bytes 1474568 | tf_op jit(solution)/shard_map/ppermute | solution.py:433
  511.0 13.6 %collective-permute-start.43 = (bf16[2,2,96,640]{3,2,0,1:T(8,128)(2,1)S(1)}, bf16[2,2,96,640]{3,2,0,1:T(8,128)(2,1)S(1)}, u32[]{:S(2)}, u32[]{:S(2)}) collective-permute-start(bf16[2,2,96,640]{3,2,0,1:T(8,128)(2,1)S(1)} %fusion.38), channel_id=1, source_target_pairs={{0,4},{2,6},{4,0},{6,2},{8,12},{10,14},{12,8},{14,10},{16,20},{18,... | collective-permute-start | bytes 1474568 | tf_op jit(solution)/shard_map/ppermute | solution.py:433
  522.5 20.1 %collective-permute-start.40 = (bf16[2,96,1024]{2,1,0:T(8,128)(2,1)S(1)}, bf16[2,96,1024]{2,1,0:T(8,128)(2,1)S(1)}, u32[]{:S(2)}, u32[]{:S(2)}) collective-permute-start(bf16[2,96,1024]{2,1,0:T(8,128)(2,1)S(1)} %fusion.42), channel_id=1, source_target_pairs={{0,16},{2,18},{4,20},{6,22},{8,24},{10,26},{12,28},{14,30},{16,0},... | collective-permute-start | bytes 1179656 | tf_op jit(solution)/shard_map/ppermute | solution.py:433
  524.7 17.8 %collective-permute-start.36 = (bf16[2,96,1024]{2,1,0:T(8,128)(2,1)S(1)}, bf16[2,96,1024]{2,1,0:T(8,128)(2,1)S(1)}, u32[]{:S(2)}, u32[]{:S(2)}) collective-permute-start(bf16[2,96,1024]{2,1,0:T(8,128)(2,1)S(1)} %fusion.41), channel_id=1, source_target_pairs={{0,8},{2,10},{4,12},{6,14},{8,0},{10,2},{12,4},{14,6},{16,24},{18,... | collective-permute-start | bytes 1179656 | tf_op jit(solution)/shard_map/ppermute | solution.py:433
  531.2 13.8 %collective-permute-start.52 = (bf16[2,96,640]{2,1,0:T(8,128)(2,1)S(1)}, bf16[2,96,640]{2,1,0:T(8,128)(2,1)S(1)}, u32[]{:S(2)}, u32[]{:S(2)}) collective-permute-start(bf16[2,96,640]{2,1,0:T(8,128)(2,1)S(1)} %fusion.46), channel_id=1, source_target_pairs={{0,4},{2,6},{4,0},{6,2},{8,12},{10,14},{12,8},{14,10},{16,20},{18,... | collective-permute-start | bytes 737288 | tf_op jit(solution)/shard_map/ppermute | solution.py:433
  542.4 17.3 %collective-permute-start.48 = (bf16[2,96,640]{2,1,0:T(8,128)(2,1)S(1)}, bf16[2,96,640]{2,1,0:T(8,128)(2,1)S(1)}, u32[]{:S(2)}, u32[]{:S(2)}) collective-permute-start(bf16[2,96,640]{2,1,0:T(8,128)(2,1)S(1)} %fusion.45), channel_id=1, source_target_pairs={{0,16},{2,18},{4,20},{6,22},{8,24},{10,26},{12,28},{14,30},{16,0},... | collective-permute-start | bytes 737288 | tf_op jit(solution)/shard_map/ppermute | solution.py:433
  542.6 18.5 %collective-permute-start.44 = (bf16[2,96,640]{2,1,0:T(8,128)(2,1)S(1)}, bf16[2,96,640]{2,1,0:T(8,128)(2,1)S(1)}, u32[]{:S(2)}, u32[]{:S(2)}) collective-permute-start(bf16[2,96,640]{2,1,0:T(8,128)(2,1)S(1)} %fusion.44), channel_id=1, source_target_pairs={{0,8},{2,10},{4,12},{6,14},{8,0},{10,2},{12,4},{14,6},{16,24},{18,... | collective-permute-start | bytes 737288 | tf_op jit(solution)/shard_map/ppermute | solution.py:433
  545.0 37.9 %collective-permute-start.57 = (bf16[96,1024]{1,0:T(8,128)(2,1)}, bf16[96,1024]{1,0:T(8,128)(2,1)}, u32[]{:S(2)}, u32[]{:S(2)}) collective-permute-start(bf16[96,1024]{1,0:T(8,128)(2,1)} %fusion.49), channel_id=1, source_target_pairs={{0,16},{2,18},{4,20},{6,22},{8,24},{10,26},{12,28},{14,30},{16,0},... | collective-permute-start | bytes 589832 | tf_op jit(solution)/shard_map/ppermute | solution.py:433
  559.7 29.9 %collective-permute-start.41 = (bf16[96,1024]{1,0:T(8,128)(2,1)}, bf16[96,1024]{1,0:T(8,128)(2,1)}, u32[]{:S(2)}, u32[]{:S(2)}) collective-permute-start(bf16[96,1024]{1,0:T(8,128)(2,1)} %fusion.48), channel_id=1, source_target_pairs={{0,2},{2,0},{4,6},{6,4},{8,10},{10,8},{12,14},{14,12},{16,18},{18,... | collective-permute-start | bytes 589832 | tf_op jit(solution)/shard_map/ppermute | solution.py:433
  581.1 11.7 %collective-permute-start.37 = (bf16[96,1024]{1,0:T(8,128)(2,1)}, bf16[96,1024]{1,0:T(8,128)(2,1)}, u32[]{:S(2)}, u32[]{:S(2)}) collective-permute-start(bf16[96,1024]{1,0:T(8,128)(2,1)} %fusion.47), channel_id=1, source_target_pairs={{0,16},{2,18},{4,20},{6,22},{8,24},{10,26},{12,28},{14,30},{16,0},... | collective-permute-start | bytes 589832 | tf_op jit(solution)/shard_map/ppermute | solution.py:433
  (127 other events, 1545.2 us)

commit v4 on v3

--- a/solution.py
+++ b/solution.py
@@ -64,17 +64,20 @@
     y_out, states_out, state,
 ):
     width = xr.shape[1]
-    head_size = width // dt.shape[2]
+    head_size = width // HEADS_STEP
     pair_width = 2 * head_size
     chunks = xr.shape[0] // CHUNK
+    lane_count = dt.shape[1]
+    to_front = lax.rem(lane_count - pl.program_id(0) * HEADS_STEP, lane_count)
     state[...] = jnp.zeros_like(state)
 
     def chunk_body(place, unused):
         start = pl.multiple_of(place * CHUNK, CHUNK)
         rows = pl.ds(start, CHUNK)
         before = pl.ds(pl.multiple_of(jnp.maximum(start - 8, 0), 8), 8)
-        dt_cols, cum_cols = dt[0, rows, :], cumc[0, rows, :]
-        reach_cols, end_cols = reach[0, rows, :], toend[0, rows, :]
+        dt_cols, cum_cols, reach_cols, end_cols = (
+            pltpu.roll(ref[rows, :], to_front, 1) for ref in (dt, cumc, reach, toend)
+        )
         score_now, cs_now, bst_now = score[rows, :], cs[rows, :], bst[:, rows]
         lane = lax.broadcasted_iota(jnp.int32, (CHUNK, pair_width), 1)
         row_of = pl.ds(pl.multiple_of(place * 8, 8), 8)
@@ -91,14 +94,14 @@
             states_out[rows, lanes] = held_low
             halves = []
             for head in (2 * pair, 2 * pair + 1):
-                spread = cum_cols[:, head : head + 1] - cumr[0, head : head + 1, rows]
+                spread = cum_cols[:, head : head + 1] - cumr[head : head + 1, rows]
                 mixing = score_now * jnp.exp(jnp.minimum(spread, 0.0))
                 halves.append(dot(mixing.astype(BF16), xb))
             y = jnp.where(lane < head_size, halves[0], halves[1])
             y = y + spread_heads(reach_cols, pair, head_size) * dot(cs_now, held_low)
             y_out[rows, lanes] = y + skip[0:1, lanes] * x
             fresh = dot(bst_now, (xdt * spread_heads(end_cols, pair, head_size)).astype(BF16))
-            state[:, lanes] = fresh + kept[0, row_of, lanes][0:1] * held
+            state[:, lanes] = fresh + kept[row_of, lanes][0:1] * held
         return unused
 
     lax.fori_loop(0, chunks, chunk_body, 0)
@@ -107,15 +110,18 @@
 def ssd_backward_kernel(
     xr, taps, bias, skip, masks, score_t, cs, bs, cst, pick, dt, cumc, reach, toend, cumr, kept,
     states, dy,
-    dxr_out, dscore_out, dbs_out, dcs_out, cols_out, rows_out, span_out, sums_out,
+    dxr_out, dscore_out, dbs_out, dcs_out, up_out, on_out, step_out, rows_out, span_out, sums_out,
     dstate, dvalue_next,
 ):
     width = xr.shape[1]
-    head_size = width // dt.shape[2]
+    head_size = width // HEADS_STEP
     pair_width = 2 * head_size
     length = xr.shape[0]
     chunks = length // CHUNK
     count = taps.shape[0]
+    lane_count = dt.shape[1]
+    first_head = pl.program_id(0) * HEADS_STEP
+    to_front = lax.rem(lane_count - first_head, lane_count)
     dstate[...] = jnp.zeros_like(dstate)
     dvalue_next[...] = jnp.zeros_like(dvalue_next)
     sums_out[...] = jnp.zeros_like(sums_out)
@@ -125,6 +131,9 @@
         dscore_out[...] = jnp.zeros_like(dscore_out)
         dbs_out[...] = jnp.zeros_like(dbs_out)
         dcs_out[...] = jnp.zeros_like(dcs_out)
+        up_out[...] = jnp.zeros_like(up_out)
+        on_out[...] = jnp.zeros_like(on_out)
+        step_out[...] = jnp.zeros_like(step_out)
 
     def chunk_body(step, unused):
         place = chunks - 1 - step
@@ -132,15 +141,16 @@
         rows = pl.ds(start, CHUNK)
         before = pl.ds(pl.multiple_of(jnp.maximum(start - 8, 0), 8), 8)
         after = pl.ds(pl.multiple_of(jnp.minimum(start + CHUNK, length - 8), 8), 8)
-        dt_cols, cum_cols = dt[0, rows, :], cumc[0, rows, :]
-        reach_cols, end_cols = reach[0, rows, :], toend[0, rows, :]
+        dt_cols, cum_cols, reach_cols, end_cols = (
+            pltpu.roll(ref[rows, :], to_front, 1) for ref in (dt, cumc, reach, toend)
+        )
         score_now, cs_now, bs_now, cst_now = score_t[rows, :], cs[rows, :], bs[rows, :], cst[:, rows]
         lane = lax.broadcasted_iota(jnp.int32, (CHUNK, pair_width), 1)
         row_of = pl.ds(pl.multiple_of(place * 8, 8), 8)
         dscore = jnp.zeros((CHUNK, CHUNK), F32)
         dbs = jnp.zeros((CHUNK, bs_now.shape[1]), F32)
         dcs = jnp.zeros((CHUNK, bs_now.shape[1]), F32)
-        columns = jnp.zeros((CHUNK, cols_out.shape[2]), F32)
+        columns = jnp.zeros((CHUNK, lane_count), F32)
         column_lane = lax.broadcasted_iota(jnp.int32, columns.shape, 1)
         for pair in range(width // pair_width):
             lanes = slice(pair * pair_width, (pair + 1) * pair_width)
@@ -165,7 +175,7 @@
             halves = []
             for side in (0, 1):
                 head = 2 * pair + side
-                spread = cumr[0, head : head + 1, rows] - cum_cols[:, head : head + 1]
+                spread = cumr[head : head + 1, rows] - cum_cols[:, head : head + 1]
                 decay = jnp.exp(jnp.minimum(spread, 0.0))
                 weight = score_now * decay
                 own = (lane < head_size) if side == 0 else (lane >= head_size)
@@ -175,7 +185,7 @@
                 columns = columns - jnp.where(
                     column_lane == head, jnp.sum(share, axis=1, keepdims=True), 0.0
                 )
-                rows_out[0, head : head + 1, rows] = jnp.sum(share, axis=0, keepdims=True)
+                rows_out[head : head + 1, rows] = jnp.sum(share, axis=0, keepdims=True)
                 halves.append(dot(weight.astype(BF16), dyb))
             dxdt = jnp.where(lane < head_size, halves[0], halves[1]) + dxdt_end
             picked = jnp.concatenate(
@@ -188,9 +198,9 @@
             )
             columns = columns + dot(picked, pick[pair])
             dx = skip[0:1, lanes] * dy_now + dt_now * dxdt
-            kept_row = kept[0, row_of, lanes][0:1]
+            kept_row = kept[row_of, lanes][0:1]
             span_row = kept_row * jnp.sum(dheld * held_low.astype(F32), axis=0, keepdims=True)
-            span_out[0, row_of, lanes] = jnp.broadcast_to(span_row, (8, pair_width))
+            span_out[row_of, lanes] = jnp.broadcast_to(span_row, (8, pair_width))
             dstate[:, lanes] = kept_row * dheld + dot(cst_now, dyr_low)
             dvalue = dx * (gate * (1.0 + value * (1.0 - gate)))
             dxr = taps[count - 1 : count, lanes] * dvalue
@@ -213,15 +223,18 @@
         dscore_out[rows, :] += dscore
         dbs_out[rows, :] += dbs
         dcs_out[rows, :] += dcs
-        cols_out[0, rows, :] = columns
+        held_lane = (column_lane >= first_head) & (column_lane < first_head + HEADS_STEP)
+        for slot, out in enumerate((up_out, on_out, step_out)):
+            turn = lax.rem(first_head + lane_count - slot * HEADS_STEP, lane_count)
+            out[rows, :] += jnp.where(held_lane, pltpu.roll(columns, turn, 1), 0.0)
         return unused
 
     lax.fori_loop(0, chunks, chunk_body, 0)
 
 
-def chunk_terms(step_size, log_decay, segment, head_size):
+def chunk_terms(step_size, log_decay, segment, real_heads, head_size):
     length, heads = step_size.shape
-    chunks, groups = length // CHUNK, heads // HEADS_STEP
+    chunks = length // CHUNK
     parted = segment.reshape(chunks, CHUNK)
     places = jnp.arange(CHUNK)
     lower = (places[:, None] >= places[None, :]).astype(F32)
@@ -240,13 +253,9 @@
     to_end = jnp.exp(total[:, None, :] - cumulative) * at_end[:, :, None]
     kept = jnp.exp(total) * (final == last).astype(F32)[:, None]
 
-    def by_group(array):
-        return array.reshape(length, groups, HEADS_STEP).transpose(1, 0, 2)
-
-    columns = tuple(by_group(a.reshape(length, heads)) for a in (step_size, cumulative, reach, to_end))
-    cum_rows = cumulative.reshape(length, heads).T.reshape(groups, HEADS_STEP, length)
-    kept_rows = jnp.repeat(kept, head_size, axis=1).reshape(chunks, groups, -1).transpose(1, 0, 2)
-    kept_rows = jnp.repeat(kept_rows, 8, axis=1)
+    columns = (step_size, *(a.reshape(length, heads) for a in (cumulative, reach, to_end)))
+    cum_rows = columns[1].T
+    kept_rows = jnp.repeat(jnp.repeat(kept[:, :real_heads], head_size, axis=1), 8, axis=0)
     masks = jnp.stack(
         [
             jnp.broadcast_to(
@@ -264,20 +273,15 @@
     return pl.BlockSpec(array.shape, lambda g: zeros)
 
 
-def group_spec(array):
-    rest = (0,) * (array.ndim - 1)
-    return pl.BlockSpec((1,) + array.shape[1:], lambda g: (g,) + rest)
-
-
 def lanes_spec(array, width):
     return pl.BlockSpec((array.shape[0], width), lambda g: (0, g))
 
 
-def ssd_forward(xr, taps, bias, skip_row, terms, bs_low, cs_low):
+def ssd_forward(xr, taps, bias, skip_row, terms, bs_low, cs_low, head_size):
     allowed, columns, cum_rows, kept_rows, masks = terms
-    length, inner = xr.shape
-    groups = cum_rows.shape[0]
-    width = inner // groups
+    length, inner = xr.shape[0], taps.shape[1]
+    width = HEADS_STEP * head_size
+    groups = inner // width
     state_dim = bs_low.shape[1]
     chunks = length // CHUNK
     score = (
@@ -289,14 +293,14 @@
         )
         * allowed
     )
-    shared = (masks, score.reshape(length, CHUNK), cs_low, bs_low.T)
-    grouped = (*columns, cum_rows, kept_rows)
+    shared = (masks, score.reshape(length, CHUNK), cs_low, bs_low.T, *columns)
+    rows_spec = pl.BlockSpec((HEADS_STEP, length), lambda g: (g, 0))
     y, states = pl.pallas_call(
         ssd_forward_kernel,
         grid=(groups,),
         in_specs=[lanes_spec(a, width) for a in (xr, taps, bias, skip_row)]
         + [whole_spec(a) for a in shared]
-        + [group_spec(a) for a in grouped],
+        + [rows_spec, lanes_spec(kept_rows, width)],
         out_specs=[
             pl.BlockSpec((length, width), lambda g: (0, g)),
             pl.BlockSpec((chunks * state_dim, width), lambda g: (0, g)),
@@ -310,16 +314,18 @@
             flops=130 * length * inner * CHUNK, bytes_accessed=12 * length * inner, transcendentals=0
         ),
         name="ssd_forward",
-    )(xr, taps, bias, skip_row, *shared, *grouped)
+    )(xr, taps, bias, skip_row, *shared, cum_rows, kept_rows)
     return y, states, score
 
 
-def ssd_backward(xr, taps, bias, skip_row, terms, score, bs_low, cs_low, states, dy):
+def ssd_backward(
+    xr, taps, bias, skip_row, terms, score, bs_low, cs_low, states, dy, head_size
+):
     allowed, columns, cum_rows, kept_rows, masks = terms
-    length, inner = xr.shape
-    groups, heads_step = cum_rows.shape[:2]
-    width = inner // groups
-    head_size = width // heads_step
+    length, inner = xr.shape[0], taps.shape[1]
+    heads_step, heads = HEADS_STEP, columns[0].shape[1]
+    width = heads_step * head_size
+    groups = inner // width
     state_dim = bs_low.shape[1]
     chunks = length // CHUNK
     lane = jnp.arange(2 * head_size) // head_size
@@ -337,24 +343,24 @@
         ]
     )
     score_t = score.transpose(0, 2, 1).reshape(length, CHUNK)
-    shared = (masks, score_t, cs_low, bs_low, cs_low.T, pick)
-    grouped = (*columns, cum_rows, kept_rows)
+    shared = (masks, score_t, cs_low, bs_low, cs_low.T, pick, *columns)
+    rows_spec = pl.BlockSpec((heads_step, length), lambda g: (g, 0))
     fixed = pl.BlockSpec((length, CHUNK), lambda g: (0, 0))
     out = pl.pallas_call(
         ssd_backward_kernel,
         grid=(groups,),
         in_specs=[lanes_spec(a, width) for a in (xr, taps, bias, skip_row)]
         + [whole_spec(a) for a in shared]
-        + [group_spec(a) for a in grouped]
+        + [rows_spec, lanes_spec(kept_rows, width)]
         + [lanes_spec(a, width) for a in (states, dy)],
         out_specs=[
             pl.BlockSpec((length, width), lambda g: (0, g)),
             fixed,
             pl.BlockSpec((length, state_dim), lambda g: (0, 0)),
             pl.BlockSpec((length, state_dim), lambda g: (0, 0)),
-            pl.BlockSpec((1, length, CHUNK), lambda g: (g, 0, 0)),
-            pl.BlockSpec((1, heads_step, length), lambda g: (g, 0, 0)),
-            pl.BlockSpec((1, 8 * chunks, width), lambda g: (g, 0, 0)),
+            *[pl.BlockSpec((length, heads), lambda g: (0, 0))] * 3,
+            rows_spec,
+            pl.BlockSpec((8 * chunks, width), lambda g: (0, g)),
             pl.BlockSpec((8, width), lambda g: (0, g)),
         ],
         out_shape=[
@@ -362,9 +368,9 @@
             jax.ShapeDtypeStruct((length, CHUNK), F32),
             jax.ShapeDtypeStruct((length, state_dim), F32),
             jax.ShapeDtypeStruct((length, state_dim), F32),
-            jax.ShapeDtypeStruct((groups, length, CHUNK), F32),
-            jax.ShapeDtypeStruct((groups, heads_step, length), F32),
-            jax.ShapeDtypeStruct((groups, 8 * chunks, width), F32),
+            *[jax.ShapeDtypeStruct((length, heads), F32)] * 3,
+            jax.ShapeDtypeStruct((groups * heads_step, length), F32),
+            jax.ShapeDtypeStruct((8 * chunks, inner), F32),
             jax.ShapeDtypeStruct((8, inner), F32),
         ],
         scratch_shapes=[pltpu.VMEM((state_dim, width), F32), pltpu.VMEM((8, width), F32)],
@@ -372,8 +378,8 @@
             flops=290 * length * inner * CHUNK, bytes_accessed=16 * length * inner, transcendentals=0
         ),
         name="ssd_backward",
-    )(xr, taps, bias, skip_row, *shared, *grouped, states, dy)
-    dxr, dscore_t, dbs, dcs, cols, rows, span, sums = out
+    )(xr, taps, bias, skip_row, *shared, cum_rows, kept_rows, states, dy)
+    dxr, dscore_t, dbs, dcs, upward, onward, dstep, rows, span, sums = out
     dscore_t = (dscore_t.reshape(chunks, CHUNK, CHUNK) * allowed.transpose(0, 2, 1)).astype(BF16)
     parted_c = cs_low.reshape(chunks, CHUNK, state_dim)
     parted_b = bs_low.reshape(chunks, CHUNK, state_dim)
@@ -381,27 +387,21 @@
     from_score_c = jnp.einsum("cst,csn->ctn", dscore_t, parted_b, preferred_element_type=F32)
     dbs = dbs + from_score_b.reshape(length, state_dim)
     dcs = dcs + from_score_c.reshape(length, state_dim)
-    heads = groups * heads_step
-
-    def from_columns(slot):
-        part = cols[:, :, slot * heads_step : (slot + 1) * heads_step]
-        return part.transpose(1, 0, 2).reshape(length, heads)
-
-    upward = from_columns(0) + rows.reshape(heads, length).T
-    onward = from_columns(1)
-    dstep = from_columns(2)
-    spans = jnp.sum(span[:, ::8].reshape(groups, chunks, heads_step, head_size), axis=3)
-    spans = spans.transpose(1, 0, 2).reshape(chunks, 1, heads)
+    real_heads = groups * heads_step
+    spare = heads - real_heads
+    upward = upward + jnp.pad(rows.T, ((0, 0), (0, spare)))
+    spans = jnp.sum(span[::8].reshape(chunks, real_heads, head_size), axis=2)
+    spans = jnp.pad(spans, ((0, 0), (0, spare))).reshape(chunks, 1, heads)
     places = jnp.arange(CHUNK)
     at_or_after = (places[None, :] >= places[:, None]).astype(F32)
     ahead = (places[None, :] < places[:, None]).astype(F32)
-    dlog = (
-        jnp.einsum(
-            "rt,cth->crh", at_or_after, upward.reshape(chunks, CHUNK, heads), precision=HIGHEST
-        )
-        + jnp.einsum("rs,csh->crh", ahead, onward.reshape(chunks, CHUNK, heads), precision=HIGHEST)
-        + spans
-    ).reshape(length, heads)
+    dlog = jnp.einsum(
+        "rt,cth->crh", at_or_after, upward.reshape(chunks, CHUNK, heads), precision=HIGHEST
+    )
+    dlog = dlog + jnp.einsum(
+        "rs,csh->crh", ahead, onward.reshape(chunks, CHUNK, heads), precision=HIGHEST
+    )
+    dlog = (dlog + spans).reshape(length, heads)
     return dxr, dbs, dcs, dstep, dlog, sums
 
 
@@ -410,8 +410,10 @@
 
 
 def gather_pair(own, place):
-    joined = jnp.concatenate([own, swap_pair(own), own], axis=0)
-    return lax.dynamic_slice_in_dim(joined, place * own.shape[0], 2 * own.shape[0])
+    other = swap_pair(own)
+    lower = jnp.where(place == 0, own, other)
+    upper = jnp.where(place == 0, other, own)
+    return jnp.concatenate([lower, upper], axis=0)
 
 
 def scatter_pair(values, place):
@@ -533,7 +535,7 @@
         held.append(piece.reshape((2,) * bits + (piece.shape[0] // size, piece.shape[1])))
         left.append(list(range(bits - 1, -1, -1)))
     for stage in range(bits):
-        for turn, order in enumerate(orders):
+        for turn, order in enumerate(orders[: len(pieces)]):
             bit = order[stage]
             axis = left[turn].index(bit)
             mine = (index >> bit) & 1
@@ -543,11 +545,6 @@
             held[turn] = kept.astype(F32) + got.astype(F32)
             left[turn].pop(axis)
     return held
-
-
-def column_thirds(values):
-    width = values.shape[1] // 3
-    return [values[:, turn * width : (turn + 1) * width] for turn in range(3)]
 
 
 def sum_small(values):
@@ -597,18 +594,19 @@
         axis=1,
     )
     bits = lax.axis_size("dp").bit_length() - 1
-    first_pieces = gather_stages(split_shard(first_shard), 0, bits)
+    first_pieces = gather_stages(split_shard(first_shard), 0, bits - 1)
     later_shard = jnp.concatenate([in_gate_inner[:, 0], out_proj.T], axis=1)
-    later_pieces = gather_stages(split_shard(later_shard), 0, 2)
-    first_pieces, later_pieces = lax.optimization_barrier((first_pieces, later_pieces))
-    later_pieces = gather_stages(later_pieces, 2, bits)
+    first_pieces, later_pieces = lax.optimization_barrier((first_pieces, split_shard(later_shard)))
+    first_pieces = gather_stages(first_pieces, bits - 1, bits)
+    later_pieces = gather_stages(later_pieces, 0, bits)
     first_weights = place_rows(first_pieces)
     normed = gather_pair(normed_own, tensor_place)
     first_proj = dot(normed, first_weights)
     state_end = inner_dev + 2 * state_dim
-    inner_proj = first_proj[:, :inner_dev]
+    inner_proj = first_proj
     state_proj = first_proj[:, inner_dev:state_end]
-    step_proj = first_proj[:, state_end : state_end + heads_dev]
+    step_proj = first_proj[:, state_end:]
+    step_bias_row = jnp.pad(step_bias, (0, step_pad))[None]
 
     def state_piece(state_values, conv_taps, conv_bias):
         return jax.nn.silu(
@@ -623,14 +621,14 @@
     state_act, state_back = jax.vjp(state_piece, state_proj, conv_state, conv_state_bias)
     bs_low = state_act[:, :state_dim].astype(BF16)
     cs_low = state_act[:, state_dim:].astype(BF16)
-    step_size = jax.nn.softplus(step_proj + step_bias[None, :])
-    decay_rate = -jnp.exp(decay_log)
+    step_size = jax.nn.softplus(step_proj + step_bias_row)
+    decay_rate = -jnp.exp(jnp.pad(decay_log, (0, step_pad)))
     log_decay = step_size * decay_rate[None, :]
-    terms = chunk_terms(step_size, log_decay, segment_ids, head_size)
+    terms = chunk_terms(step_size, log_decay, segment_ids, heads_dev, head_size)
     skip_row = jnp.repeat(skip_gain, head_size)[None]
     bias_row = conv_inner_bias[None]
     mixed, states, score = ssd_forward(
-        inner_proj, conv_inner, bias_row, skip_row, terms, bs_low, cs_low
+        inner_proj, conv_inner, bias_row, skip_row, terms, bs_low, cs_low, head_size
     )
     later_weights = place_rows(later_pieces)
     gate_weights = later_weights[:, :inner_dev]
@@ -694,34 +692,42 @@
         cs_low,
         states,
         grad_mixed,
+        head_size,
     )
     low_inner, grad_bs, grad_cs, grad_step_size, grad_log, inner_sums = scan_back
     taps_count = conv_inner.shape[0]
     grad_conv_inner = inner_sums[:taps_count][::-1]
     grad_conv_inner_bias = inner_sums[taps_count]
     grad_skip_gain = jnp.sum(inner_sums[taps_count + 1].reshape(heads_dev, head_size), axis=1)
-    grad_decay_log = jnp.sum(grad_log * log_decay, axis=0)
+    grad_decay_log = jnp.sum(grad_log * log_decay, axis=0)[:heads_dev]
     grad_step_proj = (grad_step_size + grad_log * decay_rate[None, :]) * jax.nn.sigmoid(
-        step_proj + step_bias[None, :]
-    )
-    grad_step_bias = jnp.sum(grad_step_proj, axis=0)
+        step_proj + step_bias_row
+    )
+    grad_step_bias = jnp.sum(grad_step_proj, axis=0)[:heads_dev]
+    grad_inner = jnp.einsum("td,tc->dc", normed, low_inner, preferred_element_type=F32).astype(BF16)
     grad_state_part = jnp.concatenate([grad_bs, grad_cs], axis=1)
     grad_state_act = grad_state_part + swap_pair(grad_state_part)
     grad_state_proj, grad_conv_state, grad_conv_state_bias = state_back(grad_state_act)
     low_state = grad_state_proj.astype(BF16)
     low_step = grad_step_proj.astype(BF16)
     own_state = low_state * (tensor_place == 0).astype(BF16)
-    low_pad = jnp.zeros((low_step.shape[0], step_pad), BF16)
-    low_first = jnp.concatenate([low_inner, low_state, low_step, low_pad], axis=1)
-    grad_first = jnp.einsum("td,tc->dc", normed, low_first, preferred_element_type=F32).astype(BF16)
-    grad_first, low_inner, low_gate = lax.optimization_barrier((grad_first, low_inner, low_gate))
-    first_part = jnp.concatenate(scatter_rows(column_thirds(grad_first)), axis=1)
+    low_rest = jnp.concatenate([low_state, low_step], axis=1)
+    low_rest_own = jnp.concatenate([own_state, low_step], axis=1)
+    grad_rest = jnp.einsum("td,tc->dc", normed, low_rest, preferred_element_type=F32).astype(BF16)
+    third = inner_dev // 3
+    late_parts = scatter_rows(
+        [grad_inner[:, turn * third : (turn + 1) * third] for turn in range(3)]
+    )
+    first_part = jnp.concatenate(late_parts + scatter_rows([grad_rest]), axis=1)
     grad_out_proj = out_part.T
     grad_in_gate_inner = jnp.stack([gate_part, first_part[:, :inner_dev]], axis=1)
     grad_in_state = first_part[:, inner_dev:state_end].reshape(in_state.shape)
     grad_in_step = first_part[:, state_end : state_end + heads_dev]
-    low_heads = jnp.concatenate([low_inner, own_state, low_step, low_pad], axis=1)
-    head_grads = dot_nt(low_gate, gate_weights) + dot_nt(low_heads, first_weights)
+    head_grads = (
+        dot_nt(low_gate, gate_weights)
+        + dot_nt(low_inner, first_weights[:, :inner_dev])
+        + dot_nt(low_rest_own, first_weights[:, inner_dev:])
+    )
     normed_grad_own = scatter_pair(head_grads, tensor_place)
     grad_norm_part = jnp.sum(normed_grad_own * own_rows * row_scale, axis=0)
     scaled_rows = normed_grad_own * norm_gain[None, :]

time: 623 us -> 630 us (1.011)
  waiting for transfers between devices: 123 us -> 171 us
  local copies, waits for them, and re-layouts: 116 us -> 87.8 us
  other arithmetic: 119 us -> 96.5 us
    ppermute x52 -> x56, waiting for transfers between devices: 123 us -> 171 us  [partner(): return lax.ppermute(values, 'dp', [(i, i ^ 1 << bit) for i in range(size)])]
    concatenate x2 -> x0, other arithmetic: 14.2 us -> none  [gather_pair(): joined = jnp.concatenate([own, swap_pair(own), own], axis=0)]
    mul x0 -> x1, other arithmetic: none -> 13.3 us  [shards(): grad_mixed = grad_gated * (gate_proj * gate_sigmoid)]
    convert_element_type x1 -> x0, other arithmetic: 13 us -> none  [shards(): low_gate = (grad_gated * mixed * (gate_sigmoid * (1.0 + gate_proj * (1.0...]
    eq x12, other arithmetic: 12.9 us -> 1 us  [ssd_backward(): (2 * pair + lane + slot * heads_step)[:, None] == jnp.arange(CHUNK)[None, :]]
    concatenate x2 -> x0, local copies, waits for them, and re-layouts: 11.4 us -> none  [the longest x1 5.71 us: shards(): jnp.concatenate([low_inner, low_state, low_step, low_pad], axis=1)]
    select_n x0 -> x2, other arithmetic: none -> 7.13 us  [gather_pair(): lower = jnp.where(place == 0, own, other)]
    transpose x8 -> x1, local copies, waits for them, and re-layouts: 7.82 us -> 0.91 us  [ssd_backward(): shared = (masks, score_t, cs_low, bs_low, cs_low.T, pick, *columns)]
  transfers between devices with their start and end apart: 58 -> 62, of which waited for: 26 -> 33; matrix products, arithmetic and copies ran while one was open for 35% -> 25% of each run, Pallas kernels for 4% -> 5%
where the time goes in v4:
time: 630 us; the launch traced here: 622 us
  waiting for transfers between devices  171 us (27%)
  Pallas kernels  104 us (17%)
  other arithmetic  96.5 us (15%)
  matrix products  95.2 us (15%)
  local copies, waits for them, and re-layouts  87.8 us (14%)
  starting transfers between devices  59.1 us (9%)
    ppermute x56, waiting for transfers between devices, partner(): return lax.ppermute(values, 'dp', [(i, i ^ 1 << bit) for i in range(size)])  171 us
    pallas_call x1, Pallas kernels, ssd_backward(): pl.pallas_call(ssd_backward_kernel, grid=(groups,), in_specs=[lanes_spec(...  61 us
    ppermute x56, starting transfers between devices, partner(): return lax.ppermute(values, 'dp', [(i, i ^ 1 << bit) for i in range(size)])  58.1 us
    pallas_call x1, Pallas kernels, ssd_forward(): pl.pallas_call(ssd_forward_kernel, grid=(groups,), in_specs=[lanes_spec(a...  27.4 us
    dot_general x2, matrix products, dot(): return jnp.dot(a, b, preferred_element_type=F32)  24.1 us
    unnamed x232, local copies, waits for them, and re-layouts  22.1 us
    dot_general x3, matrix products, dot_nt(): lax.dot_general(a, b, (((1,), (1,)), ((), ())), preferred_element_type=F32)  22.1 us
    concatenate x15, other arithmetic, gather_stages(): joined.append(jnp.concatenate([piece, other], axis=0))  15.8 us
  transfers between devices with their start and end apart: 62, of which 33 were waited for; matrix products, arithmetic and copies ran while one was open for 25% of the time, Pallas kernels for 5%

profile of v4, /device:TPU:0, one launch (start us, length us, event | category | flops | bytes accessed | tf_op | source)
XLA Modules:
  0.0 621.9 jit_solution(12299707150621105587)
XLA Ops:
  4.7 4.1 collective-permute-start.1
  40.0 2.9 collective-permute-done.2
  64.5 6.5 %collective-permute-done.9 = bf16[4,96,640]{2,1,0:T(8,128)(2,1)S(1)} collective-permute-done((bf16[4,96,640]{2,1,0:T(8,128)(2,1)S(1)}, bf16[4,96,640]{2,1,0:T(8,128)(2,1)S(1)}, u32[]{:S(2)}, u32[]{:S(2)}) %collective-permute-start.9) | collective-permute-done | bytes 491552 | tf_op jit(solution)/shard_map/ppermute | solution.py:435
  72.3 3.4 collective-permute-start.13
  77.1 10.5 %collective-permute-done.13 = bf16[1,96,1024]{2,1,0:T(8,128)(2,1)S(1)} collective-permute-done((bf16[1,96,1024]{2,1,0:T(8,128)(2,1)S(1)}, bf16[1,96,1024]{2,1,0:T(8,128)(2,1)S(1)}, u32[]{:S(2)}, u32[]{:S(2)}) %collective-permute-start.13) | collective-permute-done | bytes 196640 | tf_op jit(solution)/shard_map/ppermute | solution.py:435
  88.0 3.4 collective-permute-start.18
  94.2 12.5 %collective-permute-done.14 = bf16[2,96,1024]{2,1,0:T(8,128)(2,1)S(1)} collective-permute-done((bf16[2,96,1024]{2,1,0:T(8,128)(2,1)S(1)}, bf16[2,96,1024]{2,1,0:T(8,128)(2,1)S(1)}, u32[]{:S(2)}, u32[]{:S(2)}) %collective-permute-start.14) | collective-permute-done | bytes 393248 | tf_op jit(solution)/shard_map/ppermute | solution.py:435
  115.1 3.8 broadcast_select_fusion.1
  119.8 3.4 broadcast_select_fusion.3
  123.2 7.2 %collective-permute-done.10.refs_1_ = bf16[8,96,640]{2,1,0:T(8,128)(2,1)S(1)} collective-permute-done((bf16[8,96,640]{2,1,0:T(8,128)(2,1)S(1)}, bf16[8,96,640]{2,1,0:T(8,128)(2,1)S(1)}, u32[]{:S(2)}, u32[]{:S(2)}) %collective-permute-start.10) | collective-permute-done | bytes 983072 | tf_op jit(solution)/shard_map/ppermute | solution.py:435
  134.5 6.6 %place_rows.2 = bf16[16,96,1920]{2,1,0:T(8,128)(2,1)} custom-call(s32[3,16]{1,0:T(4,128)} %pad_add_fusion.1.table, bf16[8,96,640]{2,1,0:T(8,128)(2,1)} %copy-done.21, bf16[8,96,640]{2,1,0:T(8,128)(2,1)} %copy-done.47, bf16[8,96,640]{2,1,0:T(8,128)(2,1)} %copy-done.22, bf16[8,96,640]{2,1,0:T(8,128)(2,1)} %copy-done.48, bf16[8,96,640]{2,1,0:T(8,128)(2,1)} %copy-done.23, ...), custom_call_target="tpu_custom_call" | custom-call | bytes 11796480 | tf_op jit(solution)/shard_map/place_rows/pallas_call | solution.py:510
  141.2 8.8 %fusion.78.xr = f32[1024,1920]{1,0:T(8,128)S(1)} fusion(bf16[1536,1920]{1,0:T(8,128)(2,1)} %bitcast.281, bf16[512,1536]{1,0:T(8,128)(2,1)S(1)} %copy-done.39, bf16[512,1536]{1,0:T(8,128)(2,1)S(1)} %get-tuple-element.171), kind=kOutput, calls=%fused_computation.325 | convolution fusion | flops 6046089216 | bytes 16908288 | tf_op jit(solution)/shard_map/dot_general | solution.py:35
  150.3 2.8 copy-done.24
  158.2 3.7 multiply_convert_fusion.2
  180.5 27.4 %ssd_forward.1 = (f32[1024,1536]{1,0:T(8,128)}, bf16[1024,1536]{1,0:T(8,128)(2,1)}) custom-call(f32[1024,1920]{1,0:T(8,128)} %copy-done.24, f32[4,1536]{1,0:T(4,128)} %taps.3, f32[1,1536]{1,0:T(1,128)} %broadcast_in_dim.29.bias, f32[1,1536]{1,0:T(1,128)} %broadcast_in_dim_reshape.2.skip, f32[3,1024,128]{2,1,0:T(8,128)} %pad_maximum_fusion.5.masks, ...), custom_call_target="tpu_custom_call" | custom-call | flops 26172456960 | bytes 18874368 | tf_op jit(solution)/shard_map/ssd_forward/pallas_call | solution.py:298
  211.1 3.4 collective-permute-done.24.refs_5_
  214.5 9.1 %place_rows.3 = bf16[16,96,3072]{2,1,0:T(8,128)(2,1)} custom-call(s32[3,16]{1,0:T(4,128)} %pad_add_fusion.1.table, bf16[8,96,1024]{2,1,0:T(8,128)(2,1)} %constant_dynamic-update-slice_fusion.refs_0_, bf16[8,96,1024]{2,1,0:T(8,128)(2,1)} %copy-done.33, bf16[8,96,1024]{2,1,0:T(8,128)(2,1)} %constant_dynamic-update-slice_fusion.4.refs_2_, ...), custom_call_target="tpu_custom_call" | custom-call | bytes 18874368 | tf_op jit(solution)/shard_map/place_rows/pallas_call | solution.py:510
  223.6 15.3 %multiply_reduce_fusion.2 = (f32[1024]{0:T(1024)S(1)}, f32[1024,1536]{1,0:T(8,128)}, f32[1024,1536]{1,0:T(8,128)}) fusion(f32[1024,1536]{1,0:T(8,128)} %get-tuple-element.39, bf16[1536,3072]{1,0:T(8,128)(2,1)} %bitcast.277, bf16[512,1536]{1,0:T(8,128)(2,1)} %get-tuple-element.172, bf16[512,1536]{1,0:T(8,128)(2,1)} %copy-done.35), kind=kOutput, calls=%fused_computation.15 | convolution fusion | flops 4849138688 | bytes 26742784 | tf_op jit(solution)/shard_map/dot_general | solution.py:35
  241.4 12.0 %multiply_reduce_fusion = (f32[1536]{0:T(1024)}, f32[1024]{0:T(1024)S(1)}, f32[1024,1536]{1,0:T(8,128)}) fusion(f32[1024,1536]{1,0:T(8,128)} %get-tuple-element.153, f32[1024]{0:T(1024)S(1)} %get-tuple-element.210, f32[1536]{0:T(1024)S(1)} %copy-done.90, bf16[1536,3072]{1,0:T(8,128)(2,1)} %bitcast.278, bf16[512,1536]{1,0:T(8,128)(2,1)S(1)} %copy-done.44, ...), kind=kOutput, calls=%fused_computation.9 | convolution fusion | flops 4847564288 | bytes 20467712 | tf_op jit(solution)/shard_map/td,dc->tc/dot_general | solution.py:654
  255.9 13.3 %fusion.22 = (f32[1024,1536]{1,0:T(8,128)}, bf16[1024,1536]{1,0:T(8,128)(2,1)S(1)}) fusion(f32[1024]{0:T(1024)S(1)} %broadcast_multiply_fusion.5, f32[1024,1536]{1,0:T(8,128)} %get-tuple-element.153, f32[1024,1536]{1,0:T(8,128)} %get-tuple-element.225, f32[1024]{0:T(1024)S(1)} %get-tuple-element.209, f32[1536]{0:T(1024)S(1)} %copy-done.90, ...), kind=kLoop, calls=%fused_computation.48 | loop fusion | flops 26738688 | bytes 34621440 | tf_op jit(solution)/shard_map/mul | solution.py:666
  269.1 9.4 %fusion.7 = f32[1024,1536]{1,0:T(8,128)} fusion(bf16[1024,1536]{1,0:T(8,128)(2,1)S(1)} %get-tuple-element.159, bf16[1536,3072]{1,0:T(8,128)(2,1)} %bitcast.279), kind=kOutput, calls=%fused_computation.24 | convolution fusion | flops 4831838208 | bytes 14155776 | tf_op jit(solution)/shard_map/dot_general | solution.py:39
  278.6 6.8 %convolution_convert_fusion.2 = bf16[1536,1536]{1,0:T(8,128)(2,1)} fusion(bf16[1024,1536]{1,0:T(8,128)(2,1)S(1)} %get-tuple-element.159, bf16[512,1536]{1,0:T(8,128)(2,1)S(1)} %copy-done.40, bf16[512,1536]{1,0:T(8,128)(2,1)S(1)} %copy-done.36), kind=kOutput, calls=%fused_computation.2 | convolution fusion | flops 4840488960 | bytes 11010048 | tf_op jit(solution)/shard_map/td,tc->dc/dot_general | solution.py:667
  285.3 7.3 %convolution_convert_fusion.1 = bf16[1536,1536]{1,0:T(8,128)(2,1)} fusion(bf16[512,1536]{1,0:T(8,128)(2,1)S(1)} %copy-done.44, bf16[512,1536]{1,0:T(8,128)(2,1)S(1)} %copy-done.43, f32[1024,1536]{1,0:T(8,128)S(1)} %bitcast.292, f32[1536]{0:T(1024)S(1)} %copy-done.90, f32[1024]{0:T(1024)S(1)} %get-tuple-element.210), kind=kOutput, calls=%fused_computation.1 | convolution fusion | flops 4845207552 | bytes 14166016 | tf_op jit(solution)/shard_map/td,tc->dc/dot_general | solution.py:651
  292.6 61.0 %ssd_backward.1 = (bf16[1024,1536]{1,0:T(8,128)(2,1)}, f32[1024,128]{1,0:T(8,128)}, f32[1024,128]{1,0:T(8,128)}, f32[1024,128]{1,0:T(8,128)}, f32[1024,128]{1,0:...) custom-call(f32[1024,1920]{1,0:T(8,128)} %copy-done.24, ...), custom_call_target="tpu_custom_call" | custom-call | flops 58384711680 | bytes 25165824 | tf_op jit(solution)/shard_map/ssd_backward/pallas_call | solution.py:349
  355.7 10.9 %fusion.5 = f32[1024,1536]{1,0:T(8,128)} fusion(bf16[1536,3072]{1,0:T(8,128)(2,1)} %bitcast.280, f32[1024,1536]{1,0:T(8,128)} %get-tuple-element.153, f32[1536]{0:T(1024)S(1)} %copy-done.90, f32[1024]{0:T(1024)S(1)} %get-tuple-element.210), kind=kOutput, calls=%fused_computation.22 | convolution fusion | flops 4836556800 | bytes 17311744 | tf_op jit(solution)/shard_map/tc,dc->td/dot_general | solution.py:643
  367.3 9.5 %fusion.1 = f32[1024,1536]{1,0:T(8,128)} fusion(bf16[1024,1536]{1,0:T(8,128)(2,1)S(1)} %copy-done.98, bf16[1536,1920]{1,0:T(8,128)(2,1)} %bitcast.282), kind=kOutput, calls=%fused_computation.18 | convolution fusion | flops 4831838208 | bytes 14155776 | tf_op jit(solution)/shard_map/dot_general | solution.py:39
  376.8 6.7 %convolution_convert_fusion = bf16[1536,1536]{1,0:T(8,128)(2,1)} fusion(bf16[1024,1536]{1,0:T(8,128)(2,1)S(1)} %copy-done.98, bf16[512,1536]{1,0:T(8,128)(2,1)S(1)} %copy-done.41, bf16[512,1536]{1,0:T(8,128)(2,1)S(1)} %copy-done.37), kind=kOutput, calls=%fused_computation | convolution fusion | flops 4840488960 | bytes 11010048 | tf_op jit(solution)/shard_map/td,tc->dc/dot_general | solution.py:707
  393.5 3.7 constant_dynamic-slice_fusion.13
  412.2 9.9 %collective-permute-done.50 = bf16[2,2,2,96,512]{4,3,0,1,2:T(8,128)(2,1)S(1)} collective-permute-done((bf16[2,2,2,96,512]{4,3,0,1,2:T(8,128)(2,1)S(1)}, bf16[2,2,2,96,512]{4,3,0,1,2:T(8,128)(2,1)S(1)}, u32[]{:S(2)}, u32[]{:S(2)}) %collective-permute-start.50) | collective-permute-done | bytes 786464 | tf_op jit(solution)/shard_map/ppermute | solution.py:435
  440.0 3.2 add_add_fusion
  449.6 16.7 %collective-permute-done.47 = bf16[2,2,96,512]{3,2,1,0:T(8,128)(2,1)} collective-permute-done((bf16[2,2,96,512]{3,2,1,0:T(8,128)(2,1)}, bf16[2,2,96,512]{3,2,1,0:T(8,128)(2,1)}, u32[]{:S(2)}, u32[]{:S(2)}) %collective-permute-start.47) | collective-permute-done | bytes 393248 | tf_op jit(solution)/shard_map/ppermute | solution.py:435
  469.4 5.0 collective-permute-done.52
  475.1 8.4 %collective-permute-done.48 = bf16[2,96,512]{2,1,0:T(8,128)(2,1)S(1)} collective-permute-done((bf16[2,96,512]{2,1,0:T(8,128)(2,1)S(1)}, bf16[2,96,512]{2,1,0:T(8,128)(2,1)S(1)}, u32[]{:S(2)}, u32[]{:S(2)}) %collective-permute-start.48) | collective-permute-done | bytes 196640 | tf_op jit(solution)/shard_map/ppermute | solution.py:435
  483.7 5.5 collective-permute-done.44
  489.7 5.6 collective-permute-done.53
  496.2 7.2 %collective-permute-done.49 = bf16[96,512]{1,0:T(8,128)(2,1)S(1)} collective-permute-done((bf16[96,512]{1,0:T(8,128)(2,1)S(1)}, bf16[96,512]{1,0:T(8,128)(2,1)S(1)}, u32[]{:S(2)}, u32[]{:S(2)}) %collective-permute-start.49) | collective-permute-done | bytes 98336 | tf_op jit(solution)/shard_map/ppermute | solution.py:435
  503.9 5.8 collective-permute-done.45
  514.9 8.3 %collective-permute-done.54 = bf16[2,2,2,96,384]{4,3,2,1,0:T(8,128)(2,1)S(1)} collective-permute-done((bf16[2,2,2,96,384]{4,3,2,1,0:T(8,128)(2,1)}, bf16[2,2,2,96,384]{4,3,2,1,0:T(8,128)(2,1)S(1)}, u32[]{:S(2)}, u32[]{:S(2)}) %collective-permute-start.54) | collective-permute-done | bytes 589856 | tf_op jit(solution)/shard_map/ppermute | solution.py:435
  528.4 3.0 collective-permute-done.55
  534.2 13.3 %collective-permute-done.56 = bf16[2,96,384]{2,1,0:T(8,128)(2,1)S(1)} collective-permute-done((bf16[2,96,384]{2,1,0:T(8,128)(2,1)S(1)}, bf16[2,96,384]{2,1,0:T(8,128)(2,1)S(1)}, u32[]{:S(2)}, u32[]{:S(2)}) %collective-permute-start.56) | collective-permute-done | bytes 147488 | tf_op jit(solution)/shard_map/ppermute | solution.py:435
  549.2 4.3 collective-permute-done.57
  560.3 7.3 %collective-permute-done.35 = bf16[2,2,96,1024]{3,2,0,1:T(8,128)(2,1)} collective-permute-done((bf16[2,2,96,1024]{3,2,0,1:T(8,128)(2,1)}, bf16[2,2,96,1024]{3,2,0,1:T(8,128)(2,1)}, u32[]{:S(2)}, u32[]{:S(2)}) %collective-permute-start.35) | collective-permute-done | bytes 786464 | tf_op jit(solution)/shard_map/ppermute | solution.py:435
  572.7 10.4 %collective-permute-done.40 = bf16[2,96,1024]{2,1,0:T(8,128)(2,1)S(1)} collective-permute-done((bf16[2,96,1024]{2,1,0:T(8,128)(2,1)S(1)}, bf16[2,96,1024]{2,1,0:T(8,128)(2,1)S(1)}, u32[]{:S(2)}, u32[]{:S(2)}) %collective-permute-start.40) | collective-permute-done | bytes 393248 | tf_op jit(solution)/shard_map/ppermute | solution.py:435
  584.3 2.9 collective-permute-done.36
  588.1 5.3 fusion.21
  597.6 3.3 collective-permute-done.30
  610.3 3.3 collective-permute-start.33
  613.6 5.0 fusion.12
  (560 shorter events, 210.0 us)
Async XLA Ops:
  4.7 25.1 %collective-permute-start.1 = (bf16[1,96,640]{2,1,0:T(8,128)(2,1)}, bf16[1,96,640]{2,1,0:T(8,128)(2,1)}, u32[]{:S(2)}, u32[]{:S(2)}) collective-permute-start(bf16[1,96,640]{2,1,0:T(8,128)(2,1)} %get-tuple-element.200), channel_id=1, source_target_pairs={{0,16},{2,18},{4,20},{6,22},{8,24},{10,26},{12,28},{14,30},{16,0},... | collective-permute-start | bytes 368648 | tf_op jit(solution)/shard_map/ppermute | solution.py:435
  8.8 23.7 %collective-permute-start.4 = (bf16[1,96,640]{2,1,0:T(8,128)(2,1)}, bf16[1,96,640]{2,1,0:T(8,128)(2,1)}, u32[]{:S(2)}, u32[]{:S(2)}) collective-permute-start(bf16[1,96,640]{2,1,0:T(8,128)(2,1)} %get-tuple-element.199), channel_id=1, source_target_pairs={{0,2},{2,0},{4,6},{6,4},{8,10},{10,8},{12,14},{14,12},{16,18},{18,... | collective-permute-start | bytes 368648 | tf_op jit(solution)/shard_map/ppermute | solution.py:435
  13.5 23.2 %collective-permute-start.7 = (bf16[1,96,640]{2,1,0:T(8,128)(2,1)}, bf16[1,96,640]{2,1,0:T(8,128)(2,1)}, u32[]{:S(2)}, u32[]{:S(2)}) collective-permute-start(bf16[1,96,640]{2,1,0:T(8,128)(2,1)} %slice_bitcast_fusion.2), channel_id=1, source_target_pairs={{0,16},{2,18},{4,20},{6,22},{8,24},{10,26},{12,28},{14,30},{16,0},... | collective-permute-start | bytes 368648 | tf_op jit(solution)/shard_map/ppermute | solution.py:435
  16.4 102.4 %collective-permute-start = (bf16[512,1536]{1,0:T(8,128)(2,1)}, bf16[512,1536]{1,0:T(8,128)(2,1)}, u32[]{:S(2)}, u32[]{:S(2)}) collective-permute-start(bf16[512,1536]{1,0:T(8,128)(2,1)} %fusion.15), channel_id=1, source_target_pairs={{0,1},{1,0},{2,3},{3,2},{4,5},{5,4},{6,7},{7,6},{8,9},{9,8},{10,11... | collective-permute-start | bytes 4718600 | tf_op jit(solution)/shard_map/ppermute | solution.py:409
  18.0 96.6 %collective-permute-start.26 = (bf16[512,1536]{1,0:T(8,128)(2,1)}, bf16[512,1536]{1,0:T(8,128)(2,1)}, u32[]{:S(2)}, u32[]{:S(2)}) collective-permute-start(bf16[512,1536]{1,0:T(8,128)(2,1)} %fusion.11), channel_id=1, source_target_pairs={{0,1},{1,0},{2,3},{3,2},{4,5},{5,4},{6,7},{7,6},{8,9},{9,8},{10,11... | collective-permute-start | bytes 4718600 | tf_op jit(solution)/shard_map/ppermute | solution.py:409
  30.9 12.0 %collective-permute-start.2 = (bf16[2,96,640]{2,1,0:T(8,128)(2,1)S(1)}, bf16[2,96,640]{2,1,0:T(8,128)(2,1)S(1)}, u32[]{:S(2)}, u32[]{:S(2)}) collective-permute-start(bf16[2,96,640]{2,1,0:T(8,128)(2,1)S(1)} %pad_maximum_fusion.26), channel_id=1, source_target_pairs={{0,8},{2,10},{4,12},{6,14},{8,0},{10,2},{12,4},{14,6},{16,24},{18,... | collective-permute-start | bytes 737288 | tf_op jit(solution)/shard_map/ppermute | solution.py:435
  33.5 13.9 %collective-permute-start.5 = (bf16[2,96,640]{2,1,0:T(8,128)(2,1)S(1)}, bf16[2,96,640]{2,1,0:T(8,128)(2,1)S(1)}, u32[]{:S(2)}, u32[]{:S(2)}) collective-permute-start(bf16[2,96,640]{2,1,0:T(8,128)(2,1)S(1)} %pad_maximum_fusion.27), channel_id=1, source_target_pairs={{0,16},{2,18},{4,20},{6,22},{8,24},{10,26},{12,28},{14,30},{16,0},... | collective-permute-start | bytes 737288 | tf_op jit(solution)/shard_map/ppermute | solution.py:435
  38.5 20.0 %collective-permute-start.8 = (bf16[2,96,640]{2,1,0:T(8,128)(2,1)}, bf16[2,96,640]{2,1,0:T(8,128)(2,1)}, u32[]{:S(2)}, u32[]{:S(2)}) collective-permute-start(bf16[2,96,640]{2,1,0:T(8,128)(2,1)} %pad_maximum_fusion.28), channel_id=1, source_target_pairs={{0,4},{2,6},{4,0},{6,2},{8,12},{10,14},{12,8},{14,10},{16,20},{18,... | collective-permute-start | bytes 737288 | tf_op jit(solution)/shard_map/ppermute | solution.py:435
  44.8 16.7 %collective-permute-start.3 = (bf16[4,96,640]{2,1,0:T(8,128)(2,1)}, bf16[4,96,640]{2,1,0:T(8,128)(2,1)}, u32[]{:S(2)}, u32[]{:S(2)}) collective-permute-start(bf16[4,96,640]{2,1,0:T(8,128)(2,1)} %pad_maximum_fusion.20), channel_id=1, source_target_pairs={{0,4},{2,6},{4,0},{6,2},{8,12},{10,14},{12,8},{14,10},{16,20},{18,... | collective-permute-start | bytes 1474568 | tf_op jit(solution)/shard_map/ppermute | solution.py:435
  49.9 13.0 %collective-permute-start.6 = (bf16[4,96,640]{2,1,0:T(8,128)(2,1)}, bf16[4,96,640]{2,1,0:T(8,128)(2,1)}, u32[]{:S(2)}, u32[]{:S(2)}) collective-permute-start(bf16[4,96,640]{2,1,0:T(8,128)(2,1)} %pad_maximum_fusion.21), channel_id=1, source_target_pairs={{0,8},{2,10},{4,12},{6,14},{8,0},{10,2},{12,4},{14,6},{16,24},{18,... | collective-permute-start | bytes 1474568 | tf_op jit(solution)/shard_map/ppermute | solution.py:435
  59.6 11.5 %collective-permute-start.9 = (bf16[4,96,640]{2,1,0:T(8,128)(2,1)S(1)}, bf16[4,96,640]{2,1,0:T(8,128)(2,1)S(1)}, u32[]{:S(2)}, u32[]{:S(2)}) collective-permute-start(bf16[4,96,640]{2,1,0:T(8,128)(2,1)S(1)} %pad_maximum_fusion.22), channel_id=1, source_target_pairs={{0,2},{2,0},{4,6},{6,4},{8,10},{10,8},{12,14},{14,12},{16,18},{18,... | collective-permute-start | bytes 1474568 | tf_op jit(solution)/shard_map/ppermute | solution.py:435
  72.3 15.2 %collective-permute-start.13 = (bf16[1,96,1024]{2,1,0:T(8,128)(2,1)S(1)}, bf16[1,96,1024]{2,1,0:T(8,128)(2,1)S(1)}, u32[]{:S(2)}, u32[]{:S(2)}) collective-permute-start(bf16[1,96,1024]{2,1,0:T(8,128)(2,1)S(1)} %copy-done.25), channel_id=1, source_target_pairs={{0,16},{2,18},{4,20},{6,22},{8,24},{10,26},{12,28},{14,30},{16,0},... | collective-permute-start | bytes 589832 | tf_op jit(solution)/shard_map/ppermute | solution.py:435
  75.8 12.2 %collective-permute-start.17 = (bf16[1,96,1024]{2,1,0:T(8,128)(2,1)S(1)}, bf16[1,96,1024]{2,1,0:T(8,128)(2,1)S(1)}, u32[]{:S(2)}, u32[]{:S(2)}) collective-permute-start(bf16[1,96,1024]{2,1,0:T(8,128)(2,1)S(1)} %get-tuple-element.41), channel_id=1, source_target_pairs={{0,2},{2,0},{4,6},{6,4},{8,10},{10,8},{12,14},{14,12},{16,18},{18,... | collective-permute-start | bytes 589832 | tf_op jit(solution)/shard_map/ppermute | solution.py:435
  76.3 15.6 %collective-permute-start.21 = (bf16[1,96,1024]{2,1,0:T(8,128)(2,1)S(1)}, bf16[1,96,1024]{2,1,0:T(8,128)(2,1)S(1)}, u32[]{:S(2)}, u32[]{:S(2)}) collective-permute-start(bf16[1,96,1024]{2,1,0:T(8,128)(2,1)S(1)} %get-tuple-element.42), channel_id=1, source_target_pairs={{0,16},{2,18},{4,20},{6,22},{8,24},{10,26},{12,28},{14,30},{16,0},... | collective-permute-start | bytes 589832 | tf_op jit(solution)/shard_map/ppermute | solution.py:435
  87.6 19.1 %collective-permute-start.14 = (bf16[2,96,1024]{2,1,0:T(8,128)(2,1)S(1)}, bf16[2,96,1024]{2,1,0:T(8,128)(2,1)S(1)}, u32[]{:S(2)}, u32[]{:S(2)}) collective-permute-start(bf16[2,96,1024]{2,1,0:T(8,128)(2,1)S(1)} %pad_maximum_fusion.23), channel_id=1, source_target_pairs={{0,8},{2,10},{4,12},{6,14},{8,0},{10,2},{12,4},{14,6},{16,24},{18,... | collective-permute-start | bytes 1179656 | tf_op jit(solution)/shard_map/ppermute | solution.py:435
  88.0 20.1 %collective-permute-start.18 = (bf16[2,96,1024]{2,1,0:T(8,128)(2,1)S(1)}, bf16[2,96,1024]{2,1,0:T(8,128)(2,1)S(1)}, u32[]{:S(2)}, u32[]{:S(2)}) collective-permute-start(bf16[2,96,1024]{2,1,0:T(8,128)(2,1)S(1)} %pad_maximum_fusion.24), channel_id=1, source_target_pairs={{0,16},{2,18},{4,20},{6,22},{8,24},{10,26},{12,28},{14,30},{16,0},... | collective-permute-start | bytes 1179656 | tf_op jit(solution)/shard_map/ppermute | solution.py:435
  91.9 17.8 %collective-permute-start.22 = (bf16[2,96,1024]{2,1,0:T(8,128)(2,1)S(1)}, bf16[2,96,1024]{2,1,0:T(8,128)(2,1)S(1)}, u32[]{:S(2)}, u32[]{:S(2)}) collective-permute-start(bf16[2,96,1024]{2,1,0:T(8,128)(2,1)S(1)} %pad_maximum_fusion.25), channel_id=1, source_target_pairs={{0,4},{2,6},{4,0},{6,2},{8,12},{10,14},{12,8},{14,10},{16,20},{18,... | collective-permute-start | bytes 1179656 | tf_op jit(solution)/shard_map/ppermute | solution.py:435
  106.7 23.7 %collective-permute-start.10 = (bf16[8,96,640]{2,1,0:T(8,128)(2,1)S(1)}, bf16[8,96,640]{2,1,0:T(8,128)(2,1)S(1)}, u32[]{:S(2)}, u32[]{:S(2)}) collective-permute-start(bf16[8,96,640]{2,1,0:T(8,128)(2,1)S(1)} %pad_maximum_fusion.8.refs_0_), channel_id=1, source_target_pairs={{0,2},{2,0},{4,6},{6,4},{8,10},{10,8},{12,14},{14,12},{16,18},{18,... | collective-permute-start | bytes 2949128 | tf_op jit(solution)/shard_map/ppermute | solution.py:435
  108.1 24.6 %collective-permute-start.11 = (bf16[8,96,640]{2,1,0:T(8,128)(2,1)S(1)}, bf16[8,96,640]{2,1,0:T(8,128)(2,1)S(1)}, u32[]{:S(2)}, u32[]{:S(2)}) collective-permute-start(bf16[8,96,640]{2,1,0:T(8,128)(2,1)S(1)} %pad_maximum_fusion.9.refs_2_), channel_id=1, source_target_pairs={{0,4},{2,6},{4,0},{6,2},{8,12},{10,14},{12,8},{14,10},{16,20},{18,... | collective-permute-start | bytes 2949128 | tf_op jit(solution)/shard_map/ppermute | solution.py:435
  109.7 24.8 %collective-permute-start.12 = (bf16[8,96,640]{2,1,0:T(8,128)(2,1)S(1)}, bf16[8,96,640]{2,1,0:T(8,128)(2,1)}, u32[]{:S(2)}, u32[]{:S(2)}) collective-permute-start(bf16[8,96,640]{2,1,0:T(8,128)(2,1)S(1)} %pad_maximum_fusion.10.refs_4_), channel_id=1, source_target_pairs={{0,8},{2,10},{4,12},{6,14},{8,0},{10,2},{12,4},{14,6},{16,24},{18,... | collective-permute-start | bytes 2949128 | tf_op jit(solution)/shard_map/ppermute | solution.py:435
  114.5 58.2 %collective-permute-start.15 = (bf16[4,96,1024]{2,1,0:T(8,128)(2,1)}, bf16[4,96,1024]{2,1,0:T(8,128)(2,1)}, u32[]{:S(2)}, u32[]{:S(2)}) collective-permute-start(bf16[4,96,1024]{2,1,0:T(8,128)(2,1)} %pad_maximum_fusion.15), channel_id=1, source_target_pairs={{0,4},{2,6},{4,0},{6,2},{8,12},{10,14},{12,8},{14,10},{16,20},{18,... | collective-permute-start | bytes 2359304 | tf_op jit(solution)/shard_map/ppermute | solution.py:435
  118.8 56.8 %collective-permute-start.19 = (bf16[4,96,1024]{2,1,0:T(8,128)(2,1)}, bf16[4,96,1024]{2,1,0:T(8,128)(2,1)}, u32[]{:S(2)}, u32[]{:S(2)}) collective-permute-start(bf16[4,96,1024]{2,1,0:T(8,128)(2,1)} %pad_maximum_fusion.16), channel_id=1, source_target_pairs={{0,8},{2,10},{4,12},{6,14},{8,0},{10,2},{12,4},{14,6},{16,24},{18,... | collective-permute-start | bytes 2359304 | tf_op jit(solution)/shard_map/ppermute | solution.py:435
  130.3 48.1 %collective-permute-start.23 = (bf16[4,96,1024]{2,1,0:T(8,128)(2,1)}, bf16[4,96,1024]{2,1,0:T(8,128)(2,1)}, u32[]{:S(2)}, u32[]{:S(2)}) collective-permute-start(bf16[4,96,1024]{2,1,0:T(8,128)(2,1)} %pad_maximum_fusion.17), channel_id=1, source_target_pairs={{0,2},{2,0},{4,6},{6,4},{8,10},{10,8},{12,14},{14,12},{16,18},{18,... | collective-permute-start | bytes 2359304 | tf_op jit(solution)/shard_map/ppermute | solution.py:435
  174.9 33.6 %collective-permute-start.16 = (bf16[8,96,1024]{2,1,0:T(8,128)(2,1)}, bf16[8,96,1024]{2,1,0:T(8,128)(2,1)S(1)}, u32[]{:S(2)}, u32[]{:S(2)}) collective-permute-start(bf16[8,96,1024]{2,1,0:T(8,128)(2,1)} %constant_dynamic-update-slice_fusion.refs_0_), channel_id=1, source_target_pairs={{0,2},{2,0},{4,6},{6,4},{8,10},{10,8},{12,14},{14,12},{16,18},{18,... | collective-permute-start | bytes 4718600 | tf_op jit(solution)/shard_map/ppermute | solution.py:435
  177.7 33.4 %collective-permute-start.20 = (bf16[8,96,1024]{2,1,0:T(8,128)(2,1)}, bf16[8,96,1024]{2,1,0:T(8,128)(2,1)S(1)}, u32[]{:S(2)}, u32[]{:S(2)}) collective-permute-start(bf16[8,96,1024]{2,1,0:T(8,128)(2,1)} %constant_dynamic-update-slice_fusion.4.refs_2_), channel_id=1, source_target_pairs={{0,4},{2,6},{4,0},{6,2},{8,12},{10,14},{12,8},{14,10},{16,20},{18,... | collective-permute-start | bytes 4718600 | tf_op jit(solution)/shard_map/ppermute | solution.py:435
  180.5 34.0 %collective-permute-start.24 = (bf16[8,96,1024]{2,1,0:T(8,128)(2,1)}, bf16[8,96,1024]{2,1,0:T(8,128)(2,1)}, u32[]{:S(2)}, u32[]{:S(2)}) collective-permute-start(bf16[8,96,1024]{2,1,0:T(8,128)(2,1)} %constant_dynamic-update-slice_fusion.8.refs_4_), channel_id=1, source_target_pairs={{0,8},{2,10},{4,12},{6,14},{8,0},{10,2},{12,4},{14,6},{16,24},{18,... | collective-permute-start | bytes 4718600 | tf_op jit(solution)/shard_map/ppermute | solution.py:435
  393.3 34.0 %collective-permute-start.27 = (f32[1024,256]{0,1:T(8,128)}, f32[1024,256]{0,1:T(8,128)}, u32[]{:S(2)}, u32[]{:S(2)}) collective-permute-start(f32[1024,256]{0,1:T(8,128)} %pad_maximum_fusion.7), channel_id=1, source_target_pairs={{0,1},{1,0},{2,3},{3,2},{4,5},{5,4},{6,7},{7,6},{8,9},{9,8},{10,11... | collective-permute-start | bytes 3145736 | tf_op jit(solution)/shard_map/ppermute | solution.py:409
  397.3 216.3 %collective-permute-start.25 = (f32[512,1536]{1,0:T(8,128)}, f32[512,1536]{1,0:T(8,128)}, u32[]{:S(2)}, u32[]{:S(2)}) collective-permute-start(f32[512,1536]{1,0:T(8,128)} %constant_dynamic-slice_fusion.13), channel_id=1, source_target_pairs={{0,1},{1,0},{2,3},{3,2},{4,5},{5,4},{6,7},{7,6},{8,9},{9,8},{10,11... | collective-permute-start | bytes 9437192 | tf_op jit(solution)/shard_map/ppermute | solution.py:409
  402.5 19.7 %collective-permute-start.50 = (bf16[2,2,2,96,512]{4,3,0,1,2:T(8,128)(2,1)S(1)}, bf16[2,2,2,96,512]{4,3,0,1,2:T(8,128)(2,1)S(1)}, u32[]{:S(2)}, u32[]{:S(2)}) collective-permute-start(bf16[2,2,2,96,512]{4,3,0,1,2:T(8,128)(2,1)S(1)} %bitcast.320), channel_id=1, source_target_pairs={{0,8},{2,10},{4,12},{6,14},{8,0},{10,2},{12,4},{14,6},{16,24},{18,... | collective-permute-start | bytes 2359304 | tf_op jit(solution)/shard_map/ppermute | solution.py:435
  403.0 20.5 %collective-permute-start.46 = (bf16[2,2,2,96,512]{4,3,2,0,1:T(8,128)(2,1)S(1)}, bf16[2,2,2,96,512]{4,3,2,0,1:T(8,128)(2,1)S(1)}, u32[]{:S(2)}, u32[]{:S(2)}) collective-permute-start(bf16[2,2,2,96,512]{4,3,2,0,1:T(8,128)(2,1)S(1)} %bitcast.319), channel_id=1, source_target_pairs={{0,4},{2,6},{4,0},{6,2},{8,12},{10,14},{12,8},{14,10},{16,20},{18,... | collective-permute-start | bytes 2359304 | tf_op jit(solution)/shard_map/ppermute | solution.py:435
  404.0 21.3 %collective-permute-start.42 = (bf16[2,2,2,96,512]{4,3,0,1,2:T(8,128)(2,1)S(1)}, bf16[2,2,2,96,512]{4,3,0,1,2:T(8,128)(2,1)S(1)}, u32[]{:S(2)}, u32[]{:S(2)}) collective-permute-start(bf16[2,2,2,96,512]{4,3,0,1,2:T(8,128)(2,1)S(1)} %bitcast.318), channel_id=1, source_target_pairs={{0,2},{2,0},{4,6},{6,4},{8,10},{10,8},{12,14},{14,12},{16,18},{18,... | collective-permute-start | bytes 2359304 | tf_op jit(solution)/shard_map/ppermute | solution.py:435
  422.2 89.6 %collective-permute-start.58 = (bf16[2,2,2,96,1024]{4,3,0,1,2:T(8,128)(2,1)S(1)}, bf16[2,2,2,96,1024]{4,3,0,1,2:T(8,128)(2,1)}, u32[]{:S(2)}, u32[]{:S(2)}) collective-permute-start(bf16[2,2,2,96,1024]{4,3,0,1,2:T(8,128)(2,1)S(1)} %bitcast.305), channel_id=1, source_target_pairs={{0,8},{2,10},{4,12},{6,14},{8,0},{10,2},{12,4},{14,6},{16,24},{18,... | collective-permute-start | bytes 4718600 | tf_op jit(solution)/shard_map/ppermute | solution.py:435
  423.5 101.1 %collective-permute-start.38 = (bf16[2,2,2,96,1024]{4,3,2,0,1:T(8,128)(2,1)}, bf16[2,2,2,96,1024]{4,3,2,0,1:T(8,128)(2,1)}, u32[]{:S(2)}, u32[]{:S(2)}) collective-permute-start(bf16[2,2,2,96,1024]{4,3,2,0,1:T(8,128)(2,1)} %bitcast.260), channel_id=1, source_target_pairs={{0,4},{2,6},{4,0},{6,2},{8,12},{10,14},{12,8},{14,10},{16,20},{18,... | collective-permute-start | bytes 4718600 | tf_op jit(solution)/shard_map/ppermute | solution.py:435
  425.3 21.6 %collective-permute-start.51 = (bf16[2,2,96,512]{3,2,0,1:T(8,128)(2,1)}, bf16[2,2,96,512]{3,2,0,1:T(8,128)(2,1)}, u32[]{:S(2)}, u32[]{:S(2)}) collective-permute-start(bf16[2,2,96,512]{3,2,0,1:T(8,128)(2,1)} %fusion.45), channel_id=1, source_target_pairs={{0,2},{2,0},{4,6},{6,4},{8,10},{10,8},{12,14},{14,12},{16,18},{18,... | collective-permute-start | bytes 1179656 | tf_op jit(solution)/shard_map/ppermute | solution.py:435
  427.3 39.0 %collective-permute-start.47 = (bf16[2,2,96,512]{3,2,1,0:T(8,128)(2,1)}, bf16[2,2,96,512]{3,2,1,0:T(8,128)(2,1)}, u32[]{:S(2)}, u32[]{:S(2)}) collective-permute-start(bf16[2,2,96,512]{3,2,1,0:T(8,128)(2,1)} %fusion.44), channel_id=1, source_target_pairs={{0,8},{2,10},{4,12},{6,14},{8,0},{10,2},{12,4},{14,6},{16,24},{18,... | collective-permute-start | bytes 1179656 | tf_op jit(solution)/shard_map/ppermute | solution.py:435
  446.9 21.8 %collective-permute-start.43 = (bf16[2,2,96,512]{3,2,0,1:T(8,128)(2,1)S(1)}, bf16[2,2,96,512]{3,2,0,1:T(8,128)(2,1)S(1)}, u32[]{:S(2)}, u32[]{:S(2)}) collective-permute-start(bf16[2,2,96,512]{3,2,0,1:T(8,128)(2,1)S(1)} %copy-done.55), channel_id=1, source_target_pairs={{0,4},{2,6},{4,0},{6,2},{8,12},{10,14},{12,8},{14,10},{16,20},{18,... | collective-permute-start | bytes 1179656 | tf_op jit(solution)/shard_map/ppermute | solution.py:435
  466.3 65.2 %collective-permute-start.34 = (bf16[2,2,2,96,1024]{4,3,0,1,2:T(8,128)(2,1)}, bf16[2,2,2,96,1024]{4,3,0,1,2:T(8,128)(2,1)S(1)}, u32[]{:S(2)}, u32[]{:S(2)}) collective-permute-start(bf16[2,2,2,96,1024]{4,3,0,1,2:T(8,128)(2,1)} %bitcast.261), channel_id=1, source_target_pairs={{0,2},{2,0},{4,6},{6,4},{8,10},{10,8},{12,14},{14,12},{16,18},{18,... | collective-permute-start | bytes 4718600 | tf_op jit(solution)/shard_map/ppermute | solution.py:435
  509.7 13.5 %collective-permute-start.54 = (bf16[2,2,2,96,384]{4,3,2,1,0:T(8,128)(2,1)}, bf16[2,2,2,96,384]{4,3,2,1,0:T(8,128)(2,1)S(1)}, u32[]{:S(2)}, u32[]{:S(2)}) collective-permute-start(bf16[2,2,2,96,384]{4,3,2,1,0:T(8,128)(2,1)} %dynamic-slice_bitcast_fusion), channel_id=1, source_target_pairs={{0,2},{2,0},{4,6},{6,4},{8,10},{10,8},{12,14},{14,12},{16,18},{18,... | collective-permute-start | bytes 1769480 | tf_op jit(solution)/shard_map/ppermute | solution.py:435
  511.8 76.3 %collective-permute-start.28 = (f32[512,1536]{1,0:T(8,128)}, f32[512,1536]{1,0:T(8,128)}, u32[]{:S(2)}, u32[]{:S(2)}) collective-permute-start(f32[512,1536]{1,0:T(8,128)} %constant_dynamic-slice_fusion.12), channel_id=1, source_target_pairs={{0,1},{1,0},{2,3},{3,2},{4,5},{5,4},{6,7},{7,6},{8,9},{9,8},{10,11... | collective-permute-start | bytes 9437192 | tf_op jit(solution)/shard_map/ppermute | solution.py:409
  523.2 32.2 %collective-permute-start.59 = (bf16[2,2,96,1024]{3,2,0,1:T(8,128)(2,1)}, bf16[2,2,96,1024]{3,2,0,1:T(8,128)(2,1)}, u32[]{:S(2)}, u32[]{:S(2)}) collective-permute-start(bf16[2,2,96,1024]{3,2,0,1:T(8,128)(2,1)} %fusion.33), channel_id=1, source_target_pairs={{0,2},{2,0},{4,6},{6,4},{8,10},{10,8},{12,14},{14,12},{16,18},{18,... | collective-permute-start | bytes 2359304 | tf_op jit(solution)/shard_map/ppermute | solution.py:435
  531.4 27.2 %collective-permute-start.39 = (bf16[2,2,96,1024]{3,2,1,0:T(8,128)(2,1)}, bf16[2,2,96,1024]{3,2,1,0:T(8,128)(2,1)}, u32[]{:S(2)}, u32[]{:S(2)}) collective-permute-start(bf16[2,2,96,1024]{3,2,1,0:T(8,128)(2,1)} %fusion.32), channel_id=1, source_target_pairs={{0,8},{2,10},{4,12},{6,14},{8,0},{10,2},{12,4},{14,6},{16,24},{18,... | collective-permute-start | bytes 2359304 | tf_op jit(solution)/shard_map/ppermute | solution.py:435
  531.5 16.1 %collective-permute-start.56 = (bf16[2,96,384]{2,1,0:T(8,128)(2,1)S(1)}, bf16[2,96,384]{2,1,0:T(8,128)(2,1)S(1)}, u32[]{:S(2)}, u32[]{:S(2)}) collective-permute-start(bf16[2,96,384]{2,1,0:T(8,128)(2,1)S(1)} %fusion.55), channel_id=1, source_target_pairs={{0,8},{2,10},{4,12},{6,14},{8,0},{10,2},{12,4},{14,6},{16,24},{18,... | collective-permute-start | bytes 442376 | tf_op jit(solution)/shard_map/ppermute | solution.py:435
  553.4 14.1 %collective-permute-start.35 = (bf16[2,2,96,1024]{3,2,0,1:T(8,128)(2,1)}, bf16[2,2,96,1024]{3,2,0,1:T(8,128)(2,1)}, u32[]{:S(2)}, u32[]{:S(2)}) collective-permute-start(bf16[2,2,96,1024]{3,2,0,1:T(8,128)(2,1)} %fusion.31), channel_id=1, source_target_pairs={{0,4},{2,6},{4,0},{6,2},{8,12},{10,14},{12,8},{14,10},{16,20},{18,... | collective-permute-start | bytes 2359304 | tf_op jit(solution)/shard_map/ppermute | solution.py:435
  557.0 14.7 %collective-permute-start.60 = (bf16[2,96,1024]{2,1,0:T(8,128)(2,1)S(1)}, bf16[2,96,1024]{2,1,0:T(8,128)(2,1)S(1)}, u32[]{:S(2)}, u32[]{:S(2)}) collective-permute-start(bf16[2,96,1024]{2,1,0:T(8,128)(2,1)S(1)} %fusion.46), channel_id=1, source_target_pairs={{0,4},{2,6},{4,0},{6,2},{8,12},{10,14},{12,8},{14,10},{16,20},{18,... | collective-permute-start | bytes 1179656 | tf_op jit(solution)/shard_map/ppermute | solution.py:435
  560.2 22.9 %collective-permute-start.40 = (bf16[2,96,1024]{2,1,0:T(8,128)(2,1)S(1)}, bf16[2,96,1024]{2,1,0:T(8,128)(2,1)S(1)}, u32[]{:S(2)}, u32[]{:S(2)}) collective-permute-start(bf16[2,96,1024]{2,1,0:T(8,128)(2,1)S(1)} %fusion.42), channel_id=1, source_target_pairs={{0,16},{2,18},{4,20},{6,22},{8,24},{10,26},{12,28},{14,30},{16,0},... | collective-permute-start | bytes 1179656 | tf_op jit(solution)/shard_map/ppermute | solution.py:435
  569.1 18.1 %collective-permute-start.36 = (bf16[2,96,1024]{2,1,0:T(8,128)(2,1)S(1)}, bf16[2,96,1024]{2,1,0:T(8,128)(2,1)S(1)}, u32[]{:S(2)}, u32[]{:S(2)}) collective-permute-start(bf16[2,96,1024]{2,1,0:T(8,128)(2,1)S(1)} %fusion.41), channel_id=1, source_target_pairs={{0,8},{2,10},{4,12},{6,14},{8,0},{10,2},{12,4},{14,6},{16,24},{18,... | collective-permute-start | bytes 1179656 | tf_op jit(solution)/shard_map/ppermute | solution.py:435
  571.9 16.1 %collective-permute-start.61 = (bf16[96,1024]{1,0:T(8,128)(2,1)S(1)}, bf16[96,1024]{1,0:T(8,128)(2,1)S(1)}, u32[]{:S(2)}, u32[]{:S(2)}) collective-permute-start(bf16[96,1024]{1,0:T(8,128)(2,1)S(1)} %fusion.53), channel_id=1, source_target_pairs={{0,16},{2,18},{4,20},{6,22},{8,24},{10,26},{12,28},{14,30},{16,0},... | collective-permute-start | bytes 589832 | tf_op jit(solution)/shard_map/ppermute | solution.py:435
  583.2 10.1 %collective-permute-start.41 = (bf16[96,1024]{1,0:T(8,128)(2,1)S(1)}, bf16[96,1024]{1,0:T(8,128)(2,1)S(1)}, u32[]{:S(2)}, u32[]{:S(2)}) collective-permute-start(bf16[96,1024]{1,0:T(8,128)(2,1)S(1)} %fusion.49), channel_id=1, source_target_pairs={{0,2},{2,0},{4,6},{6,4},{8,10},{10,8},{12,14},{14,12},{16,18},{18,... | collective-permute-start | bytes 589832 | tf_op jit(solution)/shard_map/ppermute | solution.py:435
  (125 other events, 1327.7 us)

commit v5 on v4

--- a/solution.py
+++ b/solution.py
@@ -437,8 +437,8 @@
 
 def place_kernel(table, *refs):
     sources, (out, buffer, arrived, left) = refs[:-4], refs[-4:]
-    turns, size = len(sources) // 2, out.shape[0]
-    half = size // 2
+    turns, size = len(sources) // 4, out.shape[0]
+    part = size // 4
     width = sources[0].shape[2]
 
     def arrival(turn, source, block, target):
@@ -451,19 +451,18 @@
         for turn in range(turns):
             block = table[turn, target]
 
-            @pl.when(block < half)
-            def from_own():
-                arrival(turn, sources[2 * turn], block, target).start()
-
-            @pl.when(block >= half)
-            def from_other():
-                arrival(turn, sources[2 * turn + 1], block - half, target).start()
+            for place in range(4):
+
+                @pl.when((block >= place * part) & (block < (place + 1) * part))
+                def from_part():
+                    source = sources[4 * turn + place]
+                    arrival(turn, source, block - place * part, target).start()
 
         return unused
 
     def start_out(target, unused):
         for turn in range(turns):
-            arrival(turn, sources[2 * turn], 0, target).wait()
+            arrival(turn, sources[4 * turn], 0, target).wait()
         pltpu.make_async_copy(buffer.at[target], out.at[target], left.at[target]).start()
         return unused
 
@@ -477,15 +476,16 @@
 
 
 def gather_stages(pieces, first_stage, last_stage):
-    orders = stage_orders(lax.axis_size("dp"))
+    size = lax.axis_size("dp")
+    bits = size.bit_length() - 1
     for stage in range(first_stage, last_stage):
         joined = []
-        for piece, order in zip(pieces, orders):
-            other = partner(piece, order[::-1][stage])
-            if stage == len(order) - 1:
-                joined.append((piece, other))
+        for parts, order in zip(pieces, stage_orders(size)):
+            others = [partner(part, order[::-1][stage]) for part in parts]
+            if stage < bits - 2:
+                joined.append([jnp.concatenate(parts + others, axis=0)])
             else:
-                joined.append(jnp.concatenate([piece, other], axis=0))
+                joined.append(parts + others)
         pieces = joined
     return pieces
 
@@ -493,7 +493,7 @@
 def split_shard(shard):
     turns = len(stage_orders(lax.axis_size("dp")))
     width = shard.shape[1] // turns
-    return [shard[None, :, turn * width : (turn + 1) * width] for turn in range(turns)]
+    return [[shard[None, :, turn * width : (turn + 1) * width]] for turn in range(turns)]
 
 
 def place_rows(pieces):
@@ -571,14 +571,6 @@
     out_proj,
     cotangent,
 ):
-    half_rows = tokens.shape[0]
-    model_width = tokens.shape[1]
-    tensor_place = lax.axis_index("tensor")
-    own_segment = lax.dynamic_slice_in_dim(segment_ids, tensor_place * half_rows, half_rows)
-    own_live = (own_segment >= 0).astype(F32)[:, None]
-    own_rows = tokens.astype(F32)
-    row_scale = lax.rsqrt(jnp.mean(own_rows * own_rows, axis=1, keepdims=True) + EPSILON)
-    normed_own = (own_rows * row_scale * norm_gain[None, :]).astype(BF16)
     width, _, inner_dev = in_gate_inner.shape
     state_dim = in_state.shape[2]
     heads_dev = in_step.shape[1]
@@ -595,10 +587,51 @@
     )
     bits = lax.axis_size("dp").bit_length() - 1
     first_pieces = gather_stages(split_shard(first_shard), 0, bits - 1)
+    held_back = (
+        in_gate_inner,
+        out_proj,
+        tokens,
+        cotangent,
+        segment_ids,
+        norm_gain,
+        conv_inner,
+        conv_inner_bias,
+        conv_state,
+        conv_state_bias,
+        step_bias,
+        decay_log,
+        skip_gain,
+        gate_gain,
+    )
+    first_pieces, held_back = lax.optimization_barrier((first_pieces, held_back))
+    (
+        in_gate_inner,
+        out_proj,
+        tokens,
+        cotangent,
+        segment_ids,
+        norm_gain,
+        conv_inner,
+        conv_inner_bias,
+        conv_state,
+        conv_state_bias,
+        step_bias,
+        decay_log,
+        skip_gain,
+        gate_gain,
+    ) = held_back
     later_shard = jnp.concatenate([in_gate_inner[:, 0], out_proj.T], axis=1)
-    first_pieces, later_pieces = lax.optimization_barrier((first_pieces, split_shard(later_shard)))
+    later_pieces = split_shard(later_shard)
     first_pieces = gather_stages(first_pieces, bits - 1, bits)
     later_pieces = gather_stages(later_pieces, 0, bits)
+    half_rows = tokens.shape[0]
+    model_width = tokens.shape[1]
+    tensor_place = lax.axis_index("tensor")
+    own_segment = lax.dynamic_slice_in_dim(segment_ids, tensor_place * half_rows, half_rows)
+    own_live = (own_segment >= 0).astype(F32)[:, None]
+    own_rows = tokens.astype(F32)
+    row_scale = lax.rsqrt(jnp.mean(own_rows * own_rows, axis=1, keepdims=True) + EPSILON)
+    normed_own = (own_rows * row_scale * norm_gain[None, :]).astype(BF16)
     first_weights = place_rows(first_pieces)
     normed = gather_pair(normed_own, tensor_place)
     first_proj = dot(normed, first_weights)

time: 630 us -> 607 us (0.963)
  waiting for transfers between devices: 171 us -> 146 us
  starting transfers between devices: 59.1 us -> 73.8 us
    ppermute x56 -> x62, waiting for transfers between devices: 171 us -> 146 us  [partner(): return lax.ppermute(values, 'dp', [(i, i ^ 1 << bit) for i in range(size)])]
    ppermute x56 -> x62, starting transfers between devices: 58.1 us -> 73.3 us  [partner(): return lax.ppermute(values, 'dp', [(i, i ^ 1 << bit) for i in range(size)])]
    mul x1 -> x0, other arithmetic: 13.3 us -> none  [shards(): grad_mixed = grad_gated * (gate_proj * gate_sigmoid)]
    convert_element_type x0 -> x1, other arithmetic: none -> 13.2 us  [shards(): low_gate = (grad_gated * mixed * (gate_sigmoid * (1.0 + gate_proj * (1.0...]
    concatenate x15 -> x12, other arithmetic: 15.8 us -> 9.51 us  [gather_stages(): joined.append([jnp.concatenate(parts + others, axis=0)])]
    unnamed x232 -> x256, local copies, waits for them, and re-layouts: 22.1 us -> 18.1 us
  transfers between devices with their start and end apart: 62 -> 68, of which waited for: 33 -> 33; matrix products, arithmetic and copies ran while one was open for 25% -> 27% of each run, Pallas kernels for 5% -> 6%
where the time goes in v5:
time: 607 us; the launch traced here: 601 us
  waiting for transfers between devices  146 us (24%)
  Pallas kernels  104 us (17%)
  other arithmetic  93.6 us (15%)
  matrix products  93 us (15%)
  local copies, waits for them, and re-layouts  82.5 us (14%)
  starting transfers between devices  73.8 us (12%)
    ppermute x62, waiting for transfers between devices, partner(): return lax.ppermute(values, 'dp', [(i, i ^ 1 << bit) for i in range(size)])  146 us
    ppermute x62, starting transfers between devices, partner(): return lax.ppermute(values, 'dp', [(i, i ^ 1 << bit) for i in range(size)])  73.3 us
    pallas_call x1, Pallas kernels, ssd_backward(): pl.pallas_call(ssd_backward_kernel, grid=(groups,), in_specs=[lanes_spec(...  61.1 us
    pallas_call x1, Pallas kernels, ssd_forward(): pl.pallas_call(ssd_forward_kernel, grid=(groups,), in_specs=[lanes_spec(a...  27.4 us
    dot_general x3, matrix products, dot_nt(): lax.dot_general(a, b, (((1,), (1,)), ((), ())), preferred_element_type=F32)  22.8 us
    dot_general x2, matrix products, dot(): return jnp.dot(a, b, preferred_element_type=F32)  19.4 us
    unnamed x256, local copies, waits for them, and re-layouts  18.1 us
    pallas_call x2, Pallas kernels, place_rows(): pl.pallas_call(place_kernel, in_specs=[pl.BlockSpec(memory_space=pltpu.SM...  15.8 us
  transfers between devices with their start and end apart: 68, of which 33 were waited for; matrix products, arithmetic and copies ran while one was open for 27% of the time, Pallas kernels for 6%

profile of v5, /device:TPU:0, one launch (start us, length us, event | category | flops | bytes accessed | tf_op | source)
XLA Modules:
  0.0 600.9 jit_solution(7932824387480609094)
XLA Ops:
  2.5 4.1 collective-permute-start
  17.3 2.7 collective-permute-start.4
  21.6 6.5 %collective-permute-done.1 = bf16[2,96,640]{2,1,0:T(8,128)(2,1)S(1)} collective-permute-done((bf16[2,96,640]{2,1,0:T(8,128)(2,1)S(1)}, bf16[2,96,640]{2,1,0:T(8,128)(2,1)S(1)}, u32[]{:S(2)}, u32[]{:S(2)}) %collective-permute-start.1) | collective-permute-done | bytes 245792 | tf_op jit(solution)/shard_map/ppermute | solution.py:435
  50.0 2.6 collective-permute-start.16
  56.2 6.3 %collective-permute-done.16 = bf16[1,96,1024]{2,1,0:T(8,128)(2,1)S(1)} collective-permute-done((bf16[1,96,1024]{2,1,0:T(8,128)(2,1)S(1)}, bf16[1,96,1024]{2,1,0:T(8,128)(2,1)S(1)}, u32[]{:S(2)}, u32[]{:S(2)}) %collective-permute-start.16) | collective-permute-done | bytes 196640 | tf_op jit(solution)/shard_map/ppermute | solution.py:435
  63.1 7.3 %collective-permute-done.21 = bf16[1,96,1024]{2,1,0:T(8,128)(2,1)S(1)} collective-permute-done((bf16[1,96,1024]{2,1,0:T(8,128)(2,1)S(1)}, bf16[1,96,1024]{2,1,0:T(8,128)(2,1)S(1)}, u32[]{:S(2)}, u32[]{:S(2)}) %collective-permute-start.21) | collective-permute-done | bytes 196640 | tf_op jit(solution)/shard_map/ppermute | solution.py:435
  80.6 3.8 collective-permute-done.12.refs_6_
  85.7 5.6 collective-permute-done.13.refs_7_
  101.7 7.3 %collective-permute-done.15.refs_11_ = bf16[4,96,640]{2,1,0:T(8,128)(2,1)} collective-permute-done((bf16[4,96,640]{2,1,0:T(8,128)(2,1)}, bf16[4,96,640]{2,1,0:T(8,128)(2,1)}, u32[]{:S(2)}, u32[]{:S(2)}) %collective-permute-start.15) | collective-permute-done | bytes 491552 | tf_op jit(solution)/shard_map/ppermute | solution.py:435
  109.0 6.8 %place_rows.2 = bf16[16,96,1920]{2,1,0:T(8,128)(2,1)} custom-call(s32[3,16]{1,0:T(4,128)} %pad_add_fusion.1.table, bf16[4,96,640]{2,1,0:T(8,128)(2,1)} %pad_maximum_fusion.17.refs_0_, bf16[4,96,640]{2,1,0:T(8,128)(2,1)} %collective-permute-done.2.refs_1_, bf16[4,96,640]{2,1,0:T(8,128)(2,1)} %copy-done.66, bf16[4,96,640]{2,1,0:T(8,128)(2,1)} %copy-done.67, ...), custom_call_target="tpu_custom_call" | custom-call | bytes 11796480 | tf_op jit(solution)/shard_map/place_rows/pallas_call | solution.py:510
  127.7 6.6 %fusion.75.xr = f32[1024,1920]{1,0:T(8,128)S(1)} fusion(bf16[1536,1920]{1,0:T(8,128)(2,1)S(1)} %bitcast.284, bf16[512,1536]{1,0:T(8,128)(2,1)S(1)} %get-tuple-element.200, bf16[512,1536]{1,0:T(8,128)(2,1)S(1)} %get-tuple-element.199), kind=kOutput, calls=%fused_computation.309 | convolution fusion | flops 6046089216 | bytes 16908288 | tf_op jit(solution)/shard_map/dot_general | solution.py:35
  142.1 2.9 copy.283
  147.6 4.0 multiply_convert_fusion.2
  170.0 27.4 %ssd_forward.1 = (f32[1024,1536]{1,0:T(8,128)}, bf16[1024,1536]{1,0:T(8,128)(2,1)}) custom-call(f32[1024,1920]{1,0:T(8,128)} %copy-done.27, f32[4,1536]{1,0:T(4,128)} %taps.1, f32[1,1536]{1,0:T(1,128)} %broadcast_in_dim.26.bias, f32[1,1536]{1,0:T(1,128)} %broadcast_in_dim_reshape.2.skip, f32[3,1024,128]{2,1,0:T(8,128)} %pad_maximum_fusion.5.masks, ...), custom_call_target="tpu_custom_call" | custom-call | flops 26172456960 | bytes 18874368 | tf_op jit(solution)/shard_map/ssd_forward/pallas_call | solution.py:298
  198.5 3.7 broadcast_select_fusion.1
  202.3 9.0 %place_rows.3 = bf16[16,96,3072]{2,1,0:T(8,128)(2,1)} custom-call(s32[3,16]{1,0:T(4,128)} %pad_add_fusion.1.table, bf16[4,96,1024]{2,1,0:T(8,128)(2,1)} %pad_maximum_fusion.12.refs_0_, bf16[4,96,1024]{2,1,0:T(8,128)(2,1)} %collective-permute-done.18.refs_1_, bf16[4,96,1024]{2,1,0:T(8,128)(2,1)} %collective-permute-done.19.refs_2_, ...), custom_call_target="tpu_custom_call" | custom-call | bytes 18874368 | tf_op jit(solution)/shard_map/place_rows/pallas_call | solution.py:510
  211.3 12.7 %multiply_reduce_fusion.2 = (f32[1024]{0:T(1024)S(1)}, f32[1024,1536]{1,0:T(8,128)}, f32[1024,1536]{1,0:T(8,128)}) fusion(f32[1024,1536]{1,0:T(8,128)} %get-tuple-element.66, bf16[1536,3072]{1,0:T(8,128)(2,1)} %bitcast.276, bf16[512,1536]{1,0:T(8,128)(2,1)S(1)} %copy-done.46, bf16[512,1536]{1,0:T(8,128)(2,1)S(1)} %copy-done.42), kind=kOutput, calls=%fused_computation.15 | convolution fusion | flops 4849138688 | bytes 26742784 | tf_op jit(solution)/shard_map/dot_general | solution.py:35
  226.5 13.7 %multiply_reduce_fusion = (f32[1536]{0:T(1024)}, f32[1024]{0:T(1024)S(1)}, f32[1024,1536]{1,0:T(8,128)}) fusion(f32[1024,1536]{1,0:T(8,128)} %get-tuple-element.181, f32[1024]{0:T(1024)S(1)} %get-tuple-element.234, f32[1536]{0:T(1024)S(1)} %copy-done.107, bf16[1536,3072]{1,0:T(8,128)(2,1)} %bitcast.277, bf16[512,1536]{1,0:T(8,128)(2,1)} %get-tuple-element.198, ...), kind=kOutput, calls=%fused_computation.9 | convolution fusion | flops 4847564288 | bytes 20467712 | tf_op jit(solution)/shard_map/td,dc->tc/dot_general | solution.py:687
  240.1 7.3 %convolution_convert_fusion.1 = bf16[1536,1536]{1,0:T(8,128)(2,1)} fusion(bf16[512,1536]{1,0:T(8,128)(2,1)S(1)} %copy-done.50, bf16[512,1536]{1,0:T(8,128)(2,1)S(1)} %copy-done.49, f32[1024,1536]{1,0:T(8,128)S(1)} %copy-done.18, f32[1536]{0:T(1024)S(1)} %copy-done.107, f32[1024]{0:T(1024)S(1)} %get-tuple-element.234), kind=kOutput, calls=%fused_computation.1 | convolution fusion | flops 4845207552 | bytes 14166016 | tf_op jit(solution)/shard_map/td,tc->dc/dot_general | solution.py:684
  249.8 13.2 %multiply_convert_fusion = (bf16[1024,1536]{1,0:T(8,128)(2,1)S(1)}, f32[1024,1536]{1,0:T(8,128)}) fusion(f32[1024,1536]{1,0:T(8,128)} %get-tuple-element.250, f32[1024,1536]{1,0:T(8,128)} %get-tuple-element.66, f32[1024]{0:T(1024)S(1)} %broadcast_multiply_fusion.5, f32[1024,1536]{1,0:T(8,128)} %get-tuple-element.181, f32[1024,1536]{1,0:T(8,128)} %get-tuple-element.251, ...), kind=kLoop, calls=%fused_computation.11 | loop fusion | flops 26738688 | bytes 34621440 | tf_op jit(solution)/shard_map/convert_element_type | solution.py:698
  263.1 6.7 %convolution_convert_fusion.2 = bf16[1536,1536]{1,0:T(8,128)(2,1)} fusion(bf16[1024,1536]{1,0:T(8,128)(2,1)S(1)} %get-tuple-element.186, bf16[512,1536]{1,0:T(8,128)(2,1)S(1)} %copy-done.46, bf16[512,1536]{1,0:T(8,128)(2,1)S(1)} %copy-done.42), kind=kOutput, calls=%fused_computation.2 | convolution fusion | flops 4840488960 | bytes 11010048 | tf_op jit(solution)/shard_map/td,tc->dc/dot_general | solution.py:700
  269.8 61.1 %ssd_backward.1 = (bf16[1024,1536]{1,0:T(8,128)(2,1)}, f32[1024,128]{1,0:T(8,128)}, f32[1024,128]{1,0:T(8,128)}, f32[1024,128]{1,0:T(8,128)}, f32[1024,128]{1,0:...) custom-call(f32[1024,1920]{1,0:T(8,128)} %copy-done.27, ...), custom_call_target="tpu_custom_call" | custom-call | flops 58384711680 | bytes 25165824 | tf_op jit(solution)/shard_map/ssd_backward/pallas_call | solution.py:349
  333.0 10.8 %fusion.5 = f32[1024,1536]{1,0:T(8,128)} fusion(bf16[1536,3072]{1,0:T(8,128)(2,1)} %bitcast.278, f32[1024,1536]{1,0:T(8,128)} %get-tuple-element.181, f32[1536]{0:T(1024)S(1)} %copy-done.107, f32[1024]{0:T(1024)S(1)} %get-tuple-element.234), kind=kOutput, calls=%fused_computation.22 | convolution fusion | flops 4836556800 | bytes 17311744 | tf_op jit(solution)/shard_map/tc,dc->td/dot_general | solution.py:676
  344.4 9.4 %fusion.1 = f32[1024,1536]{1,0:T(8,128)} fusion(bf16[1024,1536]{1,0:T(8,128)(2,1)S(1)} %copy-done.117, bf16[1536,1920]{1,0:T(8,128)(2,1)} %bitcast.282), kind=kOutput, calls=%fused_computation.18 | convolution fusion | flops 4831838208 | bytes 14155776 | tf_op jit(solution)/shard_map/dot_general | solution.py:39
  353.8 7.2 %convolution_convert_fusion = bf16[1536,1536]{1,0:T(8,128)(2,1)} fusion(bf16[1024,1536]{1,0:T(8,128)(2,1)S(1)} %copy-done.117, bf16[512,1536]{1,0:T(8,128)(2,1)S(1)} %copy-done.47, bf16[512,1536]{1,0:T(8,128)(2,1)S(1)} %copy-done.43), kind=kOutput, calls=%fused_computation | convolution fusion | flops 4840488960 | bytes 11010048 | tf_op jit(solution)/shard_map/td,tc->dc/dot_general | solution.py:740
  372.5 3.8 constant_dynamic-slice_fusion.13
  378.2 2.7 fusion.81
  397.2 3.8 collective-permute-done.56
  414.7 3.3 fusion.23
  421.8 10.1 %add_add_fusion = f32[1024,1536]{1,0:T(8,128)} fusion(f32[1024,1536]{1,0:T(8,128)S(1)} %fusion.23, f32[1024,1536]{1,0:T(8,128)} %fusion.1, bf16[1024,1536]{1,0:T(8,128)(2,1)} %copy-done.28, bf16[1536,3072]{1,0:T(8,128)(2,1)S(1)} %bitcast.281), kind=kOutput, calls=%fused_computation.10 | convolution fusion | flops 4834983936 | bytes 26738688 | tf_op jit(solution)/shard_map/dot_general | solution.py:39
  431.9 3.9 constant_dynamic-slice_fusion.12
  437.6 8.0 %collective-permute-done.53 = bf16[2,2,96,512]{3,2,1,0:T(8,128)(2,1)} collective-permute-done((bf16[2,2,96,512]{3,2,1,0:T(8,128)(2,1)}, bf16[2,2,96,512]{3,2,1,0:T(8,128)(2,1)}, u32[]{:S(2)}, u32[]{:S(2)}) %collective-permute-start.53) | collective-permute-done | bytes 393248 | tf_op jit(solution)/shard_map/ppermute | solution.py:435
  449.5 3.9 collective-permute-done.58
  455.2 7.5 %collective-permute-done.54 = bf16[2,96,512]{2,1,0:T(8,128)(2,1)S(1)} collective-permute-done((bf16[2,96,512]{2,1,0:T(8,128)(2,1)S(1)}, bf16[2,96,512]{2,1,0:T(8,128)(2,1)S(1)}, u32[]{:S(2)}, u32[]{:S(2)}) %collective-permute-start.54) | collective-permute-done | bytes 196640 | tf_op jit(solution)/shard_map/ppermute | solution.py:435
  462.8 5.5 collective-permute-done.50
  468.7 5.7 collective-permute-done.59
  475.9 6.8 %collective-permute-done.55 = bf16[96,512]{1,0:T(8,128)(2,1)S(1)} collective-permute-done((bf16[96,512]{1,0:T(8,128)(2,1)S(1)}, bf16[96,512]{1,0:T(8,128)(2,1)S(1)}, u32[]{:S(2)}, u32[]{:S(2)}) %collective-permute-start.55) | collective-permute-done | bytes 98336 | tf_op jit(solution)/shard_map/ppermute | solution.py:435
  484.3 5.0 collective-permute-done.51
  493.3 9.2 %collective-permute-done.60 = bf16[2,2,2,96,384]{4,3,2,1,0:T(8,128)(2,1)S(1)} collective-permute-done((bf16[2,2,2,96,384]{4,3,2,1,0:T(8,128)(2,1)S(1)}, bf16[2,2,2,96,384]{4,3,2,1,0:T(8,128)(2,1)S(1)}, u32[]{:S(2)}, u32[]{:S(2)}) %collective-permute-start.60) | collective-permute-done | bytes 589856 | tf_op jit(solution)/shard_map/ppermute | solution.py:435
  512.7 14.0 %collective-permute-done.62 = bf16[2,96,384]{2,1,0:T(8,128)(2,1)S(1)} collective-permute-done((bf16[2,96,384]{2,1,0:T(8,128)(2,1)S(1)}, bf16[2,96,384]{2,1,0:T(8,128)(2,1)S(1)}, u32[]{:S(2)}, u32[]{:S(2)}) %collective-permute-start.62) | collective-permute-done | bytes 147488 | tf_op jit(solution)/shard_map/ppermute | solution.py:435
  528.5 4.2 collective-permute-done.63
  539.9 7.2 %collective-permute-done.41 = bf16[2,2,96,1024]{3,2,0,1:T(8,128)(2,1)} collective-permute-done((bf16[2,2,96,1024]{3,2,0,1:T(8,128)(2,1)}, bf16[2,2,96,1024]{3,2,0,1:T(8,128)(2,1)}, u32[]{:S(2)}, u32[]{:S(2)}) %collective-permute-start.41) | collective-permute-done | bytes 786464 | tf_op jit(solution)/shard_map/ppermute | solution.py:435
  552.1 10.4 %collective-permute-done.46 = bf16[2,96,1024]{2,1,0:T(8,128)(2,1)S(1)} collective-permute-done((bf16[2,96,1024]{2,1,0:T(8,128)(2,1)S(1)}, bf16[2,96,1024]{2,1,0:T(8,128)(2,1)S(1)}, u32[]{:S(2)}, u32[]{:S(2)}) %collective-permute-start.46) | collective-permute-done | bytes 393248 | tf_op jit(solution)/shard_map/ppermute | solution.py:435
  564.0 2.6 collective-permute-done.42
  567.6 5.3 fusion.20
  577.5 3.0 collective-permute-done.36
  589.9 2.7 collective-permute-start.39
  592.6 5.0 fusion.11
  (589 shorter events, 215.7 us)
Async XLA Ops:
  2.5 13.1 %collective-permute-start = (bf16[1,96,640]{2,1,0:T(8,128)(2,1)S(1)}, bf16[1,96,640]{2,1,0:T(8,128)(2,1)S(1)}, u32[]{:S(2)}, u32[]{:S(2)}) collective-permute-start(bf16[1,96,640]{2,1,0:T(8,128)(2,1)S(1)} %get-tuple-element.226), channel_id=1, source_target_pairs={{0,16},{2,18},{4,20},{6,22},{8,24},{10,26},{12,28},{14,30},{16,0},... | collective-permute-start | bytes 368648 | tf_op jit(solution)/shard_map/ppermute | solution.py:435
  15.6 12.5 %collective-permute-start.1 = (bf16[2,96,640]{2,1,0:T(8,128)(2,1)S(1)}, bf16[2,96,640]{2,1,0:T(8,128)(2,1)S(1)}, u32[]{:S(2)}, u32[]{:S(2)}) collective-permute-start(bf16[2,96,640]{2,1,0:T(8,128)(2,1)S(1)} %pad_maximum_fusion.23), channel_id=1, source_target_pairs={{0,8},{2,10},{4,12},{6,14},{8,0},{10,2},{12,4},{14,6},{16,24},{18,... | collective-permute-start | bytes 737288 | tf_op jit(solution)/shard_map/ppermute | solution.py:435
  17.3 13.4 %collective-permute-start.4 = (bf16[2,96,640]{2,1,0:T(8,128)(2,1)S(1)}, bf16[2,96,640]{2,1,0:T(8,128)(2,1)S(1)}, u32[]{:S(2)}, u32[]{:S(2)}) collective-permute-start(bf16[2,96,640]{2,1,0:T(8,128)(2,1)S(1)} %pad_maximum_fusion.24), channel_id=1, source_target_pairs={{0,16},{2,18},{4,20},{6,22},{8,24},{10,26},{12,28},{14,30},{16,0},... | collective-permute-start | bytes 737288 | tf_op jit(solution)/shard_map/ppermute | solution.py:435
  29.0 12.2 %collective-permute-start.2 = (bf16[4,96,640]{2,1,0:T(8,128)(2,1)}, bf16[4,96,640]{2,1,0:T(8,128)(2,1)}, u32[]{:S(2)}, u32[]{:S(2)}) collective-permute-start(bf16[4,96,640]{2,1,0:T(8,128)(2,1)} %pad_maximum_fusion.17.refs_0_), channel_id=1, source_target_pairs={{0,4},{2,6},{4,0},{6,2},{8,12},{10,14},{12,8},{14,10},{16,20},{18,... | collective-permute-start | bytes 1474568 | tf_op jit(solution)/shard_map/ppermute | solution.py:435
  31.1 12.1 %collective-permute-start.8 = (bf16[4,96,640]{2,1,0:T(8,128)(2,1)S(1)}, bf16[4,96,640]{2,1,0:T(8,128)(2,1)}, u32[]{:S(2)}, u32[]{:S(2)}) collective-permute-start(bf16[4,96,640]{2,1,0:T(8,128)(2,1)S(1)} %pad_maximum_fusion.19.refs_8_), channel_id=1, source_target_pairs={{0,2},{2,0},{4,6},{6,4},{8,10},{10,8},{12,14},{14,12},{16,18},{18,... | collective-permute-start | bytes 1474568 | tf_op jit(solution)/shard_map/ppermute | solution.py:435
  44.2 31.6 %collective-permute-start.10 = (bf16[4,96,640]{2,1,0:T(8,128)(2,1)}, bf16[4,96,640]{2,1,0:T(8,128)(2,1)S(1)}, u32[]{:S(2)}, u32[]{:S(2)}) collective-permute-start(bf16[4,96,640]{2,1,0:T(8,128)(2,1)} %pad_maximum_fusion.17.refs_0_), channel_id=1, source_target_pairs={{0,2},{2,0},{4,6},{6,4},{8,10},{10,8},{12,14},{14,12},{16,18},{18,... | collective-permute-start | bytes 1474568 | tf_op jit(solution)/shard_map/ppermute | solution.py:435
  45.9 31.9 %collective-permute-start.11 = (bf16[4,96,640]{2,1,0:T(8,128)(2,1)}, bf16[4,96,640]{2,1,0:T(8,128)(2,1)S(1)}, u32[]{:S(2)}, u32[]{:S(2)}) collective-permute-start(bf16[4,96,640]{2,1,0:T(8,128)(2,1)} %collective-permute-done.2.refs_1_), channel_id=1, source_target_pairs={{0,2},{2,0},{4,6},{6,4},{8,10},{10,8},{12,14},{14,12},{16,18},{18,... | collective-permute-start | bytes 1474568 | tf_op jit(solution)/shard_map/ppermute | solution.py:435
  47.8 76.8 %collective-permute-start.9 = (bf16[512,1536]{1,0:T(8,128)(2,1)}, bf16[512,1536]{1,0:T(8,128)(2,1)}, u32[]{:S(2)}, u32[]{:S(2)}) collective-permute-start(bf16[512,1536]{1,0:T(8,128)(2,1)} %fusion.14), channel_id=1, source_target_pairs={{0,1},{1,0},{2,3},{3,2},{4,5},{5,4},{6,7},{7,6},{8,9},{9,8},{10,11... | collective-permute-start | bytes 4718600 | tf_op jit(solution)/shard_map/ppermute | solution.py:409
  50.0 12.5 %collective-permute-start.16 = (bf16[1,96,1024]{2,1,0:T(8,128)(2,1)S(1)}, bf16[1,96,1024]{2,1,0:T(8,128)(2,1)S(1)}, u32[]{:S(2)}, u32[]{:S(2)}) collective-permute-start(bf16[1,96,1024]{2,1,0:T(8,128)(2,1)S(1)} %get-tuple-element.224), channel_id=1, source_target_pairs={{0,16},{2,18},{4,20},{6,22},{8,24},{10,26},{12,28},{14,30},{16,0},... | collective-permute-start | bytes 589832 | tf_op jit(solution)/shard_map/ppermute | solution.py:435
  52.6 17.8 %collective-permute-start.21 = (bf16[1,96,1024]{2,1,0:T(8,128)(2,1)S(1)}, bf16[1,96,1024]{2,1,0:T(8,128)(2,1)S(1)}, u32[]{:S(2)}, u32[]{:S(2)}) collective-permute-start(bf16[1,96,1024]{2,1,0:T(8,128)(2,1)S(1)} %get-tuple-element.223), channel_id=1, source_target_pairs={{0,2},{2,0},{4,6},{6,4},{8,10},{10,8},{12,14},{14,12},{16,18},{18,... | collective-permute-start | bytes 589832 | tf_op jit(solution)/shard_map/ppermute | solution.py:435
  70.4 14.1 %collective-permute-start.12 = (bf16[4,96,640]{2,1,0:T(8,128)(2,1)S(1)}, bf16[4,96,640]{2,1,0:T(8,128)(2,1)S(1)}, u32[]{:S(2)}, u32[]{:S(2)}) collective-permute-start(bf16[4,96,640]{2,1,0:T(8,128)(2,1)S(1)} %copy-done.36), channel_id=1, source_target_pairs={{0,4},{2,6},{4,0},{6,2},{8,12},{10,14},{12,8},{14,10},{16,20},{18,... | collective-permute-start | bytes 1474568 | tf_op jit(solution)/shard_map/ppermute | solution.py:435
  73.7 17.7 %collective-permute-start.13 = (bf16[4,96,640]{2,1,0:T(8,128)(2,1)S(1)}, bf16[4,96,640]{2,1,0:T(8,128)(2,1)S(1)}, u32[]{:S(2)}, u32[]{:S(2)}) collective-permute-start(bf16[4,96,640]{2,1,0:T(8,128)(2,1)S(1)} %copy-done.65), channel_id=1, source_target_pairs={{0,4},{2,6},{4,0},{6,2},{8,12},{10,14},{12,8},{14,10},{16,20},{18,... | collective-permute-start | bytes 1474568 | tf_op jit(solution)/shard_map/ppermute | solution.py:435
  75.8 18.6 %collective-permute-start.14 = (bf16[4,96,640]{2,1,0:T(8,128)(2,1)S(1)}, bf16[4,96,640]{2,1,0:T(8,128)(2,1)S(1)}, u32[]{:S(2)}, u32[]{:S(2)}) collective-permute-start(bf16[4,96,640]{2,1,0:T(8,128)(2,1)S(1)} %copy-done.38), channel_id=1, source_target_pairs={{0,8},{2,10},{4,12},{6,14},{8,0},{10,2},{12,4},{14,6},{16,24},{18,... | collective-permute-start | bytes 1474568 | tf_op jit(solution)/shard_map/ppermute | solution.py:435
  77.8 31.2 %collective-permute-start.15 = (bf16[4,96,640]{2,1,0:T(8,128)(2,1)}, bf16[4,96,640]{2,1,0:T(8,128)(2,1)}, u32[]{:S(2)}, u32[]{:S(2)}) collective-permute-start(bf16[4,96,640]{2,1,0:T(8,128)(2,1)} %collective-permute-done.8.refs_9_), channel_id=1, source_target_pairs={{0,8},{2,10},{4,12},{6,14},{8,0},{10,2},{12,4},{14,6},{16,24},{18,... | collective-permute-start | bytes 1474568 | tf_op jit(solution)/shard_map/ppermute | solution.py:435
  84.5 31.7 %collective-permute-start.17 = (bf16[2,96,1024]{2,1,0:T(8,128)(2,1)}, bf16[2,96,1024]{2,1,0:T(8,128)(2,1)}, u32[]{:S(2)}, u32[]{:S(2)}) collective-permute-start(bf16[2,96,1024]{2,1,0:T(8,128)(2,1)} %pad_maximum_fusion.20), channel_id=1, source_target_pairs={{0,8},{2,10},{4,12},{6,14},{8,0},{10,2},{12,4},{14,6},{16,24},{18,... | collective-permute-start | bytes 1179656 | tf_op jit(solution)/shard_map/ppermute | solution.py:435
  91.4 27.4 %collective-permute-start.22 = (bf16[2,96,1024]{2,1,0:T(8,128)(2,1)}, bf16[2,96,1024]{2,1,0:T(8,128)(2,1)}, u32[]{:S(2)}, u32[]{:S(2)}) collective-permute-start(bf16[2,96,1024]{2,1,0:T(8,128)(2,1)} %pad_maximum_fusion.21), channel_id=1, source_target_pairs={{0,16},{2,18},{4,20},{6,22},{8,24},{10,26},{12,28},{14,30},{16,0},... | collective-permute-start | bytes 1179656 | tf_op jit(solution)/shard_map/ppermute | solution.py:435
  94.3 28.2 %collective-permute-start.27 = (bf16[2,96,1024]{2,1,0:T(8,128)(2,1)}, bf16[2,96,1024]{2,1,0:T(8,128)(2,1)}, u32[]{:S(2)}, u32[]{:S(2)}) collective-permute-start(bf16[2,96,1024]{2,1,0:T(8,128)(2,1)} %pad_maximum_fusion.22), channel_id=1, source_target_pairs={{0,4},{2,6},{4,0},{6,2},{8,12},{10,14},{12,8},{14,10},{16,20},{18,... | collective-permute-start | bytes 1179656 | tf_op jit(solution)/shard_map/ppermute | solution.py:435
  109.0 61.0 %collective-permute-start.32 = (bf16[512,1536]{1,0:T(8,128)(2,1)}, bf16[512,1536]{1,0:T(8,128)(2,1)}, u32[]{:S(2)}, u32[]{:S(2)}) collective-permute-start(bf16[512,1536]{1,0:T(8,128)(2,1)} %fusion.10), channel_id=1, source_target_pairs={{0,1},{1,0},{2,3},{3,2},{4,5},{5,4},{6,7},{7,6},{8,9},{9,8},{10,11... | collective-permute-start | bytes 4718600 | tf_op jit(solution)/shard_map/ppermute | solution.py:409
  118.3 46.5 %collective-permute-start.18 = (bf16[4,96,1024]{2,1,0:T(8,128)(2,1)}, bf16[4,96,1024]{2,1,0:T(8,128)(2,1)}, u32[]{:S(2)}, u32[]{:S(2)}) collective-permute-start(bf16[4,96,1024]{2,1,0:T(8,128)(2,1)} %pad_maximum_fusion.12.refs_0_), channel_id=1, source_target_pairs={{0,4},{2,6},{4,0},{6,2},{8,12},{10,14},{12,8},{14,10},{16,20},{18,... | collective-permute-start | bytes 2359304 | tf_op jit(solution)/shard_map/ppermute | solution.py:435
  118.8 47.5 %collective-permute-start.19 = (bf16[4,96,1024]{2,1,0:T(8,128)(2,1)}, bf16[4,96,1024]{2,1,0:T(8,128)(2,1)}, u32[]{:S(2)}, u32[]{:S(2)}) collective-permute-start(bf16[4,96,1024]{2,1,0:T(8,128)(2,1)} %pad_maximum_fusion.12.refs_0_), channel_id=1, source_target_pairs={{0,2},{2,0},{4,6},{6,4},{8,10},{10,8},{12,14},{14,12},{16,18},{18,... | collective-permute-start | bytes 2359304 | tf_op jit(solution)/shard_map/ppermute | solution.py:435
  122.6 45.7 %collective-permute-start.23 = (bf16[4,96,1024]{2,1,0:T(8,128)(2,1)}, bf16[4,96,1024]{2,1,0:T(8,128)(2,1)}, u32[]{:S(2)}, u32[]{:S(2)}) collective-permute-start(bf16[4,96,1024]{2,1,0:T(8,128)(2,1)} %pad_maximum_fusion.13.refs_4_), channel_id=1, source_target_pairs={{0,8},{2,10},{4,12},{6,14},{8,0},{10,2},{12,4},{14,6},{16,24},{18,... | collective-permute-start | bytes 2359304 | tf_op jit(solution)/shard_map/ppermute | solution.py:435
  124.6 44.9 %collective-permute-start.28 = (bf16[4,96,1024]{2,1,0:T(8,128)(2,1)}, bf16[4,96,1024]{2,1,0:T(8,128)(2,1)}, u32[]{:S(2)}, u32[]{:S(2)}) collective-permute-start(bf16[4,96,1024]{2,1,0:T(8,128)(2,1)} %pad_maximum_fusion.14.refs_8_), channel_id=1, source_target_pairs={{0,2},{2,0},{4,6},{6,4},{8,10},{10,8},{12,14},{14,12},{16,18},{18,... | collective-permute-start | bytes 2359304 | tf_op jit(solution)/shard_map/ppermute | solution.py:435
  164.8 37.4 %collective-permute-start.24 = (bf16[4,96,1024]{2,1,0:T(8,128)(2,1)}, bf16[4,96,1024]{2,1,0:T(8,128)(2,1)}, u32[]{:S(2)}, u32[]{:S(2)}) collective-permute-start(bf16[4,96,1024]{2,1,0:T(8,128)(2,1)} %pad_maximum_fusion.13.refs_4_), channel_id=1, source_target_pairs={{0,4},{2,6},{4,0},{6,2},{8,12},{10,14},{12,8},{14,10},{16,20},{18,... | collective-permute-start | bytes 2359304 | tf_op jit(solution)/shard_map/ppermute | solution.py:435
  166.3 35.9 %collective-permute-start.29 = (bf16[4,96,1024]{2,1,0:T(8,128)(2,1)}, bf16[4,96,1024]{2,1,0:T(8,128)(2,1)}, u32[]{:S(2)}, u32[]{:S(2)}) collective-permute-start(bf16[4,96,1024]{2,1,0:T(8,128)(2,1)} %pad_maximum_fusion.14.refs_8_), channel_id=1, source_target_pairs={{0,8},{2,10},{4,12},{6,14},{8,0},{10,2},{12,4},{14,6},{16,24},{18,... | collective-permute-start | bytes 2359304 | tf_op jit(solution)/shard_map/ppermute | solution.py:435
  168.3 33.9 %collective-permute-start.20 = (bf16[4,96,1024]{2,1,0:T(8,128)(2,1)}, bf16[4,96,1024]{2,1,0:T(8,128)(2,1)}, u32[]{:S(2)}, u32[]{:S(2)}) collective-permute-start(bf16[4,96,1024]{2,1,0:T(8,128)(2,1)} %collective-permute-done.18.refs_1_), channel_id=1, source_target_pairs={{0,2},{2,0},{4,6},{6,4},{8,10},{10,8},{12,14},{14,12},{16,18},{18,... | collective-permute-start | bytes 2359304 | tf_op jit(solution)/shard_map/ppermute | solution.py:435
  169.5 32.8 %collective-permute-start.25 = (bf16[4,96,1024]{2,1,0:T(8,128)(2,1)}, bf16[4,96,1024]{2,1,0:T(8,128)(2,1)}, u32[]{:S(2)}, u32[]{:S(2)}) collective-permute-start(bf16[4,96,1024]{2,1,0:T(8,128)(2,1)} %collective-permute-done.23.refs_5_), channel_id=1, source_target_pairs={{0,4},{2,6},{4,0},{6,2},{8,12},{10,14},{12,8},{14,10},{16,20},{18,... | collective-permute-start | bytes 2359304 | tf_op jit(solution)/shard_map/ppermute | solution.py:435
  170.0 32.3 %collective-permute-start.30 = (bf16[4,96,1024]{2,1,0:T(8,128)(2,1)}, bf16[4,96,1024]{2,1,0:T(8,128)(2,1)}, u32[]{:S(2)}, u32[]{:S(2)}) collective-permute-start(bf16[4,96,1024]{2,1,0:T(8,128)(2,1)} %collective-permute-done.28.refs_9_), channel_id=1, source_target_pairs={{0,8},{2,10},{4,12},{6,14},{8,0},{10,2},{12,4},{14,6},{16,24},{18,... | collective-permute-start | bytes 2359304 | tf_op jit(solution)/shard_map/ppermute | solution.py:435
  372.3 36.1 %collective-permute-start.33 = (f32[1024,256]{0,1:T(8,128)}, f32[1024,256]{0,1:T(8,128)}, u32[]{:S(2)}, u32[]{:S(2)}) collective-permute-start(f32[1024,256]{0,1:T(8,128)} %pad_maximum_fusion.7), channel_id=1, source_target_pairs={{0,1},{1,0},{2,3},{3,2},{4,5},{5,4},{6,7},{7,6},{8,9},{9,8},{10,11... | collective-permute-start | bytes 3145736 | tf_op jit(solution)/shard_map/ppermute | solution.py:409
  376.3 216.3 %collective-permute-start.31 = (f32[512,1536]{1,0:T(8,128)}, f32[512,1536]{1,0:T(8,128)}, u32[]{:S(2)}, u32[]{:S(2)}) collective-permute-start(f32[512,1536]{1,0:T(8,128)} %constant_dynamic-slice_fusion.13), channel_id=1, source_target_pairs={{0,1},{1,0},{2,3},{3,2},{4,5},{5,4},{6,7},{7,6},{8,9},{9,8},{10,11... | collective-permute-start | bytes 9437192 | tf_op jit(solution)/shard_map/ppermute | solution.py:409
  381.1 19.9 %collective-permute-start.56 = (bf16[2,2,2,96,512]{4,3,0,1,2:T(8,128)(2,1)S(1)}, bf16[2,2,2,96,512]{4,3,0,1,2:T(8,128)(2,1)S(1)}, u32[]{:S(2)}, u32[]{:S(2)}) collective-permute-start(bf16[2,2,2,96,512]{4,3,0,1,2:T(8,128)(2,1)S(1)} %bitcast.319), channel_id=1, source_target_pairs={{0,8},{2,10},{4,12},{6,14},{8,0},{10,2},{12,4},{14,6},{16,24},{18,... | collective-permute-start | bytes 2359304 | tf_op jit(solution)/shard_map/ppermute | solution.py:435
  383.3 20.4 %collective-permute-start.52 = (bf16[2,2,2,96,512]{4,3,2,0,1:T(8,128)(2,1)S(1)}, bf16[2,2,2,96,512]{4,3,2,0,1:T(8,128)(2,1)S(1)}, u32[]{:S(2)}, u32[]{:S(2)}) collective-permute-start(bf16[2,2,2,96,512]{4,3,2,0,1:T(8,128)(2,1)S(1)} %bitcast.318), channel_id=1, source_target_pairs={{0,4},{2,6},{4,0},{6,2},{8,12},{10,14},{12,8},{14,10},{16,20},{18,... | collective-permute-start | bytes 2359304 | tf_op jit(solution)/shard_map/ppermute | solution.py:435
  385.1 21.3 %collective-permute-start.48 = (bf16[2,2,2,96,512]{4,3,0,1,2:T(8,128)(2,1)S(1)}, bf16[2,2,2,96,512]{4,3,0,1,2:T(8,128)(2,1)S(1)}, u32[]{:S(2)}, u32[]{:S(2)}) collective-permute-start(bf16[2,2,2,96,512]{4,3,0,1,2:T(8,128)(2,1)S(1)} %bitcast.317), channel_id=1, source_target_pairs={{0,2},{2,0},{4,6},{6,4},{8,10},{10,8},{12,14},{14,12},{16,18},{18,... | collective-permute-start | bytes 2359304 | tf_op jit(solution)/shard_map/ppermute | solution.py:435
  401.0 89.1 %collective-permute-start.64 = (bf16[2,2,2,96,1024]{4,3,0,1,2:T(8,128)(2,1)}, bf16[2,2,2,96,1024]{4,3,0,1,2:T(8,128)(2,1)}, u32[]{:S(2)}, u32[]{:S(2)}) collective-permute-start(bf16[2,2,2,96,1024]{4,3,0,1,2:T(8,128)(2,1)} %bitcast.259), channel_id=1, source_target_pairs={{0,8},{2,10},{4,12},{6,14},{8,0},{10,2},{12,4},{14,6},{16,24},{18,... | collective-permute-start | bytes 4718600 | tf_op jit(solution)/shard_map/ppermute | solution.py:435
  403.8 99.0 %collective-permute-start.44 = (bf16[2,2,2,96,1024]{4,3,2,0,1:T(8,128)(2,1)}, bf16[2,2,2,96,1024]{4,3,2,0,1:T(8,128)(2,1)}, u32[]{:S(2)}, u32[]{:S(2)}) collective-permute-start(bf16[2,2,2,96,1024]{4,3,2,0,1:T(8,128)(2,1)} %bitcast.260), channel_id=1, source_target_pairs={{0,4},{2,6},{4,0},{6,2},{8,12},{10,14},{12,8},{14,10},{16,20},{18,... | collective-permute-start | bytes 4718600 | tf_op jit(solution)/shard_map/ppermute | solution.py:435
  406.4 29.4 %collective-permute-start.57 = (bf16[2,2,96,512]{3,2,0,1:T(8,128)(2,1)}, bf16[2,2,96,512]{3,2,0,1:T(8,128)(2,1)}, u32[]{:S(2)}, u32[]{:S(2)}) collective-permute-start(bf16[2,2,96,512]{3,2,0,1:T(8,128)(2,1)} %fusion.42), channel_id=1, source_target_pairs={{0,2},{2,0},{4,6},{6,4},{8,10},{10,8},{12,14},{14,12},{16,18},{18,... | collective-permute-start | bytes 1179656 | tf_op jit(solution)/shard_map/ppermute | solution.py:435
  408.4 37.2 %collective-permute-start.53 = (bf16[2,2,96,512]{3,2,1,0:T(8,128)(2,1)}, bf16[2,2,96,512]{3,2,1,0:T(8,128)(2,1)}, u32[]{:S(2)}, u32[]{:S(2)}) collective-permute-start(bf16[2,2,96,512]{3,2,1,0:T(8,128)(2,1)} %fusion.41), channel_id=1, source_target_pairs={{0,8},{2,10},{4,12},{6,14},{8,0},{10,2},{12,4},{14,6},{16,24},{18,... | collective-permute-start | bytes 1179656 | tf_op jit(solution)/shard_map/ppermute | solution.py:435
  435.9 11.9 %collective-permute-start.49 = (bf16[2,2,96,512]{3,2,0,1:T(8,128)(2,1)S(1)}, bf16[2,2,96,512]{3,2,0,1:T(8,128)(2,1)S(1)}, u32[]{:S(2)}, u32[]{:S(2)}) collective-permute-start(bf16[2,2,96,512]{3,2,0,1:T(8,128)(2,1)S(1)} %copy-done.71), channel_id=1, source_target_pairs={{0,4},{2,6},{4,0},{6,2},{8,12},{10,14},{12,8},{14,10},{16,20},{18,... | collective-permute-start | bytes 1179656 | tf_op jit(solution)/shard_map/ppermute | solution.py:435
  445.6 65.2 %collective-permute-start.40 = (bf16[2,2,2,96,1024]{4,3,0,1,2:T(8,128)(2,1)S(1)}, bf16[2,2,2,96,1024]{4,3,0,1,2:T(8,128)(2,1)S(1)}, u32[]{:S(2)}, u32[]{:S(2)}) collective-permute-start(bf16[2,2,2,96,1024]{4,3,0,1,2:T(8,128)(2,1)S(1)} %bitcast.304), channel_id=1, source_target_pairs={{0,2},{2,0},{4,6},{6,4},{8,10},{10,8},{12,14},{14,12},{16,18},{18,... | collective-permute-start | bytes 4718600 | tf_op jit(solution)/shard_map/ppermute | solution.py:435
  489.3 13.3 %collective-permute-start.60 = (bf16[2,2,2,96,384]{4,3,2,1,0:T(8,128)(2,1)S(1)}, bf16[2,2,2,96,384]{4,3,2,1,0:T(8,128)(2,1)S(1)}, u32[]{:S(2)}, u32[]{:S(2)}) collective-permute-start(bf16[2,2,2,96,384]{4,3,2,1,0:T(8,128)(2,1)S(1)} %copy-done.61), channel_id=1, source_target_pairs={{0,2},{2,0},{4,6},{6,4},{8,10},{10,8},{12,14},{14,12},{16,18},{18,... | collective-permute-start | bytes 1769480 | tf_op jit(solution)/shard_map/ppermute | solution.py:435
  490.1 77.4 %collective-permute-start.34 = (f32[512,1536]{1,0:T(8,128)}, f32[512,1536]{1,0:T(8,128)}, u32[]{:S(2)}, u32[]{:S(2)}) collective-permute-start(f32[512,1536]{1,0:T(8,128)} %constant_dynamic-slice_fusion.12), channel_id=1, source_target_pairs={{0,1},{1,0},{2,3},{3,2},{4,5},{5,4},{6,7},{7,6},{8,9},{9,8},{10,11... | collective-permute-start | bytes 9437192 | tf_op jit(solution)/shard_map/ppermute | solution.py:409
  502.5 33.2 %collective-permute-start.65 = (bf16[2,2,96,1024]{3,2,0,1:T(8,128)(2,1)}, bf16[2,2,96,1024]{3,2,0,1:T(8,128)(2,1)}, u32[]{:S(2)}, u32[]{:S(2)}) collective-permute-start(bf16[2,2,96,1024]{3,2,0,1:T(8,128)(2,1)} %fusion.30), channel_id=1, source_target_pairs={{0,2},{2,0},{4,6},{6,4},{8,10},{10,8},{12,14},{14,12},{16,18},{18,... | collective-permute-start | bytes 2359304 | tf_op jit(solution)/shard_map/ppermute | solution.py:435
  509.9 27.9 %collective-permute-start.45 = (bf16[2,2,96,1024]{3,2,1,0:T(8,128)(2,1)}, bf16[2,2,96,1024]{3,2,1,0:T(8,128)(2,1)}, u32[]{:S(2)}, u32[]{:S(2)}) collective-permute-start(bf16[2,2,96,1024]{3,2,1,0:T(8,128)(2,1)} %fusion.29), channel_id=1, source_target_pairs={{0,8},{2,10},{4,12},{6,14},{8,0},{10,2},{12,4},{14,6},{16,24},{18,... | collective-permute-start | bytes 2359304 | tf_op jit(solution)/shard_map/ppermute | solution.py:435
  510.8 16.0 %collective-permute-start.62 = (bf16[2,96,384]{2,1,0:T(8,128)(2,1)S(1)}, bf16[2,96,384]{2,1,0:T(8,128)(2,1)S(1)}, u32[]{:S(2)}, u32[]{:S(2)}) collective-permute-start(bf16[2,96,384]{2,1,0:T(8,128)(2,1)S(1)} %fusion.52), channel_id=1, source_target_pairs={{0,8},{2,10},{4,12},{6,14},{8,0},{10,2},{12,4},{14,6},{16,24},{18,... | collective-permute-start | bytes 442376 | tf_op jit(solution)/shard_map/ppermute | solution.py:435
  532.6 14.5 %collective-permute-start.41 = (bf16[2,2,96,1024]{3,2,0,1:T(8,128)(2,1)}, bf16[2,2,96,1024]{3,2,0,1:T(8,128)(2,1)}, u32[]{:S(2)}, u32[]{:S(2)}) collective-permute-start(bf16[2,2,96,1024]{3,2,0,1:T(8,128)(2,1)} %fusion.28), channel_id=1, source_target_pairs={{0,4},{2,6},{4,0},{6,2},{8,12},{10,14},{12,8},{14,10},{16,20},{18,... | collective-permute-start | bytes 2359304 | tf_op jit(solution)/shard_map/ppermute | solution.py:435
  537.4 13.9 %collective-permute-start.66 = (bf16[2,96,1024]{2,1,0:T(8,128)(2,1)S(1)}, bf16[2,96,1024]{2,1,0:T(8,128)(2,1)S(1)}, u32[]{:S(2)}, u32[]{:S(2)}) collective-permute-start(bf16[2,96,1024]{2,1,0:T(8,128)(2,1)S(1)} %fusion.43), channel_id=1, source_target_pairs={{0,4},{2,6},{4,0},{6,2},{8,12},{10,14},{12,8},{14,10},{16,20},{18,... | collective-permute-start | bytes 1179656 | tf_op jit(solution)/shard_map/ppermute | solution.py:435
  539.7 22.8 %collective-permute-start.46 = (bf16[2,96,1024]{2,1,0:T(8,128)(2,1)S(1)}, bf16[2,96,1024]{2,1,0:T(8,128)(2,1)S(1)}, u32[]{:S(2)}, u32[]{:S(2)}) collective-permute-start(bf16[2,96,1024]{2,1,0:T(8,128)(2,1)S(1)} %fusion.39), channel_id=1, source_target_pairs={{0,16},{2,18},{4,20},{6,22},{8,24},{10,26},{12,28},{14,30},{16,0},... | collective-permute-start | bytes 1179656 | tf_op jit(solution)/shard_map/ppermute | solution.py:435
  548.7 18.0 %collective-permute-start.42 = (bf16[2,96,1024]{2,1,0:T(8,128)(2,1)S(1)}, bf16[2,96,1024]{2,1,0:T(8,128)(2,1)S(1)}, u32[]{:S(2)}, u32[]{:S(2)}) collective-permute-start(bf16[2,96,1024]{2,1,0:T(8,128)(2,1)S(1)} %fusion.38), channel_id=1, source_target_pairs={{0,8},{2,10},{4,12},{6,14},{8,0},{10,2},{12,4},{14,6},{16,24},{18,... | collective-permute-start | bytes 1179656 | tf_op jit(solution)/shard_map/ppermute | solution.py:435
  551.5 16.0 %collective-permute-start.67 = (bf16[96,1024]{1,0:T(8,128)(2,1)S(1)}, bf16[96,1024]{1,0:T(8,128)(2,1)S(1)}, u32[]{:S(2)}, u32[]{:S(2)}) collective-permute-start(bf16[96,1024]{1,0:T(8,128)(2,1)S(1)} %fusion.50), channel_id=1, source_target_pairs={{0,16},{2,18},{4,20},{6,22},{8,24},{10,26},{12,28},{14,30},{16,0},... | collective-permute-start | bytes 589832 | tf_op jit(solution)/shard_map/ppermute | solution.py:435
  (147 other events, 1787.9 us)

commit v6 on v5

--- a/solution.py
+++ b/solution.py
@@ -430,9 +430,13 @@
     return tuple(tuple((bit + turn) % bits for bit in range(bits)) for turn in range(3))
 
 
+def exchange(values, mask):
+    size = lax.axis_size("dp")
+    return lax.ppermute(values, "dp", [(i, i ^ mask) for i in range(size)])
+
+
 def partner(values, bit):
-    size = lax.axis_size("dp")
-    return lax.ppermute(values, "dp", [(i, i ^ (1 << bit)) for i in range(size)])
+    return exchange(values, 1 << bit)
 
 
 def place_kernel(table, *refs):
@@ -548,8 +552,13 @@
 
 
 def sum_small(values):
-    for bit in range(lax.axis_size("dp").bit_length() - 1):
-        values = values + partner(values, bit)
+    bits = lax.axis_size("dp").bit_length() - 1
+    for bit in range(0, bits, 2):
+        if bit + 1 == bits:
+            values = values + exchange(values, 1 << bit)
+        else:
+            near, far, cross = (exchange(values, turn << bit) for turn in (1, 2, 3))
+            values = (values + near) + (far + cross)
     return values
 
 

time: 607 us -> 605 us (level)
    ppermute x62 -> x64, waiting for transfers between devices: 146 us -> 149 us  [exchange(): return lax.ppermute(values, 'dp', [(i, i ^ mask) for i in range(size)])]
    ppermute x62 -> x64, starting transfers between devices: 73.3 us -> 72.5 us  [exchange(): return lax.ppermute(values, 'dp', [(i, i ^ mask) for i in range(size)])]
    unnamed x256 -> x264, local copies, waits for them, and re-layouts: 18.1 us -> 18.1 us
  transfers between devices with their start and end apart: 68 -> 70, of which waited for: 33 -> 33; matrix products, arithmetic and copies ran while one was open for 27% -> 26% of each run, Pallas kernels for 6% -> 6%
where the time goes in v6:
time: 605 us; the launch traced here: 599 us
  waiting for transfers between devices  150 us (25%)
  Pallas kernels  104 us (17%)
  matrix products  93 us (15%)
  other arithmetic  91.5 us (15%)
  local copies, waits for them, and re-layouts  79.9 us (13%)
  starting transfers between devices  73 us (12%)
    ppermute x64, waiting for transfers between devices, exchange(): return lax.ppermute(values, 'dp', [(i, i ^ mask) for i in range(size)])  149 us
    ppermute x64, starting transfers between devices, exchange(): return lax.ppermute(values, 'dp', [(i, i ^ mask) for i in range(size)])  72.5 us
    pallas_call x1, Pallas kernels, ssd_backward(): pl.pallas_call(ssd_backward_kernel, grid=(groups,), in_specs=[lanes_spec(...  61 us
    pallas_call x1, Pallas kernels, ssd_forward(): pl.pallas_call(ssd_forward_kernel, grid=(groups,), in_specs=[lanes_spec(a...  27.4 us
    dot_general x3, matrix products, dot_nt(): lax.dot_general(a, b, (((1,), (1,)), ((), ())), preferred_element_type=F32)  22.8 us
    dot_general x2, matrix products, dot(): return jnp.dot(a, b, preferred_element_type=F32)  19.3 us
    unnamed x264, local copies, waits for them, and re-layouts  18.1 us
    pallas_call x2, Pallas kernels, place_rows(): pl.pallas_call(place_kernel, in_specs=[pl.BlockSpec(memory_space=pltpu.SM...  15.8 us
  transfers between devices with their start and end apart: 70, of which 33 were waited for; matrix products, arithmetic and copies ran while one was open for 26% of the time, Pallas kernels for 6%

profile of v6, /device:TPU:0, one launch (start us, length us, event | category | flops | bytes accessed | tf_op | source)
XLA Modules:
  0.0 599.1 jit_solution(5550444005669140872)
XLA Ops:
  2.5 4.1 collective-permute-start
  17.3 2.7 collective-permute-start.4
  21.6 6.5 %collective-permute-done.1 = bf16[2,96,640]{2,1,0:T(8,128)(2,1)S(1)} collective-permute-done((bf16[2,96,640]{2,1,0:T(8,128)(2,1)S(1)}, bf16[2,96,640]{2,1,0:T(8,128)(2,1)S(1)}, u32[]{:S(2)}, u32[]{:S(2)}) %collective-permute-start.1) | collective-permute-done | bytes 245792 | tf_op jit(solution)/shard_map/ppermute | solution.py:435
  50.0 2.6 collective-permute-start.16
  56.2 6.3 %collective-permute-done.16 = bf16[1,96,1024]{2,1,0:T(8,128)(2,1)S(1)} collective-permute-done((bf16[1,96,1024]{2,1,0:T(8,128)(2,1)S(1)}, bf16[1,96,1024]{2,1,0:T(8,128)(2,1)S(1)}, u32[]{:S(2)}, u32[]{:S(2)}) %collective-permute-start.16) | collective-permute-done | bytes 196640 | tf_op jit(solution)/shard_map/ppermute | solution.py:435
  63.1 7.3 %collective-permute-done.21 = bf16[1,96,1024]{2,1,0:T(8,128)(2,1)S(1)} collective-permute-done((bf16[1,96,1024]{2,1,0:T(8,128)(2,1)S(1)}, bf16[1,96,1024]{2,1,0:T(8,128)(2,1)S(1)}, u32[]{:S(2)}, u32[]{:S(2)}) %collective-permute-start.21) | collective-permute-done | bytes 196640 | tf_op jit(solution)/shard_map/ppermute | solution.py:435
  80.6 3.9 collective-permute-done.12.refs_6_
  85.8 5.6 collective-permute-done.13.refs_7_
  101.7 7.3 %collective-permute-done.15.refs_11_ = bf16[4,96,640]{2,1,0:T(8,128)(2,1)} collective-permute-done((bf16[4,96,640]{2,1,0:T(8,128)(2,1)}, bf16[4,96,640]{2,1,0:T(8,128)(2,1)}, u32[]{:S(2)}, u32[]{:S(2)}) %collective-permute-start.15) | collective-permute-done | bytes 491552 | tf_op jit(solution)/shard_map/ppermute | solution.py:435
  109.0 6.8 %place_rows.2 = bf16[16,96,1920]{2,1,0:T(8,128)(2,1)} custom-call(s32[3,16]{1,0:T(4,128)} %pad_add_fusion.1.table, bf16[4,96,640]{2,1,0:T(8,128)(2,1)} %pad_maximum_fusion.17.refs_0_, bf16[4,96,640]{2,1,0:T(8,128)(2,1)} %collective-permute-done.2.refs_1_, bf16[4,96,640]{2,1,0:T(8,128)(2,1)} %copy-done.65, bf16[4,96,640]{2,1,0:T(8,128)(2,1)} %copy-done.66, ...), custom_call_target="tpu_custom_call" | custom-call | bytes 11796480 | tf_op jit(solution)/shard_map/place_rows/pallas_call | solution.py:514
  127.7 6.6 %fusion.75.xr = f32[1024,1920]{1,0:T(8,128)S(1)} fusion(bf16[1536,1920]{1,0:T(8,128)(2,1)S(1)} %bitcast.284, bf16[512,1536]{1,0:T(8,128)(2,1)S(1)} %get-tuple-element.200, bf16[512,1536]{1,0:T(8,128)(2,1)S(1)} %get-tuple-element.199), kind=kOutput, calls=%fused_computation.311 | convolution fusion | flops 6046089216 | bytes 16908288 | tf_op jit(solution)/shard_map/dot_general | solution.py:35
  142.1 2.9 copy.283
  147.7 4.0 multiply_convert_fusion.2
  170.1 27.4 %ssd_forward.1 = (f32[1024,1536]{1,0:T(8,128)}, bf16[1024,1536]{1,0:T(8,128)(2,1)}) custom-call(f32[1024,1920]{1,0:T(8,128)} %copy-done.27, f32[4,1536]{1,0:T(4,128)} %taps.1, f32[1,1536]{1,0:T(1,128)} %broadcast_in_dim.26.bias, f32[1,1536]{1,0:T(1,128)} %broadcast_in_dim_reshape.2.skip, f32[3,1024,128]{2,1,0:T(8,128)} %pad_maximum_fusion.5.masks, ...), custom_call_target="tpu_custom_call" | custom-call | flops 26172456960 | bytes 18874368 | tf_op jit(solution)/shard_map/ssd_forward/pallas_call | solution.py:298
  198.6 3.7 broadcast_select_fusion.1
  202.4 8.9 %place_rows.3 = bf16[16,96,3072]{2,1,0:T(8,128)(2,1)} custom-call(s32[3,16]{1,0:T(4,128)} %pad_add_fusion.1.table, bf16[4,96,1024]{2,1,0:T(8,128)(2,1)} %pad_maximum_fusion.12.refs_0_, bf16[4,96,1024]{2,1,0:T(8,128)(2,1)} %collective-permute-done.18.refs_1_, bf16[4,96,1024]{2,1,0:T(8,128)(2,1)} %collective-permute-done.19.refs_2_, ...), custom_call_target="tpu_custom_call" | custom-call | bytes 18874368 | tf_op jit(solution)/shard_map/place_rows/pallas_call | solution.py:514
  211.4 12.7 %multiply_reduce_fusion.2 = (f32[1024]{0:T(1024)S(1)}, f32[1024,1536]{1,0:T(8,128)}, f32[1024,1536]{1,0:T(8,128)}) fusion(f32[1024,1536]{1,0:T(8,128)} %get-tuple-element.66, bf16[1536,3072]{1,0:T(8,128)(2,1)} %bitcast.276, bf16[512,1536]{1,0:T(8,128)(2,1)S(1)} %copy-done.45, bf16[512,1536]{1,0:T(8,128)(2,1)S(1)} %copy-done.41), kind=kOutput, calls=%fused_computation.15 | convolution fusion | flops 4849138688 | bytes 26742784 | tf_op jit(solution)/shard_map/dot_general | solution.py:35
  226.5 13.7 %multiply_reduce_fusion = (f32[1536]{0:T(1024)}, f32[1024]{0:T(1024)S(1)}, f32[1024,1536]{1,0:T(8,128)}) fusion(f32[1024,1536]{1,0:T(8,128)} %get-tuple-element.181, f32[1024]{0:T(1024)S(1)} %get-tuple-element.234, f32[1536]{0:T(1024)S(1)} %copy-done.107, bf16[1536,3072]{1,0:T(8,128)(2,1)} %bitcast.277, bf16[512,1536]{1,0:T(8,128)(2,1)} %get-tuple-element.198, ...), kind=kOutput, calls=%fused_computation.9 | convolution fusion | flops 4847564288 | bytes 20467712 | tf_op jit(solution)/shard_map/td,dc->tc/dot_general | solution.py:696
  240.2 7.2 %convolution_convert_fusion.1 = bf16[1536,1536]{1,0:T(8,128)(2,1)} fusion(bf16[512,1536]{1,0:T(8,128)(2,1)S(1)} %copy-done.49, bf16[512,1536]{1,0:T(8,128)(2,1)S(1)} %copy-done.48, f32[1024,1536]{1,0:T(8,128)S(1)} %copy-done.18, f32[1536]{0:T(1024)S(1)} %copy-done.107, f32[1024]{0:T(1024)S(1)} %get-tuple-element.234), kind=kOutput, calls=%fused_computation.1 | convolution fusion | flops 4845207552 | bytes 14166016 | tf_op jit(solution)/shard_map/td,tc->dc/dot_general | solution.py:693
  249.9 13.2 %multiply_convert_fusion = (bf16[1024,1536]{1,0:T(8,128)(2,1)S(1)}, f32[1024,1536]{1,0:T(8,128)}) fusion(f32[1024,1536]{1,0:T(8,128)} %get-tuple-element.250, f32[1024,1536]{1,0:T(8,128)} %get-tuple-element.66, f32[1024]{0:T(1024)S(1)} %broadcast_multiply_fusion.5, f32[1024,1536]{1,0:T(8,128)} %get-tuple-element.181, f32[1024,1536]{1,0:T(8,128)} %get-tuple-element.251, ...), kind=kLoop, calls=%fused_computation.11 | loop fusion | flops 26738688 | bytes 34621440 | tf_op jit(solution)/shard_map/convert_element_type | solution.py:707
  263.1 6.8 %convolution_convert_fusion.2 = bf16[1536,1536]{1,0:T(8,128)(2,1)} fusion(bf16[1024,1536]{1,0:T(8,128)(2,1)S(1)} %get-tuple-element.186, bf16[512,1536]{1,0:T(8,128)(2,1)S(1)} %copy-done.45, bf16[512,1536]{1,0:T(8,128)(2,1)S(1)} %copy-done.41), kind=kOutput, calls=%fused_computation.2 | convolution fusion | flops 4840488960 | bytes 11010048 | tf_op jit(solution)/shard_map/td,tc->dc/dot_general | solution.py:709
  269.9 61.0 %ssd_backward.1 = (bf16[1024,1536]{1,0:T(8,128)(2,1)}, f32[1024,128]{1,0:T(8,128)}, f32[1024,128]{1,0:T(8,128)}, f32[1024,128]{1,0:T(8,128)}, f32[1024,128]{1,0:...) custom-call(f32[1024,1920]{1,0:T(8,128)} %copy-done.27, ...), custom_call_target="tpu_custom_call" | custom-call | flops 58384711680 | bytes 25165824 | tf_op jit(solution)/shard_map/ssd_backward/pallas_call | solution.py:349
  333.0 10.8 %fusion.5 = f32[1024,1536]{1,0:T(8,128)} fusion(bf16[1536,3072]{1,0:T(8,128)(2,1)} %bitcast.278, f32[1024,1536]{1,0:T(8,128)} %get-tuple-element.181, f32[1536]{0:T(1024)S(1)} %copy-done.107, f32[1024]{0:T(1024)S(1)} %get-tuple-element.234), kind=kOutput, calls=%fused_computation.22 | convolution fusion | flops 4836556800 | bytes 17311744 | tf_op jit(solution)/shard_map/tc,dc->td/dot_general | solution.py:685
  344.4 9.4 %fusion.1 = f32[1024,1536]{1,0:T(8,128)} fusion(bf16[1024,1536]{1,0:T(8,128)(2,1)S(1)} %copy-done.121, bf16[1536,1920]{1,0:T(8,128)(2,1)} %bitcast.282), kind=kOutput, calls=%fused_computation.18 | convolution fusion | flops 4831838208 | bytes 14155776 | tf_op jit(solution)/shard_map/dot_general | solution.py:39
  353.8 7.2 %convolution_convert_fusion = bf16[1536,1536]{1,0:T(8,128)(2,1)} fusion(bf16[1024,1536]{1,0:T(8,128)(2,1)S(1)} %copy-done.121, bf16[512,1536]{1,0:T(8,128)(2,1)S(1)} %copy-done.46, bf16[512,1536]{1,0:T(8,128)(2,1)S(1)} %copy-done.42), kind=kOutput, calls=%fused_computation | convolution fusion | flops 4840488960 | bytes 11010048 | tf_op jit(solution)/shard_map/td,tc->dc/dot_general | solution.py:749
  372.6 3.8 constant_dynamic-slice_fusion.13
  377.7 2.7 fusion.81
  396.7 3.8 collective-permute-done.58
  408.3 2.7 multiply_reduce_fusion.6
  414.3 3.3 fusion.23
  421.4 10.1 %add_add_fusion = f32[1024,1536]{1,0:T(8,128)} fusion(f32[1024,1536]{1,0:T(8,128)S(1)} %fusion.23, f32[1024,1536]{1,0:T(8,128)} %fusion.1, bf16[1024,1536]{1,0:T(8,128)(2,1)} %copy-done.28, bf16[1536,3072]{1,0:T(8,128)(2,1)S(1)} %bitcast.281), kind=kOutput, calls=%fused_computation.10 | convolution fusion | flops 4834983936 | bytes 26738688 | tf_op jit(solution)/shard_map/dot_general | solution.py:39
  431.4 3.9 constant_dynamic-slice_fusion.12
  437.2 7.9 %collective-permute-done.55 = bf16[2,2,96,512]{3,2,1,0:T(8,128)(2,1)} collective-permute-done((bf16[2,2,96,512]{3,2,1,0:T(8,128)(2,1)}, bf16[2,2,96,512]{3,2,1,0:T(8,128)(2,1)}, u32[]{:S(2)}, u32[]{:S(2)}) %collective-permute-start.55) | collective-permute-done | bytes 393248 | tf_op jit(solution)/shard_map/ppermute | solution.py:435
  448.9 3.9 collective-permute-done.60
  454.6 7.5 %collective-permute-done.56 = bf16[2,96,512]{2,1,0:T(8,128)(2,1)S(1)} collective-permute-done((bf16[2,96,512]{2,1,0:T(8,128)(2,1)S(1)}, bf16[2,96,512]{2,1,0:T(8,128)(2,1)S(1)}, u32[]{:S(2)}, u32[]{:S(2)}) %collective-permute-start.56) | collective-permute-done | bytes 196640 | tf_op jit(solution)/shard_map/ppermute | solution.py:435
  462.2 5.5 collective-permute-done.52
  468.1 5.7 collective-permute-done.61
  475.3 6.8 %collective-permute-done.57 = bf16[96,512]{1,0:T(8,128)(2,1)S(1)} collective-permute-done((bf16[96,512]{1,0:T(8,128)(2,1)S(1)}, bf16[96,512]{1,0:T(8,128)(2,1)S(1)}, u32[]{:S(2)}, u32[]{:S(2)}) %collective-permute-start.57) | collective-permute-done | bytes 98336 | tf_op jit(solution)/shard_map/ppermute | solution.py:435
  483.7 5.0 collective-permute-done.53
  492.8 9.2 %collective-permute-done.62 = bf16[2,2,2,96,384]{4,3,2,1,0:T(8,128)(2,1)S(1)} collective-permute-done((bf16[2,2,2,96,384]{4,3,2,1,0:T(8,128)(2,1)S(1)}, bf16[2,2,2,96,384]{4,3,2,1,0:T(8,128)(2,1)S(1)}, u32[]{:S(2)}, u32[]{:S(2)}) %collective-permute-start.62) | collective-permute-done | bytes 589856 | tf_op jit(solution)/shard_map/ppermute | solution.py:435
  512.2 14.0 %collective-permute-done.64 = bf16[2,96,384]{2,1,0:T(8,128)(2,1)S(1)} collective-permute-done((bf16[2,96,384]{2,1,0:T(8,128)(2,1)S(1)}, bf16[2,96,384]{2,1,0:T(8,128)(2,1)S(1)}, u32[]{:S(2)}, u32[]{:S(2)}) %collective-permute-start.64) | collective-permute-done | bytes 147488 | tf_op jit(solution)/shard_map/ppermute | solution.py:435
  527.9 4.2 collective-permute-done.65
  539.4 7.2 %collective-permute-done.43 = bf16[2,2,96,1024]{3,2,0,1:T(8,128)(2,1)} collective-permute-done((bf16[2,2,96,1024]{3,2,0,1:T(8,128)(2,1)}, bf16[2,2,96,1024]{3,2,0,1:T(8,128)(2,1)}, u32[]{:S(2)}, u32[]{:S(2)}) %collective-permute-start.43) | collective-permute-done | bytes 786464 | tf_op jit(solution)/shard_map/ppermute | solution.py:435
  551.5 10.5 %collective-permute-done.48 = bf16[2,96,1024]{2,1,0:T(8,128)(2,1)S(1)} collective-permute-done((bf16[2,96,1024]{2,1,0:T(8,128)(2,1)S(1)}, bf16[2,96,1024]{2,1,0:T(8,128)(2,1)S(1)}, u32[]{:S(2)}, u32[]{:S(2)}) %collective-permute-start.48) | collective-permute-done | bytes 393248 | tf_op jit(solution)/shard_map/ppermute | solution.py:435
  563.4 2.7 collective-permute-done.44
  568.0 6.0 %collective-permute-done.45 = bf16[96,1024]{1,0:T(8,128)(2,1)S(1)} collective-permute-done((bf16[96,1024]{1,0:T(8,128)(2,1)S(1)}, bf16[96,1024]{1,0:T(8,128)(2,1)S(1)}, u32[]{:S(2)}, u32[]{:S(2)}) %collective-permute-start.45) | collective-permute-done | bytes 196640 | tf_op jit(solution)/shard_map/ppermute | solution.py:435
  574.2 4.7 fusion.20
  590.7 5.0 fusion.11
  (599 shorter events, 211.5 us)
Async XLA Ops:
  2.5 13.1 %collective-permute-start = (bf16[1,96,640]{2,1,0:T(8,128)(2,1)S(1)}, bf16[1,96,640]{2,1,0:T(8,128)(2,1)S(1)}, u32[]{:S(2)}, u32[]{:S(2)}) collective-permute-start(bf16[1,96,640]{2,1,0:T(8,128)(2,1)S(1)} %get-tuple-element.226), channel_id=1, source_target_pairs={{0,16},{2,18},{4,20},{6,22},{8,24},{10,26},{12,28},{14,30},{16,0},... | collective-permute-start | bytes 368648 | tf_op jit(solution)/shard_map/ppermute | solution.py:435
  15.6 12.5 %collective-permute-start.1 = (bf16[2,96,640]{2,1,0:T(8,128)(2,1)S(1)}, bf16[2,96,640]{2,1,0:T(8,128)(2,1)S(1)}, u32[]{:S(2)}, u32[]{:S(2)}) collective-permute-start(bf16[2,96,640]{2,1,0:T(8,128)(2,1)S(1)} %pad_maximum_fusion.23), channel_id=1, source_target_pairs={{0,8},{2,10},{4,12},{6,14},{8,0},{10,2},{12,4},{14,6},{16,24},{18,... | collective-permute-start | bytes 737288 | tf_op jit(solution)/shard_map/ppermute | solution.py:435
  17.3 13.3 %collective-permute-start.4 = (bf16[2,96,640]{2,1,0:T(8,128)(2,1)S(1)}, bf16[2,96,640]{2,1,0:T(8,128)(2,1)S(1)}, u32[]{:S(2)}, u32[]{:S(2)}) collective-permute-start(bf16[2,96,640]{2,1,0:T(8,128)(2,1)S(1)} %pad_maximum_fusion.24), channel_id=1, source_target_pairs={{0,16},{2,18},{4,20},{6,22},{8,24},{10,26},{12,28},{14,30},{16,0},... | collective-permute-start | bytes 737288 | tf_op jit(solution)/shard_map/ppermute | solution.py:435
  29.0 12.2 %collective-permute-start.2 = (bf16[4,96,640]{2,1,0:T(8,128)(2,1)}, bf16[4,96,640]{2,1,0:T(8,128)(2,1)}, u32[]{:S(2)}, u32[]{:S(2)}) collective-permute-start(bf16[4,96,640]{2,1,0:T(8,128)(2,1)} %pad_maximum_fusion.17.refs_0_), channel_id=1, source_target_pairs={{0,4},{2,6},{4,0},{6,2},{8,12},{10,14},{12,8},{14,10},{16,20},{18,... | collective-permute-start | bytes 1474568 | tf_op jit(solution)/shard_map/ppermute | solution.py:435
  31.1 12.1 %collective-permute-start.8 = (bf16[4,96,640]{2,1,0:T(8,128)(2,1)S(1)}, bf16[4,96,640]{2,1,0:T(8,128)(2,1)}, u32[]{:S(2)}, u32[]{:S(2)}) collective-permute-start(bf16[4,96,640]{2,1,0:T(8,128)(2,1)S(1)} %pad_maximum_fusion.19.refs_8_), channel_id=1, source_target_pairs={{0,2},{2,0},{4,6},{6,4},{8,10},{10,8},{12,14},{14,12},{16,18},{18,... | collective-permute-start | bytes 1474568 | tf_op jit(solution)/shard_map/ppermute | solution.py:435
  44.2 31.6 %collective-permute-start.10 = (bf16[4,96,640]{2,1,0:T(8,128)(2,1)}, bf16[4,96,640]{2,1,0:T(8,128)(2,1)S(1)}, u32[]{:S(2)}, u32[]{:S(2)}) collective-permute-start(bf16[4,96,640]{2,1,0:T(8,128)(2,1)} %pad_maximum_fusion.17.refs_0_), channel_id=1, source_target_pairs={{0,2},{2,0},{4,6},{6,4},{8,10},{10,8},{12,14},{14,12},{16,18},{18,... | collective-permute-start | bytes 1474568 | tf_op jit(solution)/shard_map/ppermute | solution.py:435
  45.9 31.9 %collective-permute-start.11 = (bf16[4,96,640]{2,1,0:T(8,128)(2,1)}, bf16[4,96,640]{2,1,0:T(8,128)(2,1)S(1)}, u32[]{:S(2)}, u32[]{:S(2)}) collective-permute-start(bf16[4,96,640]{2,1,0:T(8,128)(2,1)} %collective-permute-done.2.refs_1_), channel_id=1, source_target_pairs={{0,2},{2,0},{4,6},{6,4},{8,10},{10,8},{12,14},{14,12},{16,18},{18,... | collective-permute-start | bytes 1474568 | tf_op jit(solution)/shard_map/ppermute | solution.py:435
  47.8 76.8 %collective-permute-start.9 = (bf16[512,1536]{1,0:T(8,128)(2,1)}, bf16[512,1536]{1,0:T(8,128)(2,1)}, u32[]{:S(2)}, u32[]{:S(2)}) collective-permute-start(bf16[512,1536]{1,0:T(8,128)(2,1)} %fusion.14), channel_id=1, source_target_pairs={{0,1},{1,0},{2,3},{3,2},{4,5},{5,4},{6,7},{7,6},{8,9},{9,8},{10,11... | collective-permute-start | bytes 4718600 | tf_op jit(solution)/shard_map/ppermute | solution.py:409
  50.0 12.5 %collective-permute-start.16 = (bf16[1,96,1024]{2,1,0:T(8,128)(2,1)S(1)}, bf16[1,96,1024]{2,1,0:T(8,128)(2,1)S(1)}, u32[]{:S(2)}, u32[]{:S(2)}) collective-permute-start(bf16[1,96,1024]{2,1,0:T(8,128)(2,1)S(1)} %get-tuple-element.224), channel_id=1, source_target_pairs={{0,16},{2,18},{4,20},{6,22},{8,24},{10,26},{12,28},{14,30},{16,0},... | collective-permute-start | bytes 589832 | tf_op jit(solution)/shard_map/ppermute | solution.py:435
  52.6 17.8 %collective-permute-start.21 = (bf16[1,96,1024]{2,1,0:T(8,128)(2,1)S(1)}, bf16[1,96,1024]{2,1,0:T(8,128)(2,1)S(1)}, u32[]{:S(2)}, u32[]{:S(2)}) collective-permute-start(bf16[1,96,1024]{2,1,0:T(8,128)(2,1)S(1)} %get-tuple-element.223), channel_id=1, source_target_pairs={{0,2},{2,0},{4,6},{6,4},{8,10},{10,8},{12,14},{14,12},{16,18},{18,... | collective-permute-start | bytes 589832 | tf_op jit(solution)/shard_map/ppermute | solution.py:435
  70.4 14.1 %collective-permute-start.12 = (bf16[4,96,640]{2,1,0:T(8,128)(2,1)S(1)}, bf16[4,96,640]{2,1,0:T(8,128)(2,1)S(1)}, u32[]{:S(2)}, u32[]{:S(2)}) collective-permute-start(bf16[4,96,640]{2,1,0:T(8,128)(2,1)S(1)} %copy-done.35), channel_id=1, source_target_pairs={{0,4},{2,6},{4,0},{6,2},{8,12},{10,14},{12,8},{14,10},{16,20},{18,... | collective-permute-start | bytes 1474568 | tf_op jit(solution)/shard_map/ppermute | solution.py:435
  73.7 17.7 %collective-permute-start.13 = (bf16[4,96,640]{2,1,0:T(8,128)(2,1)S(1)}, bf16[4,96,640]{2,1,0:T(8,128)(2,1)S(1)}, u32[]{:S(2)}, u32[]{:S(2)}) collective-permute-start(bf16[4,96,640]{2,1,0:T(8,128)(2,1)S(1)} %copy-done.64), channel_id=1, source_target_pairs={{0,4},{2,6},{4,0},{6,2},{8,12},{10,14},{12,8},{14,10},{16,20},{18,... | collective-permute-start | bytes 1474568 | tf_op jit(solution)/shard_map/ppermute | solution.py:435
  75.8 18.6 %collective-permute-start.14 = (bf16[4,96,640]{2,1,0:T(8,128)(2,1)S(1)}, bf16[4,96,640]{2,1,0:T(8,128)(2,1)S(1)}, u32[]{:S(2)}, u32[]{:S(2)}) collective-permute-start(bf16[4,96,640]{2,1,0:T(8,128)(2,1)S(1)} %copy-done.37), channel_id=1, source_target_pairs={{0,8},{2,10},{4,12},{6,14},{8,0},{10,2},{12,4},{14,6},{16,24},{18,... | collective-permute-start | bytes 1474568 | tf_op jit(solution)/shard_map/ppermute | solution.py:435
  77.8 31.2 %collective-permute-start.15 = (bf16[4,96,640]{2,1,0:T(8,128)(2,1)}, bf16[4,96,640]{2,1,0:T(8,128)(2,1)}, u32[]{:S(2)}, u32[]{:S(2)}) collective-permute-start(bf16[4,96,640]{2,1,0:T(8,128)(2,1)} %collective-permute-done.8.refs_9_), channel_id=1, source_target_pairs={{0,8},{2,10},{4,12},{6,14},{8,0},{10,2},{12,4},{14,6},{16,24},{18,... | collective-permute-start | bytes 1474568 | tf_op jit(solution)/shard_map/ppermute | solution.py:435
  84.5 31.7 %collective-permute-start.17 = (bf16[2,96,1024]{2,1,0:T(8,128)(2,1)}, bf16[2,96,1024]{2,1,0:T(8,128)(2,1)}, u32[]{:S(2)}, u32[]{:S(2)}) collective-permute-start(bf16[2,96,1024]{2,1,0:T(8,128)(2,1)} %pad_maximum_fusion.20), channel_id=1, source_target_pairs={{0,8},{2,10},{4,12},{6,14},{8,0},{10,2},{12,4},{14,6},{16,24},{18,... | collective-permute-start | bytes 1179656 | tf_op jit(solution)/shard_map/ppermute | solution.py:435
  91.4 27.5 %collective-permute-start.22 = (bf16[2,96,1024]{2,1,0:T(8,128)(2,1)}, bf16[2,96,1024]{2,1,0:T(8,128)(2,1)}, u32[]{:S(2)}, u32[]{:S(2)}) collective-permute-start(bf16[2,96,1024]{2,1,0:T(8,128)(2,1)} %pad_maximum_fusion.21), channel_id=1, source_target_pairs={{0,16},{2,18},{4,20},{6,22},{8,24},{10,26},{12,28},{14,30},{16,0},... | collective-permute-start | bytes 1179656 | tf_op jit(solution)/shard_map/ppermute | solution.py:435
  94.4 28.2 %collective-permute-start.27 = (bf16[2,96,1024]{2,1,0:T(8,128)(2,1)}, bf16[2,96,1024]{2,1,0:T(8,128)(2,1)}, u32[]{:S(2)}, u32[]{:S(2)}) collective-permute-start(bf16[2,96,1024]{2,1,0:T(8,128)(2,1)} %pad_maximum_fusion.22), channel_id=1, source_target_pairs={{0,4},{2,6},{4,0},{6,2},{8,12},{10,14},{12,8},{14,10},{16,20},{18,... | collective-permute-start | bytes 1179656 | tf_op jit(solution)/shard_map/ppermute | solution.py:435
  109.0 61.1 %collective-permute-start.32 = (bf16[512,1536]{1,0:T(8,128)(2,1)}, bf16[512,1536]{1,0:T(8,128)(2,1)}, u32[]{:S(2)}, u32[]{:S(2)}) collective-permute-start(bf16[512,1536]{1,0:T(8,128)(2,1)} %fusion.10), channel_id=1, source_target_pairs={{0,1},{1,0},{2,3},{3,2},{4,5},{5,4},{6,7},{7,6},{8,9},{9,8},{10,11... | collective-permute-start | bytes 4718600 | tf_op jit(solution)/shard_map/ppermute | solution.py:409
  118.3 46.5 %collective-permute-start.18 = (bf16[4,96,1024]{2,1,0:T(8,128)(2,1)}, bf16[4,96,1024]{2,1,0:T(8,128)(2,1)}, u32[]{:S(2)}, u32[]{:S(2)}) collective-permute-start(bf16[4,96,1024]{2,1,0:T(8,128)(2,1)} %pad_maximum_fusion.12.refs_0_), channel_id=1, source_target_pairs={{0,4},{2,6},{4,0},{6,2},{8,12},{10,14},{12,8},{14,10},{16,20},{18,... | collective-permute-start | bytes 2359304 | tf_op jit(solution)/shard_map/ppermute | solution.py:435
  118.8 47.6 %collective-permute-start.19 = (bf16[4,96,1024]{2,1,0:T(8,128)(2,1)}, bf16[4,96,1024]{2,1,0:T(8,128)(2,1)}, u32[]{:S(2)}, u32[]{:S(2)}) collective-permute-start(bf16[4,96,1024]{2,1,0:T(8,128)(2,1)} %pad_maximum_fusion.12.refs_0_), channel_id=1, source_target_pairs={{0,2},{2,0},{4,6},{6,4},{8,10},{10,8},{12,14},{14,12},{16,18},{18,... | collective-permute-start | bytes 2359304 | tf_op jit(solution)/shard_map/ppermute | solution.py:435
  122.6 45.8 %collective-permute-start.23 = (bf16[4,96,1024]{2,1,0:T(8,128)(2,1)}, bf16[4,96,1024]{2,1,0:T(8,128)(2,1)}, u32[]{:S(2)}, u32[]{:S(2)}) collective-permute-start(bf16[4,96,1024]{2,1,0:T(8,128)(2,1)} %pad_maximum_fusion.13.refs_4_), channel_id=1, source_target_pairs={{0,8},{2,10},{4,12},{6,14},{8,0},{10,2},{12,4},{14,6},{16,24},{18,... | collective-permute-start | bytes 2359304 | tf_op jit(solution)/shard_map/ppermute | solution.py:435
  124.6 45.0 %collective-permute-start.28 = (bf16[4,96,1024]{2,1,0:T(8,128)(2,1)}, bf16[4,96,1024]{2,1,0:T(8,128)(2,1)}, u32[]{:S(2)}, u32[]{:S(2)}) collective-permute-start(bf16[4,96,1024]{2,1,0:T(8,128)(2,1)} %pad_maximum_fusion.14.refs_8_), channel_id=1, source_target_pairs={{0,2},{2,0},{4,6},{6,4},{8,10},{10,8},{12,14},{14,12},{16,18},{18,... | collective-permute-start | bytes 2359304 | tf_op jit(solution)/shard_map/ppermute | solution.py:435
  164.9 37.4 %collective-permute-start.24 = (bf16[4,96,1024]{2,1,0:T(8,128)(2,1)}, bf16[4,96,1024]{2,1,0:T(8,128)(2,1)}, u32[]{:S(2)}, u32[]{:S(2)}) collective-permute-start(bf16[4,96,1024]{2,1,0:T(8,128)(2,1)} %pad_maximum_fusion.13.refs_4_), channel_id=1, source_target_pairs={{0,4},{2,6},{4,0},{6,2},{8,12},{10,14},{12,8},{14,10},{16,20},{18,... | collective-permute-start | bytes 2359304 | tf_op jit(solution)/shard_map/ppermute | solution.py:435
  166.4 35.9 %collective-permute-start.29 = (bf16[4,96,1024]{2,1,0:T(8,128)(2,1)}, bf16[4,96,1024]{2,1,0:T(8,128)(2,1)}, u32[]{:S(2)}, u32[]{:S(2)}) collective-permute-start(bf16[4,96,1024]{2,1,0:T(8,128)(2,1)} %pad_maximum_fusion.14.refs_8_), channel_id=1, source_target_pairs={{0,8},{2,10},{4,12},{6,14},{8,0},{10,2},{12,4},{14,6},{16,24},{18,... | collective-permute-start | bytes 2359304 | tf_op jit(solution)/shard_map/ppermute | solution.py:435
  168.4 33.9 %collective-permute-start.20 = (bf16[4,96,1024]{2,1,0:T(8,128)(2,1)}, bf16[4,96,1024]{2,1,0:T(8,128)(2,1)}, u32[]{:S(2)}, u32[]{:S(2)}) collective-permute-start(bf16[4,96,1024]{2,1,0:T(8,128)(2,1)} %collective-permute-done.18.refs_1_), channel_id=1, source_target_pairs={{0,2},{2,0},{4,6},{6,4},{8,10},{10,8},{12,14},{14,12},{16,18},{18,... | collective-permute-start | bytes 2359304 | tf_op jit(solution)/shard_map/ppermute | solution.py:435
  169.6 32.8 %collective-permute-start.25 = (bf16[4,96,1024]{2,1,0:T(8,128)(2,1)}, bf16[4,96,1024]{2,1,0:T(8,128)(2,1)}, u32[]{:S(2)}, u32[]{:S(2)}) collective-permute-start(bf16[4,96,1024]{2,1,0:T(8,128)(2,1)} %collective-permute-done.23.refs_5_), channel_id=1, source_target_pairs={{0,4},{2,6},{4,0},{6,2},{8,12},{10,14},{12,8},{14,10},{16,20},{18,... | collective-permute-start | bytes 2359304 | tf_op jit(solution)/shard_map/ppermute | solution.py:435
  170.1 32.3 %collective-permute-start.30 = (bf16[4,96,1024]{2,1,0:T(8,128)(2,1)}, bf16[4,96,1024]{2,1,0:T(8,128)(2,1)}, u32[]{:S(2)}, u32[]{:S(2)}) collective-permute-start(bf16[4,96,1024]{2,1,0:T(8,128)(2,1)} %collective-permute-done.28.refs_9_), channel_id=1, source_target_pairs={{0,8},{2,10},{4,12},{6,14},{8,0},{10,2},{12,4},{14,6},{16,24},{18,... | collective-permute-start | bytes 2359304 | tf_op jit(solution)/shard_map/ppermute | solution.py:435
  372.4 35.4 %collective-permute-start.33 = (f32[1024,256]{0,1:T(8,128)}, f32[1024,256]{0,1:T(8,128)}, u32[]{:S(2)}, u32[]{:S(2)}) collective-permute-start(f32[1024,256]{0,1:T(8,128)} %pad_maximum_fusion.7), channel_id=1, source_target_pairs={{0,1},{1,0},{2,3},{3,2},{4,5},{5,4},{6,7},{7,6},{8,9},{9,8},{10,11... | collective-permute-start | bytes 3145736 | tf_op jit(solution)/shard_map/ppermute | solution.py:409
  376.3 214.4 %collective-permute-start.31 = (f32[512,1536]{1,0:T(8,128)}, f32[512,1536]{1,0:T(8,128)}, u32[]{:S(2)}, u32[]{:S(2)}) collective-permute-start(f32[512,1536]{1,0:T(8,128)} %constant_dynamic-slice_fusion.13), channel_id=1, source_target_pairs={{0,1},{1,0},{2,3},{3,2},{4,5},{5,4},{6,7},{7,6},{8,9},{9,8},{10,11... | collective-permute-start | bytes 9437192 | tf_op jit(solution)/shard_map/ppermute | solution.py:409
  380.6 19.9 %collective-permute-start.58 = (bf16[2,2,2,96,512]{4,3,0,1,2:T(8,128)(2,1)S(1)}, bf16[2,2,2,96,512]{4,3,0,1,2:T(8,128)(2,1)S(1)}, u32[]{:S(2)}, u32[]{:S(2)}) collective-permute-start(bf16[2,2,2,96,512]{4,3,0,1,2:T(8,128)(2,1)S(1)} %bitcast.319), channel_id=1, source_target_pairs={{0,8},{2,10},{4,12},{6,14},{8,0},{10,2},{12,4},{14,6},{16,24},{18,... | collective-permute-start | bytes 2359304 | tf_op jit(solution)/shard_map/ppermute | solution.py:435
  382.8 20.4 %collective-permute-start.54 = (bf16[2,2,2,96,512]{4,3,2,0,1:T(8,128)(2,1)S(1)}, bf16[2,2,2,96,512]{4,3,2,0,1:T(8,128)(2,1)S(1)}, u32[]{:S(2)}, u32[]{:S(2)}) collective-permute-start(bf16[2,2,2,96,512]{4,3,2,0,1:T(8,128)(2,1)S(1)} %bitcast.318), channel_id=1, source_target_pairs={{0,4},{2,6},{4,0},{6,2},{8,12},{10,14},{12,8},{14,10},{16,20},{18,... | collective-permute-start | bytes 2359304 | tf_op jit(solution)/shard_map/ppermute | solution.py:435
  384.6 21.2 %collective-permute-start.50 = (bf16[2,2,2,96,512]{4,3,0,1,2:T(8,128)(2,1)S(1)}, bf16[2,2,2,96,512]{4,3,0,1,2:T(8,128)(2,1)S(1)}, u32[]{:S(2)}, u32[]{:S(2)}) collective-permute-start(bf16[2,2,2,96,512]{4,3,0,1,2:T(8,128)(2,1)S(1)} %bitcast.317), channel_id=1, source_target_pairs={{0,2},{2,0},{4,6},{6,4},{8,10},{10,8},{12,14},{14,12},{16,18},{18,... | collective-permute-start | bytes 2359304 | tf_op jit(solution)/shard_map/ppermute | solution.py:435
  400.5 89.1 %collective-permute-start.66 = (bf16[2,2,2,96,1024]{4,3,0,1,2:T(8,128)(2,1)}, bf16[2,2,2,96,1024]{4,3,0,1,2:T(8,128)(2,1)}, u32[]{:S(2)}, u32[]{:S(2)}) collective-permute-start(bf16[2,2,2,96,1024]{4,3,0,1,2:T(8,128)(2,1)} %bitcast.259), channel_id=1, source_target_pairs={{0,8},{2,10},{4,12},{6,14},{8,0},{10,2},{12,4},{14,6},{16,24},{18,... | collective-permute-start | bytes 4718600 | tf_op jit(solution)/shard_map/ppermute | solution.py:435
  403.2 98.9 %collective-permute-start.46 = (bf16[2,2,2,96,1024]{4,3,2,0,1:T(8,128)(2,1)}, bf16[2,2,2,96,1024]{4,3,2,0,1:T(8,128)(2,1)}, u32[]{:S(2)}, u32[]{:S(2)}) collective-permute-start(bf16[2,2,2,96,1024]{4,3,2,0,1:T(8,128)(2,1)} %bitcast.260), channel_id=1, source_target_pairs={{0,4},{2,6},{4,0},{6,2},{8,12},{10,14},{12,8},{14,10},{16,20},{18,... | collective-permute-start | bytes 4718600 | tf_op jit(solution)/shard_map/ppermute | solution.py:435
  405.8 29.6 %collective-permute-start.59 = (bf16[2,2,96,512]{3,2,0,1:T(8,128)(2,1)}, bf16[2,2,96,512]{3,2,0,1:T(8,128)(2,1)}, u32[]{:S(2)}, u32[]{:S(2)}) collective-permute-start(bf16[2,2,96,512]{3,2,0,1:T(8,128)(2,1)} %fusion.42), channel_id=1, source_target_pairs={{0,2},{2,0},{4,6},{6,4},{8,10},{10,8},{12,14},{14,12},{16,18},{18,... | collective-permute-start | bytes 1179656 | tf_op jit(solution)/shard_map/ppermute | solution.py:435
  407.9 37.2 %collective-permute-start.55 = (bf16[2,2,96,512]{3,2,1,0:T(8,128)(2,1)}, bf16[2,2,96,512]{3,2,1,0:T(8,128)(2,1)}, u32[]{:S(2)}, u32[]{:S(2)}) collective-permute-start(bf16[2,2,96,512]{3,2,1,0:T(8,128)(2,1)} %fusion.41), channel_id=1, source_target_pairs={{0,8},{2,10},{4,12},{6,14},{8,0},{10,2},{12,4},{14,6},{16,24},{18,... | collective-permute-start | bytes 1179656 | tf_op jit(solution)/shard_map/ppermute | solution.py:435
  435.4 11.8 %collective-permute-start.51 = (bf16[2,2,96,512]{3,2,0,1:T(8,128)(2,1)S(1)}, bf16[2,2,96,512]{3,2,0,1:T(8,128)(2,1)S(1)}, u32[]{:S(2)}, u32[]{:S(2)}) collective-permute-start(bf16[2,2,96,512]{3,2,0,1:T(8,128)(2,1)S(1)} %copy-done.70), channel_id=1, source_target_pairs={{0,4},{2,6},{4,0},{6,2},{8,12},{10,14},{12,8},{14,10},{16,20},{18,... | collective-permute-start | bytes 1179656 | tf_op jit(solution)/shard_map/ppermute | solution.py:435
  445.0 65.2 %collective-permute-start.42 = (bf16[2,2,2,96,1024]{4,3,0,1,2:T(8,128)(2,1)S(1)}, bf16[2,2,2,96,1024]{4,3,0,1,2:T(8,128)(2,1)S(1)}, u32[]{:S(2)}, u32[]{:S(2)}) collective-permute-start(bf16[2,2,2,96,1024]{4,3,0,1,2:T(8,128)(2,1)S(1)} %bitcast.304), channel_id=1, source_target_pairs={{0,2},{2,0},{4,6},{6,4},{8,10},{10,8},{12,14},{14,12},{16,18},{18,... | collective-permute-start | bytes 4718600 | tf_op jit(solution)/shard_map/ppermute | solution.py:435
  488.7 13.3 %collective-permute-start.62 = (bf16[2,2,2,96,384]{4,3,2,1,0:T(8,128)(2,1)S(1)}, bf16[2,2,2,96,384]{4,3,2,1,0:T(8,128)(2,1)S(1)}, u32[]{:S(2)}, u32[]{:S(2)}) collective-permute-start(bf16[2,2,2,96,384]{4,3,2,1,0:T(8,128)(2,1)S(1)} %copy-done.60), channel_id=1, source_target_pairs={{0,2},{2,0},{4,6},{6,4},{8,10},{10,8},{12,14},{14,12},{16,18},{18,... | collective-permute-start | bytes 1769480 | tf_op jit(solution)/shard_map/ppermute | solution.py:435
  489.6 84.5 %collective-permute-start.34 = (f32[512,1536]{1,0:T(8,128)}, f32[512,1536]{1,0:T(8,128)}, u32[]{:S(2)}, u32[]{:S(2)}) collective-permute-start(f32[512,1536]{1,0:T(8,128)} %constant_dynamic-slice_fusion.12), channel_id=1, source_target_pairs={{0,1},{1,0},{2,3},{3,2},{4,5},{5,4},{6,7},{7,6},{8,9},{9,8},{10,11... | collective-permute-start | bytes 9437192 | tf_op jit(solution)/shard_map/ppermute | solution.py:409
  501.9 33.3 %collective-permute-start.67 = (bf16[2,2,96,1024]{3,2,0,1:T(8,128)(2,1)}, bf16[2,2,96,1024]{3,2,0,1:T(8,128)(2,1)}, u32[]{:S(2)}, u32[]{:S(2)}) collective-permute-start(bf16[2,2,96,1024]{3,2,0,1:T(8,128)(2,1)} %fusion.30), channel_id=1, source_target_pairs={{0,2},{2,0},{4,6},{6,4},{8,10},{10,8},{12,14},{14,12},{16,18},{18,... | collective-permute-start | bytes 2359304 | tf_op jit(solution)/shard_map/ppermute | solution.py:435
  509.3 27.9 %collective-permute-start.47 = (bf16[2,2,96,1024]{3,2,1,0:T(8,128)(2,1)}, bf16[2,2,96,1024]{3,2,1,0:T(8,128)(2,1)}, u32[]{:S(2)}, u32[]{:S(2)}) collective-permute-start(bf16[2,2,96,1024]{3,2,1,0:T(8,128)(2,1)} %fusion.29), channel_id=1, source_target_pairs={{0,8},{2,10},{4,12},{6,14},{8,0},{10,2},{12,4},{14,6},{16,24},{18,... | collective-permute-start | bytes 2359304 | tf_op jit(solution)/shard_map/ppermute | solution.py:435
  510.2 16.0 %collective-permute-start.64 = (bf16[2,96,384]{2,1,0:T(8,128)(2,1)S(1)}, bf16[2,96,384]{2,1,0:T(8,128)(2,1)S(1)}, u32[]{:S(2)}, u32[]{:S(2)}) collective-permute-start(bf16[2,96,384]{2,1,0:T(8,128)(2,1)S(1)} %fusion.52), channel_id=1, source_target_pairs={{0,8},{2,10},{4,12},{6,14},{8,0},{10,2},{12,4},{14,6},{16,24},{18,... | collective-permute-start | bytes 442376 | tf_op jit(solution)/shard_map/ppermute | solution.py:435
  532.1 14.5 %collective-permute-start.43 = (bf16[2,2,96,1024]{3,2,0,1:T(8,128)(2,1)}, bf16[2,2,96,1024]{3,2,0,1:T(8,128)(2,1)}, u32[]{:S(2)}, u32[]{:S(2)}) collective-permute-start(bf16[2,2,96,1024]{3,2,0,1:T(8,128)(2,1)} %fusion.28), channel_id=1, source_target_pairs={{0,4},{2,6},{4,0},{6,2},{8,12},{10,14},{12,8},{14,10},{16,20},{18,... | collective-permute-start | bytes 2359304 | tf_op jit(solution)/shard_map/ppermute | solution.py:435
  536.8 13.9 %collective-permute-start.68 = (bf16[2,96,1024]{2,1,0:T(8,128)(2,1)S(1)}, bf16[2,96,1024]{2,1,0:T(8,128)(2,1)S(1)}, u32[]{:S(2)}, u32[]{:S(2)}) collective-permute-start(bf16[2,96,1024]{2,1,0:T(8,128)(2,1)S(1)} %fusion.43), channel_id=1, source_target_pairs={{0,4},{2,6},{4,0},{6,2},{8,12},{10,14},{12,8},{14,10},{16,20},{18,... | collective-permute-start | bytes 1179656 | tf_op jit(solution)/shard_map/ppermute | solution.py:435
  539.2 22.8 %collective-permute-start.48 = (bf16[2,96,1024]{2,1,0:T(8,128)(2,1)S(1)}, bf16[2,96,1024]{2,1,0:T(8,128)(2,1)S(1)}, u32[]{:S(2)}, u32[]{:S(2)}) collective-permute-start(bf16[2,96,1024]{2,1,0:T(8,128)(2,1)S(1)} %fusion.39), channel_id=1, source_target_pairs={{0,16},{2,18},{4,20},{6,22},{8,24},{10,26},{12,28},{14,30},{16,0},... | collective-permute-start | bytes 1179656 | tf_op jit(solution)/shard_map/ppermute | solution.py:435
  548.2 18.0 %collective-permute-start.44 = (bf16[2,96,1024]{2,1,0:T(8,128)(2,1)S(1)}, bf16[2,96,1024]{2,1,0:T(8,128)(2,1)S(1)}, u32[]{:S(2)}, u32[]{:S(2)}) collective-permute-start(bf16[2,96,1024]{2,1,0:T(8,128)(2,1)S(1)} %fusion.38), channel_id=1, source_target_pairs={{0,8},{2,10},{4,12},{6,14},{8,0},{10,2},{12,4},{14,6},{16,24},{18,... | collective-permute-start | bytes 1179656 | tf_op jit(solution)/shard_map/ppermute | solution.py:435
  550.9 15.5 %collective-permute-start.69 = (bf16[96,1024]{1,0:T(8,128)(2,1)S(1)}, bf16[96,1024]{1,0:T(8,128)(2,1)S(1)}, u32[]{:S(2)}, u32[]{:S(2)}) collective-permute-start(bf16[96,1024]{1,0:T(8,128)(2,1)S(1)} %fusion.50), channel_id=1, source_target_pairs={{0,16},{2,18},{4,20},{6,22},{8,24},{10,26},{12,28},{14,30},{16,0},... | collective-permute-start | bytes 589832 | tf_op jit(solution)/shard_map/ppermute | solution.py:435
  (153 other events, 1799.7 us)
